TPU v7x, 256 devices: a 2x2x32 block of a 4x8x32 slice. The times are simulated.
256 devices in a mesh: groups: 4 (over x, y), space: 64 (over z, core).
Axes of the slice: x: 2, y: 2, z: 32, core: 2. Of those that a mesh axis runs over, the one named last changes fastest.
The devices are a block of a 4x8x32 slice.
Arguments:
- hidden: bfloat16 [32768, 512], P(('groups', 'space')), parts along dimension 0, may hold values from -130 to 130
- norm_gain: float32 [512], replicated, may hold values from 0.5 to 2
- norm_shift: float32 [512], replicated, may hold values from -3 to 3
- conv_weight: bfloat16 [3, 3, 3, 512, 512], P(None, None, None, 'space'), may hold values from -0.0546875 to 0.0546875
- conv_bias: bfloat16 [512], replicated, may hold values from -3 to 3
Outputs:
- decoded: bfloat16 [16, 32, 256, 512], P('groups', None, 'space'), parts along dimension 0
There are 4 independent parts, one for each index of `groups`. A program takes and returns all parts, laid end to end along the dimension named above; an argument that names none is the same for every part. Nothing has to cross between parts.
All inputs are finite; a program needn't handle non-finite values.
Results may differ from a plain program's by a relative error of at most 0.0045.
Values may be sent and summed in bfloat16 or wider, within the bound.
No kernel may reach another device: no remote copies, remote signals or barrier semaphores. Data moves between devices by JAX's collectives and lax.ppermute only.
A program may use at most 64 MiB of HBM per device.

v0:
```python
import jax
import jax.numpy as jnp
from jax import lax
from jax.sharding import Mesh
from jax.sharding import PartitionSpec as P

CHANNELS = 512
GROUPS = 32
FRAMES = 4
ROWS = 16
COL_DEV = 2
SPACE = ("space_0", "space_1")
GROUPS_SPACE = ("groups", "space_0", "space_1")


EPSILON = 1e-06


def one_axis_at_a_time(x, axes):
    for axis in axes:
        x = lax.psum(x, axis)
    return x


def with_halo(x, sides, width):
    for axis, dim in sides:
        size, length = (lax.axis_size(axis), x.shape[dim])
        up = [(i, (i + 1) % size) for i in range(size - 1)]
        down = [(j, i) for i, j in up]
        last = lax.slice_in_dim(x, length - width, length, axis=dim)
        first = lax.slice_in_dim(x, 0, width, axis=dim)
        before = lax.ppermute(last, axis, up)
        after = lax.ppermute(first, axis, down)
        x = jnp.concatenate([before, x, after], axis=dim)
    return x


def group_moments(values, population):
    grouped = values.reshape(-1, GROUPS, CHANNELS // GROUPS).astype(jnp.float32)
    totals, squares = (
        one_axis_at_a_time(jnp.sum(grouped, axis=(0, 2)), SPACE),
        one_axis_at_a_time(jnp.sum(grouped * grouped, axis=(0, 2)), SPACE),
    )
    average = totals / population
    spread = squares / population - average * average
    return (average, spread)


def shards(hidden, norm_gain, norm_shift, conv_weight, conv_bias):
    devices = lax.axis_size(SPACE)
    rows_dev = hidden.shape[0] // (COL_DEV * devices)
    population = float(FRAMES * ROWS * COL_DEV * devices * (CHANNELS // GROUPS))
    layout = hidden.reshape(rows_dev, devices * COL_DEV, CHANNELS)
    tile_cells = lax.all_to_all(layout, SPACE, split_axis=1, concat_axis=0, tiled=True)
    average, spread = group_moments(tile_cells, population)
    scaled = tile_cells.astype(jnp.float32).reshape(
        FRAMES, ROWS, COL_DEV, GROUPS, CHANNELS // GROUPS
    )
    scaled = (scaled - average[:, None]) * lax.rsqrt(spread + EPSILON)[:, None]
    normed = scaled.reshape(FRAMES, ROWS, COL_DEV, CHANNELS) * norm_gain + norm_shift
    active = jax.nn.silu(normed).astype(jnp.bfloat16)
    widened = with_halo(active, ((SPACE, 2),), 1)
    position = lax.axis_index(SPACE)
    lefthand = jnp.where(position == 0, active[:, :, :1], widened[:, :, :1])
    righthand = jnp.where(position == devices - 1, active[:, :, -1:], widened[:, :, -1:])
    widened = jnp.concatenate([lefthand, active, righthand], axis=2)
    doubled = jnp.repeat(jnp.repeat(widened, 2, axis=1), 2, axis=2)[:, :, 1:-1]
    padded = jnp.pad(doubled, ((2, 0), (1, 1), (0, 0), (0, 0)), mode="edge")
    initial = jnp.zeros((FRAMES, 2 * ROWS, 2 * COL_DEV, CHANNELS), jnp.float32)
    product = lax.conv_general_dilated(
        padded[None],
        lax.all_gather(conv_weight, SPACE, axis=3, tiled=True),
        (1, 1, 1),
        "VALID",
        dimension_numbers=("NDHWC", "DHWIO", "NDHWC"),
        preferred_element_type=jnp.float32,
    )
    summed = initial + product[0]
    return (summed + conv_bias.astype(jnp.float32)).astype(jnp.bfloat16)


def solution(mesh):
    torus = Mesh(
        mesh.devices.reshape(mesh.shape["groups"], 32, 2), ("groups", "space_0", "space_1")
    )
    return jax.shard_map(
        shards,
        mesh=torus,
        in_specs=(P(GROUPS_SPACE, None), P(), P(), P(None, None, None, SPACE, None), P()),
        out_specs=P("groups", None, SPACE, None),
        check_vma=False,
    )
```

profile of v0, /device:TPU:37, one launch (start us, length us, event | category | flops | bytes accessed | tf_op | source)
XLA Modules:
  0.0 228.4 jit_solution(5131043434642010950)
XLA Ops:
  6.6 0.7 all-gather.2.cloned.1.call-update
  7.3 1.1 copy.33
  8.4 0.5 broadcast.35
  8.9 1.4 reduce.6
  10.4 65.5 %all_to_all.4 = bf16[64,2,512]{2,1,0:T(2,128)(2,1)S(1)} all-to-all(bf16[64,2,512]{2,1,0:T(2,128)(2,1)S(1)} %reshape.40), channel_id=1, replica_groups=mesh['groups'=4,'space_0'=32,'space_1'=2] {'space_0','space_1'}, dimensions={0} | all-to-all | bytes 262144 | tf_op jit(solution)/shard_map/all_to_all | solution.py:54
  75.9 0.1 reshape.41
  76.0 1.0 convert_reduce_fusion
  77.1 0.1 reduce_sum.25
  77.2 0.1 reduce_sum.37
  77.4 43.2 %all-reduce = (f32[32]{0:T(128)S(1)}, f32[32]{0:T(128)S(1)}) all-reduce(f32[32]{0:T(128)S(1)} %reduce_sum.37, f32[32]{0:T(128)S(1)} %reduce_sum.25), channel_id=1, replica_groups=mesh['groups'=4,'space_0'=32,'space_1'=2] {'space_0'}, use_global_device_ids=true, to_apply=%region_6.7 | all-reduce | flops 64 | bytes 512 | tf_op jit(solution)/shard_map/psum | solution.py:21
  120.6 14.5 %all-reduce.1 = (f32[32]{0:T(128)S(1)}, f32[32]{0:T(128)S(1)}) all-reduce(f32[32]{0:T(128)S(1)} %get-tuple-element.8, f32[32]{0:T(128)S(1)} %get-tuple-element.9), channel_id=1, replica_groups=mesh['groups'=4,'space_0'=32,'space_1'=2] {'space_1'}, use_global_device_ids=true, to_apply=%region_7.8 | all-reduce | flops 64 | bytes 512 | tf_op jit(solution)/shard_map/psum | solution.py:21
  135.2 0.1 mul.39
  135.4 0.2 reshape.38
  135.6 0.1 multiply_convert_fusion
  135.7 3.1 %collective-permute-start = (bf16[4,16,1,512]{3,1,2,0:T(8,128)(2,1)S(1)}, bf16[4,16,1,512]{3,1,2,0:T(8,128)(2,1)S(1)}, u32[]{:S(2)}, u32[]{:S(2)}) collective-permute-start(bf16[4,16,1,512]{3,1,2,0:T(8,128)(2,1)S(1)} %get-tuple-element.14), channel_id=1, source_target_pairs={{0,1},{1,2},{2,3},{3,4},{4,5},{5,6},{6,7},{7,8},{8,9},{9,10},{10,1... | collective-permute-start | bytes 196616 | tf_op jit(solution)/shard_map/ppermute | solution.py:32
  138.8 2.0 collective-permute-start.1
  140.8 4.8 %collective-permute-done.1 = bf16[4,16,1,512]{3,1,2,0:T(8,128)(2,1)S(1)} collective-permute-done((bf16[4,16,1,512]{3,1,2,0:T(8,128)(2,1)S(1)}, bf16[4,16,1,512]{3,1,2,0:T(8,128)(2,1)S(1)}, u32[]{:S(2)}, u32[]{:S(2)}) %collective-permute-start.1) | collective-permute-done | bytes 65568 | tf_op jit(solution)/shard_map/ppermute | solution.py:33
  145.6 0.4 broadcast_in_dim.14
  146.1 0.2 reshape.35
  146.3 0.1 broadcast_in_dim.15
  146.5 0.6 fusion.9
  147.2 30.7 %all-gather.2.cloned.1.call-done = bf16[3,3,3,512,512]{4,3,2,1,0:T(8,128)(2,1)} async-done(((bf16[3,3,3,8,512]{4,3,2,1,0:T(8,128)(2,1)}), bf16[3,3,3,512,512]{4,3,2,1,0:T(8,128)(2,1)}) %all-gather.2.cloned.1.call-update) | async-done | bytes 14155792 | tf_op jit(solution)/shard_map/all_gather | solution.py:72
  177.9 42.6 %fusion.4 = f32[1,4,32,4,512]{4,0,3,2,1:T(1,128)S(1)} fusion(bf16[3,3,3,512,512]{4,3,2,1,0:T(8,128)(2,1)} %all-gather.2.cloned.1.call-done, bf16[1,6,34,6,512]{4,2,3,1,0:T(8,128)(2,1)S(1)} %fusion.9), kind=kOutput, calls=%fused_computation.6 | convolution fusion | flops 7247757312 | bytes 16457728 | tf_op jit(solution)/shard_map/conv_general_dilated | solution.py:70
  220.5 1.1 fusion.11
  (22 shorter events, 0.6 us)
Async XLA Ops:
  6.5 129.0 %copy-start.1 = (f32[512]{0:T(512)S(1)}, f32[512]{0:T(512)}, u32[]{:S(2)}) copy-start(f32[512]{0:T(512)} %param.6) | copy-start | bytes 6148
  6.5 129.1 %copy-start = (f32[512]{0:T(512)S(1)}, f32[512]{0:T(512)}, u32[]{:S(2)}) copy-start(f32[512]{0:T(512)} %param.7) | copy-start | bytes 6148
  6.6 134.2 %copy-start.2 = (bf16[512]{0:T(512)(128)(2,1)S(1)}, bf16[512]{0:T(512)(128)(2,1)}, u32[]{:S(2)}) copy-start(bf16[512]{0:T(512)(128)(2,1)} %param.9) | copy-start | bytes 3076
  6.6 171.3 %all-gather.2.cloned.1.call-start = ((), (), s32[]{:S(2)}) async-start(), calls=%async_computation.1 | async-start | bytes 14376960 | tf_op jit(solution)/shard_map/all_gather | solution.py:72
  135.7 5.1 %collective-permute-start = (bf16[4,16,1,512]{3,1,2,0:T(8,128)(2,1)S(1)}, bf16[4,16,1,512]{3,1,2,0:T(8,128)(2,1)S(1)}, u32[]{:S(2)}, u32[]{:S(2)}) collective-permute-start(bf16[4,16,1,512]{3,1,2,0:T(8,128)(2,1)S(1)} %get-tuple-element.14), channel_id=1, source_target_pairs={{0,1},{1,2},{2,3},{3,4},{4,5},{5,6},{6,7},{7,8},{8,9},{9,10},{10,1... | collective-permute-start | bytes 196616 | tf_op jit(solution)/shard_map/ppermute | solution.py:32
  138.8 6.8 %collective-permute-start.1 = (bf16[4,16,1,512]{3,1,2,0:T(8,128)(2,1)S(1)}, bf16[4,16,1,512]{3,1,2,0:T(8,128)(2,1)S(1)}, u32[]{:S(2)}, u32[]{:S(2)}) collective-permute-start(bf16[4,16,1,512]{3,1,2,0:T(8,128)(2,1)S(1)} %get-tuple-element.15), channel_id=1, source_target_pairs={{1,0},{2,1},{3,2},{4,3},{5,4},{6,5},{7,6},{8,7},{9,8},{10,9},{11,1... | collective-permute-start | bytes 196616 | tf_op jit(solution)/shard_map/ppermute | solution.py:33
Sparse Core Ops, SparseCore 0:
  9.2 168.6 all-gather.1
where the time goes:
time: 229 us; the launch traced here: 228 us
  blocking collectives  123 us (54%)
  matrix products  42.6 us (19%)
  waiting for transfers between devices  36.2 us (16%)
  between operations  13.6 us (6%)
  starting transfers between devices  5.03 us (2%)
  other arithmetic  4.5 us (2%)
  local copies, waits for them, and re-layouts  3.27 us (1%)
    all_to_all x1, blocking collectives, shards(): lax.all_to_all(layout, SPACE, split_axis=1, concat_axis=0, tiled=True)  65.5 us
    psum x2, blocking collectives, one_axis_at_a_time(): x = lax.psum(x, axis)  57.7 us
    conv_general_dilated x1, matrix products, shards(): lax.conv_general_dilated(padded[None], lax.all_gather(conv_weight, SPACE,...  42.6 us
    all_gather x1, waiting for transfers between devices, shards(): lax.all_gather(conv_weight, SPACE, axis=3, tiled=True)  30.7 us
    ppermute x1, waiting for transfers between devices, with_halo(): after = lax.ppermute(first, axis, down)  4.75 us
  transfers between devices with their start and end apart: 3, of which 2 were waited for; matrix products, arithmetic and copies ran while one was open for 3% of the time, Pallas kernels for 0%

commit v1 on v0

v1 whole, which is shorter than its diff:
```python
import functools

import jax
import jax.numpy as jnp
from jax import lax
from jax.experimental import pallas as pl
from jax.experimental.pallas import tpu as pltpu
from jax.sharding import Mesh
from jax.sharding import PartitionSpec as P

CHANNELS = 512
GROUPS = 32
FRAMES = 4
ROWS = 16
COLS = 2
CELLS = FRAMES * ROWS
MEMBERS = CHANNELS // GROUPS
QUAD = 4
SLICE = CHANNELS // QUAD
TAPS = 27
SPACE = ("zh", "zl", "c")
CHIPS = ("zh", "zl")
EPSILON = 1e-06
F32, BF16 = jnp.float32, jnp.bfloat16
HIGHEST = lax.Precision.HIGHEST


def iota(shape, dim):
    return lax.broadcasted_iota(jnp.int32, shape, dim)


def dot(a, b, precision=None):
    return jnp.dot(a, b, preferred_element_type=F32, precision=precision)


def in_pieces(v):
    high = v.astype(BF16)
    rest = v - high.astype(F32)
    middle = rest.astype(BF16)
    low = (rest - middle.astype(F32)).astype(BF16)
    lane = iota(v.shape, 1)
    return jnp.where(
        lane < GROUPS,
        high.astype(F32),
        jnp.where(lane < 2 * GROUPS, middle.astype(F32), low.astype(F32)),
    ).astype(BF16)


def pack_kernel(x_ref, w_ref, o_ref, s_ref):
    quarter = lax.axis_index("gq")
    lanes = pl.ds(pl.multiple_of(quarter * SLICE, SLICE), SLICE)
    s_ref[...] = w_ref[:, :, lanes]
    x = x_ref[...].astype(F32)
    cells = x.shape[0]
    gather = jnp.where(
        (iota((CHANNELS, 128), 0) // MEMBERS == iota((CHANNELS, 128), 1) % GROUPS)
        & (iota((CHANNELS, 128), 1) < 3 * GROUPS),
        1.0,
        0.0,
    )
    spread = jnp.where(iota((128, CHANNELS), 0) == iota((128, CHANNELS), 1) // MEMBERS, 1.0, 0.0)
    sums = jnp.broadcast_to(jnp.sum(x, axis=0, keepdims=True), (8, CHANNELS))
    mean = dot(sums, gather, HIGHEST) * (1.0 / (cells * MEMBERS))
    away = x - dot(mean, spread, HIGHEST)[:1]
    squares = jnp.broadcast_to(jnp.sum(away * away, axis=0, keepdims=True), (8, CHANNELS))
    second = dot(squares, gather, HIGHEST)
    stats = jnp.concatenate([in_pieces(mean)[:1], in_pieces(second)[:1]], axis=0)
    for d in range(cells // COLS):
        o_ref[d, :, :CHANNELS] = x_ref[d * COLS : (d + 1) * COLS, :]
        o_ref[d, :, CHANNELS:] = stats


def norm_kernel(r_ref, gain_ref, shift_ref, o_ref):
    r = r_ref[...].astype(F32)
    rows = r.shape[0]

    def whole(v):
        return v + pltpu.roll(v, 128 - GROUPS, 1) + pltpu.roll(v, 128 - 2 * GROUPS, 1)

    means = whole(r[:, 0, CHANNELS:])
    seconds = whole(r[:, 1, CHANNELS:])
    each = float(rows * COLS * MEMBERS)
    mean = jnp.sum(means, axis=0, keepdims=True) * (1.0 / rows)
    second = jnp.sum(seconds, axis=0, keepdims=True) + each * jnp.sum(
        (means - mean) * (means - mean), axis=0, keepdims=True
    )
    real = iota((1, 128), 1) < GROUPS
    mean = jnp.where(real, mean, 0.0)
    scale = lax.rsqrt(jnp.where(real, second, 0.0) * (1.0 / (each * rows)) + EPSILON)
    spread = jnp.where(iota((128, CHANNELS), 0) == iota((128, CHANNELS), 1) // MEMBERS, 1.0, 0.0)
    mean = dot(jnp.broadcast_to(mean, (8, 128)), spread, HIGHEST)[:1]
    scale = dot(jnp.broadcast_to(scale, (8, 128)), spread, HIGHEST)[:1] * gain_ref[...]
    for j in range(COLS):
        v = (r[:, j, :CHANNELS] - mean) * scale + shift_ref[...]
        o_ref[j] = (v / (1.0 + jnp.exp(-v))).astype(BF16)


def conv_kernel(xa_ref, xl_ref, xr_ref, b_ref, *rest):
    parts, (o_ref, w_ref, x_ref, p0, p1, p2, sem) = rest[:6], rest[6:]
    core, parity, quarter = (lax.axis_index(n) for n in ("c", "zl", "gq"))
    place = lax.axis_index(SPACE)
    last = lax.axis_size(SPACE) - 1
    copies = []
    for n, part in enumerate(parts):
        owner = core if n < 3 else 1 - core
        for j in range(part.shape[0]):
            chip = 2 * (j + (part.shape[0] if n % 3 == 2 else 0)) + (parity if n % 3 == 0 else 1 - parity)
            copies.append(pltpu.make_async_copy(part.at[j], w_ref.at[:, 2 * chip + owner], sem))
    for copy in copies:
        copy.start()

    half = QUAD * CELLS
    for v in range(QUAD):
        blocks = (
            (v * CELLS, jnp.where(place == 0, xa_ref[v, 0], xl_ref[v])),
            (half + v * 2 * CELLS, xa_ref[v, 0]),
            (half + (v * 2 + 1) * CELLS, xa_ref[v, 1]),
            (3 * half + v * CELLS, jnp.where(place == last, xa_ref[v, 1], xr_ref[v])),
        )
        for start, block in blocks:
            for a in range(3):
                for f in range(FRAMES):
                    g = max(f + a - 2, 0)
                    x_ref[a, start + f * ROWS : start + (f + 1) * ROWS] = block[g * ROWS : (g + 1) * ROWS]
    for copy in copies:
        copy.wait()

    taps = w_ref.reshape(TAPS, CHANNELS, SLICE)
    for e, (p_ref, lo, hi) in enumerate(((p0, 0, 3 * half), (p1, half, 3 * half), (p2, half, 4 * half))):
        for rows in ((0, 1), (2,)):
            total = 0.0
            for a in range(3):
                w = jnp.concatenate([taps[a * 9 + b * 3 + e] for b in rows], axis=1)
                total += dot(x_ref[a, lo:hi], w)
            for n, b in enumerate(rows):
                p_ref[b] = total[:, n * SLICE : (n + 1) * SLICE]

    bias = b_ref[pl.ds(quarter, 1)]
    row = iota((CELLS, SLICE), 0) % ROWS

    def combine(v, _):
        def own(p_ref, lead, b, j):
            return p_ref[b, pl.ds(pl.multiple_of(lead + v * 2 * CELLS + j * CELLS, CELLS), CELLS)]

        def edge(p_ref, lead, b):
            return p_ref[b, pl.ds(pl.multiple_of(lead + v * CELLS, CELLS), CELLS)]

        for j in range(COLS):
            for side in range(2):
                t = []
                for b in range(3):
                    if side == 0:
                        first = edge(p0, 0, b) if j == 0 else own(p0, half, b, 0)
                        t.append(first + own(p1, 0, b, j) + own(p2, 0, b, j))
                    else:
                        final = edge(p2, 2 * half, b) if j == 1 else own(p2, 0, b, 1)
                        t.append(own(p0, half, b, j) + own(p1, 0, b, j) + final)
                above = jnp.where(row == 0, t[0], pltpu.roll(t[0], 1, 0))
                below = jnp.where(row == ROWS - 1, t[2], pltpu.roll(t[2], CELLS - 1, 0))
                for up, value in enumerate((above + t[1] + t[2], t[0] + t[1] + below)):
                    at = (up * 2 * COLS + 2 * j + side) * CELLS
                    o_ref[v, at : at + CELLS] = (value + bias).astype(BF16)
        return 0

    lax.fori_loop(0, QUAD, combine, 0)


def vmem(n):
    return [pl.BlockSpec(memory_space=pltpu.VMEM)] * n


def shards(hidden, norm_gain, norm_shift, conv_weight, conv_bias):
    devices = lax.axis_size(SPACE)
    chips = lax.axis_size(CHIPS)
    share = conv_weight.shape[3]
    packed, mine = pl.pallas_call(
        pack_kernel,
        out_shape=(
            jax.ShapeDtypeStruct((devices, COLS, CHANNELS + 128), BF16),
            jax.ShapeDtypeStruct((TAPS, share, SLICE), BF16),
        ),
        in_specs=vmem(2),
        out_specs=tuple(vmem(2)),
        name="pack",
    )(hidden, conv_weight.reshape(TAPS, share, CHANNELS))

    tiles = lax.all_to_all(packed, SPACE, split_axis=0, concat_axis=0, tiled=True)
    kin = lax.all_gather(mine, "zh", axis=0)

    swap = [(0, 1), (1, 0)]
    up = [(i, (i + 1) % chips) for i in range(chips)]
    down = [(j, i) for i, j in up]
    part = kin.shape[0] // 2
    low = lax.ppermute(kin[:part], CHIPS, up)
    high = lax.ppermute(kin[part:], CHIPS, down)
    weights = (kin, low, high)
    weights += tuple(lax.ppermute(w, "c", swap) for w in weights)

    active = pl.pallas_call(
        norm_kernel,
        out_shape=jax.ShapeDtypeStruct((COLS, CELLS, CHANNELS), BF16),
        in_specs=vmem(3),
        out_specs=vmem(1)[0],
        name="norm",
    )(tiles, norm_gain[None], norm_shift[None])
    active = lax.all_gather(active, "gq", axis=0)
    right = [(i, i + 1) for i in range(devices - 1)]
    left = [(j, i) for i, j in right]
    before = lax.ppermute(active[:, 1], SPACE, right)
    after = lax.ppermute(active[:, 0], SPACE, left)

    half = QUAD * CELLS
    out = pl.pallas_call(
        conv_kernel,
        out_shape=jax.ShapeDtypeStruct((QUAD, 4 * COLS * CELLS, SLICE), BF16),
        in_specs=vmem(4) + [pl.BlockSpec(memory_space=pltpu.HBM)] * 6,
        out_specs=vmem(1)[0],
        scratch_shapes=[
            pltpu.VMEM((TAPS, CHANNELS // share, share, SLICE), BF16),
            pltpu.VMEM((3, 4 * half, CHANNELS), BF16),
            pltpu.VMEM((3, 3 * half, SLICE), F32),
            pltpu.VMEM((3, 2 * half, SLICE), F32),
            pltpu.VMEM((3, 3 * half, SLICE), F32),
            pltpu.SemaphoreType.DMA,
        ],
        name="conv",
    )(active, before, after, conv_bias.astype(F32).reshape(QUAD, SLICE), *weights)
    out = lax.all_to_all(out, "gq", split_axis=0, concat_axis=0, tiled=True)
    out = out.reshape(QUAD, 2, 2 * COLS, FRAMES, ROWS, SLICE)
    out = out.transpose(3, 4, 1, 2, 0, 5)
    return out.reshape(FRAMES, 2 * ROWS, 2 * COLS, CHANNELS)


def solution(mesh):
    groups, space = mesh.shape["groups"], mesh.shape["space"]
    torus = Mesh(
        mesh.devices.reshape(groups // QUAD, QUAD, space // 4, 2, 2), ("gh", "gq", "zh", "zl", "c")
    )
    return jax.shard_map(
        shards,
        mesh=torus,
        in_specs=(
            P(("gh", "gq") + SPACE, None),
            P(),
            P(),
            P(None, None, None, SPACE, None),
            P(),
        ),
        out_specs=P(("gh", "gq"), None, SPACE, None),
        check_vma=False,
    )
```

time: 229 us -> 152 us (0.66)
  starting transfers between devices: 5.03 us -> 59.8 us
  blocking collectives: 123 us -> 72.9 us
  matrix products: 42.6 us -> 0 us
  waiting for transfers between devices: 36.2 us -> 2.72 us
  between operations: 13.6 us -> 0.11 us
  Pallas kernels: 0 us -> 12.3 us
  other arithmetic: 4.5 us -> 0.55 us
    all_gather x0 -> x2, blocking collectives: none -> 60.9 us  [the longest x1 50.7 us: shards(): kin = lax.all_gather(mine, 'zh', axis=0)]
    psum x2 -> x0, blocking collectives: 57.7 us -> none  [one_axis_at_a_time(): x = lax.psum(x, axis)]
    all_to_all x1, blocking collectives: 65.5 us -> 12 us  [shards(): out = lax.all_to_all(out, 'gq', split_axis=0, concat_axis=0, tiled=True)]
    conv_general_dilated x1 -> x0, matrix products: 42.6 us -> none  [shards(): lax.conv_general_dilated(padded[None], lax.all_gather(conv_weight, SPACE,...]
    all_to_all x0 -> x1, starting transfers between devices: none -> 34.5 us  [shards(): lax.all_to_all(packed, SPACE, split_axis=0, concat_axis=0, tiled=True)]
    all_gather x1 -> x0, waiting for transfers between devices: 30.7 us -> none  [shards(): lax.all_gather(conv_weight, SPACE, axis=3, tiled=True)]
    ppermute x2 -> x7, starting transfers between devices: 5.02 us -> 25.4 us  [the longest x3 16.2 us: shards(): weights += tuple((lax.ppermute(w, 'c', swap) for w in weights))]
    pallas_call x0 -> x3, Pallas kernels: none -> 12.3 us  [the longest x1 7.71 us: shards(): pl.pallas_call(conv_kernel, out_shape=jax.ShapeDtypeStruct((QUAD, 4 * COL...]
  transfers between devices with their start and end apart: 3 -> 8, of which waited for: 2 -> 2; matrix products, arithmetic and copies ran while one was open for 3% -> 0% of each run, Pallas kernels for 0% -> 1%
where the time goes in v1:
time: 152 us; the launch traced here: 151 us
  blocking collectives  72.9 us (48%)
  starting transfers between devices  59.8 us (39%)
  Pallas kernels  12.3 us (8%)
  local copies, waits for them, and re-layouts  2.95 us (2%)
  waiting for transfers between devices  2.72 us (2%)
    all_gather x1, blocking collectives, shards(): kin = lax.all_gather(mine, 'zh', axis=0)  50.7 us
    all_to_all x1, starting transfers between devices, shards(): lax.all_to_all(packed, SPACE, split_axis=0, concat_axis=0, tiled=True)  34.5 us
    ppermute x3, starting transfers between devices, shards(): weights += tuple((lax.ppermute(w, 'c', swap) for w in weights))  16.2 us
    all_to_all x1, blocking collectives, shards(): out = lax.all_to_all(out, 'gq', split_axis=0, concat_axis=0, tiled=True)  12 us
    all_gather x1, blocking collectives, shards(): active = lax.all_gather(active, 'gq', axis=0)  10.1 us
    pallas_call x1, Pallas kernels, shards(): pl.pallas_call(conv_kernel, out_shape=jax.ShapeDtypeStruct((QUAD, 4 * COL...  7.71 us
    ppermute x1, starting transfers between devices, shards(): after = lax.ppermute(active[:, 0], SPACE, left)  3.58 us
    ppermute x1, starting transfers between devices, shards(): high = lax.ppermute(kin[part:], CHIPS, down)  3.3 us
  transfers between devices with their start and end apart: 8, of which 2 were waited for; matrix products, arithmetic and copies ran while one was open for 0% of the time, Pallas kernels for 1%

profile of v1, /device:TPU:37, one launch (start us, length us, event | category | flops | bytes accessed | tf_op | source)
XLA Modules:
  0.0 151.3 jit_solution(6816090403590102299)
XLA Ops:
  0.0 2.5 %pack.1 = (bf16[64,2,640]{2,1,0:T(2,128)(2,1)}, bf16[27,8,128]{2,1,0:T(8,128)(2,1)}) custom-call(bf16[128,512]{1,0:T(8,128)(2,1)} %x_ref.1, bf16[27,8,512]{2,1,0:T(8,128)(2,1)} %bitcast.28), custom_call_target="tpu_custom_call" | custom-call | tf_op jit(solution)/shard_map/pack/pallas_call | solution.py:176
  2.5 34.5 %all-to-all-start = ((bf16[64,2,640]{2,1,0:T(2,128)(2,1)}), bf16[64,2,640]{2,1,0:T(2,128)(2,1)S(1)}, u32[]{:S(2)}, u32[]{:S(2)}) async-start(bf16[64,2,640]{2,1,0:T(2,128)(2,1)} %get-tuple-element.7), calls=%async_computation | async-start | bytes 327680 | tf_op jit(solution)/shard_map/all_to_all | solution.py:187
  36.9 50.7 %all-gather.1 = bf16[432,8,128]{2,1,0:T(8,128)(2,1)S(1)} all-gather(bf16[27,8,128]{2,1,0:T(8,128)(2,1)S(1)} %copy-done.8), channel_id=3, replica_groups=mesh['gh'=1,'gq'=4,'zh'=16,'zl'=2,'c'=2] {'zh'}, dimensions={0}, use_global_device_ids=true | all-gather | bytes 940032 | tf_op jit(solution)/shard_map/all_gather | solution.py:188
  87.7 0.1 fusion
  87.7 0.1 collective-permute-start.2
  87.9 3.3 %collective-permute-start.3 = (bf16[8,27,8,128]{3,2,1,0:T(8,128)(2,1)S(1)}, bf16[8,27,8,128]{3,2,1,0:T(8,128)(2,1)S(1)}, u32[]{:S(2)}, u32[]{:S(2)}) collective-permute-start(bf16[8,27,8,128]{3,2,1,0:T(8,128)(2,1)S(1)} %bitcast.26), channel_id=1, source_target_pairs={{2,0},{4,2},{6,4},{8,6},{10,8},{12,10},{14,12},{16,14},{18,16},{20... | collective-permute-start | bytes 1327112 | tf_op jit(solution)/shard_map/ppermute | solution.py:195
  91.2 9.8 %collective-permute-start.4 = (bf16[16,27,8,128]{3,2,1,0:T(8,128)(2,1)S(1)}, bf16[16,27,8,128]{3,2,1,0:T(8,128)(2,1)S(1)}, u32[]{:S(2)}, u32[]{:S(2)}) collective-permute-start(bf16[16,27,8,128]{3,2,1,0:T(8,128)(2,1)S(1)} %bitcast.21), channel_id=1, source_target_pairs={{0,1},{1,0},{2,3},{3,2},{4,5},{5,4},{6,7},{7,6},{8,9},{9,8},{10,11... | collective-permute-start | bytes 2654216 | tf_op jit(solution)/shard_map/ppermute | solution.py:197
  101.0 0.0 collective-permute-done.2.rest_1_
  101.0 6.3 %collective-permute-start.5 = (bf16[8,27,8,128]{3,2,1,0:T(8,128)(2,1)S(1)}, bf16[8,27,8,128]{3,2,1,0:T(8,128)(2,1)S(1)}, u32[]{:S(2)}, u32[]{:S(2)}) collective-permute-start(bf16[8,27,8,128]{3,2,1,0:T(8,128)(2,1)S(1)} %collective-permute-done.2.rest_1_), channel_id=1, source_target_pairs={{0,1},{1,0},{2,3},{3,2},{4,5},{5,4},{6,7},{7,6},{8,9},{9,8},{10,11... | collective-permute-start | bytes 1327112 | tf_op jit(solution)/shard_map/ppermute | solution.py:197
  107.3 0.0 collective-permute-done.3.rest_2_
  107.3 0.1 collective-permute-start.6
  107.4 0.7 copy-done.3
  108.1 2.1 %norm.1 = bf16[2,64,512]{2,1,0:T(8,128)(2,1)} custom-call(bf16[64,2,640]{2,1,0:T(2,128)(2,1)} %copy-done.3, f32[1,512]{1,0:T(1,128)} %bitcast.29, f32[1,512]{1,0:T(1,128)} %bitcast.30), custom_call_target="tpu_custom_call" | custom-call | tf_op jit(solution)/shard_map/norm/pallas_call | solution.py:199
  110.2 10.1 %all-gather = bf16[8,64,512]{2,1,0:T(8,128)(2,1)S(1)} all-gather(bf16[2,64,512]{2,1,0:T(8,128)(2,1)} %norm.1), channel_id=2, replica_groups=mesh['gh'=1,'gq'=4,'zh'=16,'zl'=2,'c'=2] {'gq'}, dimensions={0}, use_global_device_ids=true | all-gather | bytes 655360 | tf_op jit(solution)/shard_map/all_gather | solution.py:206
  120.3 0.8 copy-done.1
  121.1 3.6 %collective-permute-start.1 = (bf16[4,64,512]{2,1,0:T(8,128)(2,1)S(1)}, bf16[4,64,512]{2,1,0:T(8,128)(2,1)S(1)}, u32[]{:S(2)}, u32[]{:S(2)}) collective-permute-start(bf16[4,64,512]{2,1,0:T(8,128)(2,1)S(1)} %get-tuple-element.11), channel_id=1, source_target_pairs={{1,0},{2,1},{3,2},{4,3},{5,4},{6,5},{7,6},{8,7},{9,8},{10,9},{11,1... | collective-permute-start | bytes 786440 | tf_op jit(solution)/shard_map/ppermute | solution.py:210
  124.7 2.2 %collective-permute-start = (bf16[4,64,512]{2,1,0:T(8,128)(2,1)S(1)}, bf16[4,64,512]{2,1,0:T(8,128)(2,1)}, u32[]{:S(2)}, u32[]{:S(2)}) collective-permute-start(bf16[4,64,512]{2,1,0:T(8,128)(2,1)S(1)} %get-tuple-element.12), channel_id=1, source_target_pairs={{0,1},{1,2},{2,3},{3,4},{4,5},{5,6},{6,7},{7,8},{8,9},{9,10},{10,1... | collective-permute-start | bytes 786440 | tf_op jit(solution)/shard_map/ppermute | solution.py:209
  126.9 0.5 bitcast_convert_fusion.b_ref
  127.4 1.5 collective-permute-done.1.xr_ref
  128.9 1.2 collective-permute-done.xl_ref
  130.2 7.7 %conv.1 = bf16[4,512,128]{2,1,0:T(8,128)(2,1)} custom-call(bf16[4,2,64,512]{3,2,1,0:T(8,128)(2,1)} %bitcast.24, bf16[4,64,512]{2,1,0:T(8,128)(2,1)} %collective-permute-done.xl_ref, bf16[4,64,512]{2,1,0:T(8,128)(2,1)} %copy-done.7, f32[4,128]{1,0:T(4,128)} %bitcast_convert_fusion.b_ref, bf16[16,27,8,128]{3,2,1,0:T(8,128)(2,1)} %bitcast.22, ...), custom_call_target="tpu_custom_call" | custom-call | tf_op jit(solution)/shard_map/conv/pallas_call | solution.py:213
  137.9 12.0 %all_to_all.10 = bf16[4,512,128]{2,1,0:T(8,128)(2,1)S(1)} all-to-all(bf16[4,512,128]{2,1,0:T(8,128)(2,1)} %conv.1), channel_id=1, replica_groups=mesh['gh'=1,'gq'=4,'zh'=16,'zl'=2,'c'=2] {'gq'}, dimensions={0} | all-to-all | bytes 1048576 | tf_op jit(solution)/shard_map/all_to_all | solution.py:228
  149.9 0.4 copy.13
  150.3 1.0 reshape.18
  (23 shorter events, 0.1 us)
Async XLA Ops:
  2.5 34.5 %copy-start.8 = (bf16[27,8,128]{2,1,0:T(8,128)(2,1)S(1)}, bf16[27,8,128]{2,1,0:T(8,128)(2,1)}, u32[]{:S(2)}) copy-start(bf16[27,8,128]{2,1,0:T(8,128)(2,1)} %get-tuple-element.8) | copy-start | bytes 165892
  2.5 104.9 %all-to-all-start = ((bf16[64,2,640]{2,1,0:T(2,128)(2,1)}), bf16[64,2,640]{2,1,0:T(2,128)(2,1)S(1)}, u32[]{:S(2)}, u32[]{:S(2)}) async-start(bf16[64,2,640]{2,1,0:T(2,128)(2,1)} %get-tuple-element.7), calls=%async_computation | async-start | bytes 327680 | tf_op jit(solution)/shard_map/all_to_all | solution.py:187
  87.7 3.5 %copy-start = (bf16[432,8,128]{2,1,0:T(8,128)(2,1)}, bf16[432,8,128]{2,1,0:T(8,128)(2,1)S(1)}, u32[]{:S(2)}) copy-start(bf16[432,8,128]{2,1,0:T(8,128)(2,1)S(1)} %all-gather.1) | copy-start | bytes 2654212
  87.7 13.2 %collective-permute-start.2 = (bf16[8,27,8,128]{3,2,1,0:T(8,128)(2,1)S(1)}, bf16[8,27,8,128]{3,2,1,0:T(8,128)(2,1)S(1)}, u32[]{:S(2)}, u32[]{:S(2)}) collective-permute-start(bf16[8,27,8,128]{3,2,1,0:T(8,128)(2,1)S(1)} %bitcast.27), channel_id=1, source_target_pairs={{0,2},{2,4},{4,6},{6,8},{8,10},{10,12},{12,14},{14,16},{16,18},{18... | collective-permute-start | bytes 1327112 | tf_op jit(solution)/shard_map/ppermute | solution.py:194
  87.9 19.4 %collective-permute-start.3 = (bf16[8,27,8,128]{3,2,1,0:T(8,128)(2,1)S(1)}, bf16[8,27,8,128]{3,2,1,0:T(8,128)(2,1)S(1)}, u32[]{:S(2)}, u32[]{:S(2)}) collective-permute-start(bf16[8,27,8,128]{3,2,1,0:T(8,128)(2,1)S(1)} %bitcast.26), channel_id=1, source_target_pairs={{2,0},{4,2},{6,4},{8,6},{10,8},{12,10},{14,12},{16,14},{18,16},{20... | collective-permute-start | bytes 1327112 | tf_op jit(solution)/shard_map/ppermute | solution.py:195
  91.2 36.2 %collective-permute-start.4 = (bf16[16,27,8,128]{3,2,1,0:T(8,128)(2,1)S(1)}, bf16[16,27,8,128]{3,2,1,0:T(8,128)(2,1)S(1)}, u32[]{:S(2)}, u32[]{:S(2)}) collective-permute-start(bf16[16,27,8,128]{3,2,1,0:T(8,128)(2,1)S(1)} %bitcast.21), channel_id=1, source_target_pairs={{0,1},{1,0},{2,3},{3,2},{4,5},{5,4},{6,7},{7,6},{8,9},{9,8},{10,11... | collective-permute-start | bytes 2654216 | tf_op jit(solution)/shard_map/ppermute | solution.py:197
  101.0 29.2 %copy-start.4 = (bf16[8,27,8,128]{3,2,1,0:T(8,128)(2,1)}, bf16[8,27,8,128]{3,2,1,0:T(8,128)(2,1)S(1)}, u32[]{:S(2)}) copy-start(bf16[8,27,8,128]{3,2,1,0:T(8,128)(2,1)S(1)} %collective-permute-done.2.rest_1_) | copy-start | bytes 1327108
  101.0 26.4 %collective-permute-start.5 = (bf16[8,27,8,128]{3,2,1,0:T(8,128)(2,1)S(1)}, bf16[8,27,8,128]{3,2,1,0:T(8,128)(2,1)S(1)}, u32[]{:S(2)}, u32[]{:S(2)}) collective-permute-start(bf16[8,27,8,128]{3,2,1,0:T(8,128)(2,1)S(1)} %collective-permute-done.2.rest_1_), channel_id=1, source_target_pairs={{0,1},{1,0},{2,3},{3,2},{4,5},{5,4},{6,7},{7,6},{8,9},{9,8},{10,11... | collective-permute-start | bytes 1327112 | tf_op jit(solution)/shard_map/ppermute | solution.py:197
  107.3 22.9 %copy-start.5 = (bf16[8,27,8,128]{3,2,1,0:T(8,128)(2,1)}, bf16[8,27,8,128]{3,2,1,0:T(8,128)(2,1)S(1)}, u32[]{:S(2)}) copy-start(bf16[8,27,8,128]{3,2,1,0:T(8,128)(2,1)S(1)} %collective-permute-done.3.rest_2_) | copy-start | bytes 1327108
  107.3 20.2 %collective-permute-start.6 = (bf16[8,27,8,128]{3,2,1,0:T(8,128)(2,1)S(1)}, bf16[8,27,8,128]{3,2,1,0:T(8,128)(2,1)}, u32[]{:S(2)}, u32[]{:S(2)}) collective-permute-start(bf16[8,27,8,128]{3,2,1,0:T(8,128)(2,1)S(1)} %collective-permute-done.3.rest_2_), channel_id=1, source_target_pairs={{0,1},{1,0},{2,3},{3,2},{4,5},{5,4},{6,7},{7,6},{8,9},{9,8},{10,11... | collective-permute-start | bytes 1327112 | tf_op jit(solution)/shard_map/ppermute | solution.py:197
  107.4 0.7 copy-start.3
  120.3 0.8 copy-start.1
  121.1 5.8 %copy-start.9 = (bf16[512]{0:T(512)(128)(2,1)S(1)}, bf16[512]{0:T(512)(128)(2,1)}, u32[]{:S(2)}) copy-start(bf16[512]{0:T(512)(128)(2,1)} %param.9) | copy-start | bytes 3076
  121.1 7.8 %collective-permute-start.1 = (bf16[4,64,512]{2,1,0:T(8,128)(2,1)S(1)}, bf16[4,64,512]{2,1,0:T(8,128)(2,1)S(1)}, u32[]{:S(2)}, u32[]{:S(2)}) collective-permute-start(bf16[4,64,512]{2,1,0:T(8,128)(2,1)S(1)} %get-tuple-element.11), channel_id=1, source_target_pairs={{1,0},{2,1},{3,2},{4,3},{5,4},{6,5},{7,6},{8,7},{9,8},{10,9},{11,1... | collective-permute-start | bytes 786440 | tf_op jit(solution)/shard_map/ppermute | solution.py:210
  124.7 5.5 %collective-permute-start = (bf16[4,64,512]{2,1,0:T(8,128)(2,1)S(1)}, bf16[4,64,512]{2,1,0:T(8,128)(2,1)}, u32[]{:S(2)}, u32[]{:S(2)}) collective-permute-start(bf16[4,64,512]{2,1,0:T(8,128)(2,1)S(1)} %get-tuple-element.12), channel_id=1, source_target_pairs={{0,1},{1,2},{2,3},{3,4},{4,5},{5,6},{6,7},{7,8},{8,9},{9,10},{10,1... | collective-permute-start | bytes 786440 | tf_op jit(solution)/shard_map/ppermute | solution.py:209
  127.4 2.7 %copy-start.6 = (bf16[8,27,8,128]{3,2,1,0:T(8,128)(2,1)}, bf16[8,27,8,128]{3,2,1,0:T(8,128)(2,1)S(1)}, u32[]{:S(2)}) copy-start(bf16[8,27,8,128]{3,2,1,0:T(8,128)(2,1)S(1)} %collective-permute-done.5.rest_4_) | copy-start | bytes 1327108
  127.4 2.7 %copy-start.2 = (bf16[16,27,8,128]{3,2,1,0:T(8,128)(2,1)}, bf16[16,27,8,128]{3,2,1,0:T(8,128)(2,1)S(1)}, u32[]{:S(2)}) copy-start(bf16[16,27,8,128]{3,2,1,0:T(8,128)(2,1)S(1)} %collective-permute-done.4.rest_3_) | copy-start | bytes 2654212
  128.9 1.2 copy-start.7

commit v2 on v1

--- a/solution.py
+++ b/solution.py
@@ -96,7 +96,7 @@
 
 
 def conv_kernel(xa_ref, xl_ref, xr_ref, b_ref, *rest):
-    parts, (o_ref, w_ref, x_ref, p0, p1, p2, sem) = rest[:6], rest[6:]
+    parts, (o_ref, w_ref, x_ref, p0, p1, p2, y_ref, sem) = rest[:6], rest[6:]
     core, parity, quarter = (lax.axis_index(n) for n in ("c", "zl", "gq"))
     place = lax.axis_index(SPACE)
     last = lax.axis_size(SPACE) - 1
@@ -158,11 +158,27 @@
                 above = jnp.where(row == 0, t[0], pltpu.roll(t[0], 1, 0))
                 below = jnp.where(row == ROWS - 1, t[2], pltpu.roll(t[2], CELLS - 1, 0))
                 for up, value in enumerate((above + t[1] + t[2], t[0] + t[1] + below)):
-                    at = (up * 2 * COLS + 2 * j + side) * CELLS
-                    o_ref[v, at : at + CELLS] = (value + bias).astype(BF16)
+                    at = up * 2 * COLS + 2 * j + side
+                    y_ref[pl.ds(at, CELLS, stride=4 * COLS), :] = value + bias
+        o_ref[v] = y_ref[...].reshape(2 * CELLS, 2 * COLS, SLICE).astype(BF16)
         return 0
 
     lax.fori_loop(0, QUAD, combine, 0)
+
+
+def spread_kernel(i_ref, o_ref, sem):
+    copies = [
+        pltpu.make_async_copy(i_ref.at[q], o_ref.at[:, :, pl.ds(q * SLICE, SLICE)], sem)
+        for q in range(QUAD)
+    ]
+    for copy in copies:
+        copy.start()
+    for copy in copies:
+        copy.wait()
+
+
+def room(mebibytes):
+    return pltpu.CompilerParams(vmem_limit_bytes=mebibytes * 2**20)
 
 
 def vmem(n):
@@ -181,6 +197,7 @@
         ),
         in_specs=vmem(2),
         out_specs=tuple(vmem(2)),
+        compiler_params=room(4),
         name="pack",
     )(hidden, conv_weight.reshape(TAPS, share, CHANNELS))
 
@@ -193,17 +210,18 @@
     part = kin.shape[0] // 2
     low = lax.ppermute(kin[:part], CHIPS, up)
     high = lax.ppermute(kin[part:], CHIPS, down)
-    weights = (kin, low, high)
-    weights += tuple(lax.ppermute(w, "c", swap) for w in weights)
-
     active = pl.pallas_call(
         norm_kernel,
         out_shape=jax.ShapeDtypeStruct((COLS, CELLS, CHANNELS), BF16),
         in_specs=vmem(3),
         out_specs=vmem(1)[0],
+        compiler_params=room(4),
         name="norm",
     )(tiles, norm_gain[None], norm_shift[None])
     active = lax.all_gather(active, "gq", axis=0)
+    active, low, high = lax.optimization_barrier((active, low, high))
+    weights = (kin, low, high)
+    weights += tuple(lax.ppermute(w, "c", swap) for w in weights)
     right = [(i, i + 1) for i in range(devices - 1)]
     left = [(j, i) for i, j in right]
     before = lax.ppermute(active[:, 1], SPACE, right)
@@ -212,7 +230,7 @@
     half = QUAD * CELLS
     out = pl.pallas_call(
         conv_kernel,
-        out_shape=jax.ShapeDtypeStruct((QUAD, 4 * COLS * CELLS, SLICE), BF16),
+        out_shape=jax.ShapeDtypeStruct((QUAD, 2 * CELLS, 2 * COLS, SLICE), BF16),
         in_specs=vmem(4) + [pl.BlockSpec(memory_space=pltpu.HBM)] * 6,
         out_specs=vmem(1)[0],
         scratch_shapes=[
@@ -221,13 +239,22 @@
             pltpu.VMEM((3, 3 * half, SLICE), F32),
             pltpu.VMEM((3, 2 * half, SLICE), F32),
             pltpu.VMEM((3, 3 * half, SLICE), F32),
+            pltpu.VMEM((4 * COLS * CELLS, SLICE), F32),
             pltpu.SemaphoreType.DMA,
         ],
+        compiler_params=room(24),
         name="conv",
     )(active, before, after, conv_bias.astype(F32).reshape(QUAD, SLICE), *weights)
     out = lax.all_to_all(out, "gq", split_axis=0, concat_axis=0, tiled=True)
-    out = out.reshape(QUAD, 2, 2 * COLS, FRAMES, ROWS, SLICE)
-    out = out.transpose(3, 4, 1, 2, 0, 5)
+    out = pl.pallas_call(
+        spread_kernel,
+        out_shape=jax.ShapeDtypeStruct((2 * CELLS, 2 * COLS, CHANNELS), BF16),
+        in_specs=vmem(1),
+        out_specs=pl.BlockSpec(memory_space=pltpu.HBM),
+        scratch_shapes=[pltpu.SemaphoreType.DMA],
+        compiler_params=room(4),
+        name="spread",
+    )(out)
     return out.reshape(FRAMES, 2 * ROWS, 2 * COLS, CHANNELS)
 
 

time: 152 us -> 139 us (0.914)
  blocking collectives: 72.9 us -> 68.3 us
  Pallas kernels: 12.3 us -> 8.04 us
  starting transfers between devices: 59.8 us -> 55.8 us
    ppermute x3, starting transfers between devices: 16.2 us -> 12.6 us  [shards(): weights += tuple((lax.ppermute(w, 'c', swap) for w in weights))]
    all_to_all x1, blocking collectives: 12 us -> 8.93 us  [shards(): out = lax.all_to_all(out, 'gq', split_axis=0, concat_axis=0, tiled=True)]
    pallas_call x1 -> x2, Pallas kernels: 7.71 us -> 6.06 us  [the longest x1 5.27 us: shards(): pl.pallas_call(conv_kernel, out_shape=jax.ShapeDtypeStruct((QUAD, 2 * CEL...]
    pallas_call x1, Pallas kernels: 2.08 us -> 0.51 us  [shards(): pl.pallas_call(norm_kernel, out_shape=jax.ShapeDtypeStruct((COLS, CELLS,...]
  transfers between devices with their start and end apart: 8 -> 8, of which waited for: 2 -> 2; matrix products, arithmetic and copies ran while one was open for 0% -> 1% of each run, Pallas kernels for 1% -> 0%
where the time goes in v2:
time: 139 us; the launch traced here: 138 us
  blocking collectives  68.3 us (49%)
  starting transfers between devices  55.8 us (40%)
  Pallas kernels  8.04 us (6%)
  waiting for transfers between devices  3.28 us (2%)
  local copies, waits for them, and re-layouts  2.71 us (2%)
    all_gather x1, blocking collectives, shards(): kin = lax.all_gather(mine, 'zh', axis=0)  50.7 us
    all_to_all x1, starting transfers between devices, shards(): lax.all_to_all(packed, SPACE, split_axis=0, concat_axis=0, tiled=True)  34.3 us
    ppermute x3, starting transfers between devices, shards(): weights += tuple((lax.ppermute(w, 'c', swap) for w in weights))  12.6 us
    all_to_all x1, blocking collectives, shards(): out = lax.all_to_all(out, 'gq', split_axis=0, concat_axis=0, tiled=True)  8.93 us
    all_gather x1, blocking collectives, shards(): active = lax.all_gather(active, 'gq', axis=0)  8.68 us
    pallas_call x1, Pallas kernels, shards(): pl.pallas_call(conv_kernel, out_shape=jax.ShapeDtypeStruct((QUAD, 2 * CEL...  5.27 us
    ppermute x1, starting transfers between devices, shards(): before = lax.ppermute(active[:, 1], SPACE, right)  3.32 us
    ppermute x1, starting transfers between devices, shards(): high = lax.ppermute(kin[part:], CHIPS, down)  3.19 us
  transfers between devices with their start and end apart: 8, of which 2 were waited for; matrix products, arithmetic and copies ran while one was open for 1% of the time, Pallas kernels for 0%

profile of v2, /device:TPU:37, one launch (start us, length us, event | category | flops | bytes accessed | tf_op | source)
XLA Modules:
  0.0 138.2 jit_solution(2619249847959533711)
XLA Ops:
  0.0 0.9 copy-done
  0.9 0.9 copy-done.1
  1.8 1.5 %pack.1 = (bf16[64,2,640]{2,1,0:T(2,128)(2,1)}, bf16[27,8,128]{2,1,0:T(8,128)(2,1)S(1)}) custom-call(bf16[128,512]{1,0:T(8,128)(2,1)S(1)} %copy-done.1, bf16[27,8,512]{2,1,0:T(8,128)(2,1)S(1)} %bitcast.19), custom_call_target="tpu_custom_call" | custom-call | tf_op jit(solution)/shard_map/pack/pallas_call | solution.py:192
  3.3 34.3 %all-to-all-start = ((bf16[64,2,640]{2,1,0:T(2,128)(2,1)}), bf16[64,2,640]{2,1,0:T(2,128)(2,1)S(1)}, u32[]{:S(2)}, u32[]{:S(2)}) async-start(bf16[64,2,640]{2,1,0:T(2,128)(2,1)} %get-tuple-element.10), calls=%async_computation | async-start | bytes 327680 | tf_op jit(solution)/shard_map/all_to_all | solution.py:204
  37.7 50.7 %all-gather.1 = bf16[432,8,128]{2,1,0:T(8,128)(2,1)S(1)} all-gather(bf16[27,8,128]{2,1,0:T(8,128)(2,1)S(1)} %get-tuple-element.11), channel_id=3, replica_groups=mesh['gh'=1,'gq'=4,'zh'=16,'zl'=2,'c'=2] {'zh'}, dimensions={0}, use_global_device_ids=true | all-gather | bytes 940032 | tf_op jit(solution)/shard_map/all_gather | solution.py:205
  88.4 0.8 fusion
  89.2 0.0 collective-permute-start
  89.2 3.2 %collective-permute-start.1 = (bf16[8,27,8,128]{3,2,1,0:T(8,128)(2,1)S(1)}, bf16[8,27,8,128]{3,2,1,0:T(8,128)(2,1)S(1)}, u32[]{:S(2)}, u32[]{:S(2)}) collective-permute-start(bf16[8,27,8,128]{3,2,1,0:T(8,128)(2,1)S(1)} %bitcast.22), channel_id=1, source_target_pairs={{2,0},{4,2},{6,4},{8,6},{10,8},{12,10},{14,12},{16,14},{18,16},{20... | collective-permute-start | bytes 1327112 | tf_op jit(solution)/shard_map/ppermute | solution.py:212
  92.4 9.9 %collective-permute-start.4 = (bf16[16,27,8,128]{3,2,1,0:T(8,128)(2,1)S(1)}, bf16[16,27,8,128]{3,2,1,0:T(8,128)(2,1)S(1)}, u32[]{:S(2)}, u32[]{:S(2)}) collective-permute-start(bf16[16,27,8,128]{3,2,1,0:T(8,128)(2,1)S(1)} %bitcast.15), channel_id=1, source_target_pairs={{0,1},{1,0},{2,3},{3,2},{4,5},{5,4},{6,7},{7,6},{8,9},{9,8},{10,11... | collective-permute-start | bytes 2654216 | tf_op jit(solution)/shard_map/ppermute | solution.py:224
  102.3 0.0 all-to-all-done.r_ref
  102.3 0.5 norm.1
  102.9 8.7 %all-gather = bf16[8,64,512]{2,1,0:T(8,128)(2,1)S(1)} all-gather(bf16[2,64,512]{2,1,0:T(8,128)(2,1)S(1)} %norm.1), channel_id=2, replica_groups=mesh['gh'=1,'gq'=4,'zh'=16,'zl'=2,'c'=2] {'gq'}, dimensions={0}, use_global_device_ids=true | all-gather | bytes 655360 | tf_op jit(solution)/shard_map/all_gather | solution.py:221
  111.5 0.0 collective-permute-done.rest_1_
  111.5 0.0 collective-permute-done.1.rest_2_
  111.6 2.5 %collective-permute-start.5 = (bf16[8,27,8,128]{3,2,1,0:T(8,128)(2,1)S(1)}, bf16[8,27,8,128]{3,2,1,0:T(8,128)(2,1)S(1)}, u32[]{:S(2)}, u32[]{:S(2)}) collective-permute-start(bf16[8,27,8,128]{3,2,1,0:T(8,128)(2,1)S(1)} %collective-permute-done.rest_1_), channel_id=1, source_target_pairs={{0,1},{1,0},{2,3},{3,2},{4,5},{5,4},{6,7},{7,6},{8,9},{9,8},{10,11... | collective-permute-start | bytes 1327112 | tf_op jit(solution)/shard_map/ppermute | solution.py:224
  114.1 0.1 collective-permute-start.6
  114.3 0.0 copy-start.4
  114.3 2.3 %collective-permute-start.3 = (bf16[4,64,512]{2,1,0:T(8,128)(2,1)S(1)}, bf16[4,64,512]{2,1,0:T(8,128)(2,1)S(1)}, u32[]{:S(2)}, u32[]{:S(2)}) collective-permute-start(bf16[4,64,512]{2,1,0:T(8,128)(2,1)S(1)} %get-tuple-element.17), channel_id=1, source_target_pairs={{1,0},{2,1},{3,2},{4,3},{5,4},{6,5},{7,6},{8,7},{9,8},{10,9},{11,1... | collective-permute-start | bytes 786440 | tf_op jit(solution)/shard_map/ppermute | solution.py:228
  116.6 3.3 %collective-permute-start.2 = (bf16[4,64,512]{2,1,0:T(8,128)(2,1)S(1)}, bf16[4,64,512]{2,1,0:T(8,128)(2,1)S(1)}, u32[]{:S(2)}, u32[]{:S(2)}) collective-permute-start(bf16[4,64,512]{2,1,0:T(8,128)(2,1)S(1)} %get-tuple-element.18), channel_id=1, source_target_pairs={{0,1},{1,2},{2,3},{3,4},{4,5},{5,6},{6,7},{7,8},{8,9},{9,10},{10,1... | collective-permute-start | bytes 786440 | tf_op jit(solution)/shard_map/ppermute | solution.py:227
  120.0 2.1 %collective-permute-done.3.xr_ref = bf16[4,64,512]{2,1,0:T(8,128)(2,1)S(1)} collective-permute-done((bf16[4,64,512]{2,1,0:T(8,128)(2,1)S(1)}, bf16[4,64,512]{2,1,0:T(8,128)(2,1)S(1)}, u32[]{:S(2)}, u32[]{:S(2)}) %collective-permute-start.3) | collective-permute-done | bytes 262176 | tf_op jit(solution)/shard_map/ppermute | solution.py:228
  122.0 1.2 collective-permute-done.2.xl_ref
  123.2 5.3 %conv.1 = bf16[4,128,4,128]{3,2,1,0:T(4,128)(2,1)S(1)} custom-call(bf16[4,2,64,512]{3,2,1,0:T(8,128)(2,1)S(1)} %bitcast.18, bf16[4,64,512]{2,1,0:T(8,128)(2,1)S(1)} %collective-permute-done.2.xl_ref, bf16[4,64,512]{2,1,0:T(8,128)(2,1)S(1)} %collective-permute-done.3.xr_ref, f32[4,128]{1,0:T(4,128)S(1)} %bitcast_convert_fusion.b_ref, ...), custom_call_target="tpu_custom_call" | custom-call | tf_op jit(solution)/shard_map/conv/pallas_call | solution.py:231
  128.5 8.9 %all_to_all.10.i_ref = bf16[4,128,4,128]{3,2,1,0:T(4,128)(2,1)S(1)} all-to-all(bf16[4,128,4,128]{3,2,1,0:T(4,128)(2,1)S(1)} %conv.1), channel_id=1, replica_groups=mesh['gh'=1,'gq'=4,'zh'=16,'zl'=2,'c'=2] {'gq'}, dimensions={0} | all-to-all | bytes 1048576 | tf_op jit(solution)/shard_map/all_to_all | solution.py:248
  137.4 0.8 spread.1
  (12 shorter events, 0.1 us)
Async XLA Ops:
  0.0 0.9 copy-start
  0.9 0.9 copy-start.1
  3.3 99.0 %all-to-all-start = ((bf16[64,2,640]{2,1,0:T(2,128)(2,1)}), bf16[64,2,640]{2,1,0:T(2,128)(2,1)S(1)}, u32[]{:S(2)}, u32[]{:S(2)}) async-start(bf16[64,2,640]{2,1,0:T(2,128)(2,1)} %get-tuple-element.10), calls=%async_computation | async-start | bytes 327680 | tf_op jit(solution)/shard_map/all_to_all | solution.py:204
  89.2 22.3 %collective-permute-start = (bf16[8,27,8,128]{3,2,1,0:T(8,128)(2,1)}, bf16[8,27,8,128]{3,2,1,0:T(8,128)(2,1)S(1)}, u32[]{:S(2)}, u32[]{:S(2)}) collective-permute-start(bf16[8,27,8,128]{3,2,1,0:T(8,128)(2,1)} %bitcast.4), channel_id=1, source_target_pairs={{0,2},{2,4},{4,6},{6,8},{8,10},{10,12},{12,14},{14,16},{16,18},{18... | collective-permute-start | bytes 1327112 | tf_op jit(solution)/shard_map/ppermute | solution.py:211
  89.2 22.3 %collective-permute-start.1 = (bf16[8,27,8,128]{3,2,1,0:T(8,128)(2,1)S(1)}, bf16[8,27,8,128]{3,2,1,0:T(8,128)(2,1)S(1)}, u32[]{:S(2)}, u32[]{:S(2)}) collective-permute-start(bf16[8,27,8,128]{3,2,1,0:T(8,128)(2,1)S(1)} %bitcast.22), channel_id=1, source_target_pairs={{2,0},{4,2},{6,4},{8,6},{10,8},{12,10},{14,12},{16,14},{18,16},{20... | collective-permute-start | bytes 1327112 | tf_op jit(solution)/shard_map/ppermute | solution.py:212
  92.4 9.9 %copy-start.3 = (f32[512]{0:T(512)S(1)}, f32[512]{0:T(512)}, u32[]{:S(2)}) copy-start(f32[512]{0:T(512)} %param.7) | copy-start | bytes 6148
  92.4 9.9 %copy-start.2 = (f32[512]{0:T(512)S(1)}, f32[512]{0:T(512)}, u32[]{:S(2)}) copy-start(f32[512]{0:T(512)} %param.6) | copy-start | bytes 6148
  92.4 27.6 %collective-permute-start.4 = (bf16[16,27,8,128]{3,2,1,0:T(8,128)(2,1)S(1)}, bf16[16,27,8,128]{3,2,1,0:T(8,128)(2,1)S(1)}, u32[]{:S(2)}, u32[]{:S(2)}) collective-permute-start(bf16[16,27,8,128]{3,2,1,0:T(8,128)(2,1)S(1)} %bitcast.15), channel_id=1, source_target_pairs={{0,1},{1,0},{2,3},{3,2},{4,5},{5,4},{6,7},{7,6},{8,9},{9,8},{10,11... | collective-permute-start | bytes 2654216 | tf_op jit(solution)/shard_map/ppermute | solution.py:224
  111.6 11.7 %collective-permute-start.5 = (bf16[8,27,8,128]{3,2,1,0:T(8,128)(2,1)S(1)}, bf16[8,27,8,128]{3,2,1,0:T(8,128)(2,1)S(1)}, u32[]{:S(2)}, u32[]{:S(2)}) collective-permute-start(bf16[8,27,8,128]{3,2,1,0:T(8,128)(2,1)S(1)} %collective-permute-done.rest_1_), channel_id=1, source_target_pairs={{0,1},{1,0},{2,3},{3,2},{4,5},{5,4},{6,7},{7,6},{8,9},{9,8},{10,11... | collective-permute-start | bytes 1327112 | tf_op jit(solution)/shard_map/ppermute | solution.py:224
  114.1 9.2 %collective-permute-start.6 = (bf16[8,27,8,128]{3,2,1,0:T(8,128)(2,1)S(1)}, bf16[8,27,8,128]{3,2,1,0:T(8,128)(2,1)S(1)}, u32[]{:S(2)}, u32[]{:S(2)}) collective-permute-start(bf16[8,27,8,128]{3,2,1,0:T(8,128)(2,1)S(1)} %collective-permute-done.1.rest_2_), channel_id=1, source_target_pairs={{0,1},{1,0},{2,3},{3,2},{4,5},{5,4},{6,7},{7,6},{8,9},{9,8},{10,11... | collective-permute-start | bytes 1327112 | tf_op jit(solution)/shard_map/ppermute | solution.py:224
  114.3 5.7 %copy-start.4 = (bf16[512]{0:T(512)(128)(2,1)S(1)}, bf16[512]{0:T(512)(128)(2,1)}, u32[]{:S(2)}) copy-start(bf16[512]{0:T(512)(128)(2,1)} %param.9) | copy-start | bytes 3076
  114.3 7.7 %collective-permute-start.3 = (bf16[4,64,512]{2,1,0:T(8,128)(2,1)S(1)}, bf16[4,64,512]{2,1,0:T(8,128)(2,1)S(1)}, u32[]{:S(2)}, u32[]{:S(2)}) collective-permute-start(bf16[4,64,512]{2,1,0:T(8,128)(2,1)S(1)} %get-tuple-element.17), channel_id=1, source_target_pairs={{1,0},{2,1},{3,2},{4,3},{5,4},{6,5},{7,6},{8,7},{9,8},{10,9},{11,1... | collective-permute-start | bytes 786440 | tf_op jit(solution)/shard_map/ppermute | solution.py:228
  116.6 6.6 %collective-permute-start.2 = (bf16[4,64,512]{2,1,0:T(8,128)(2,1)S(1)}, bf16[4,64,512]{2,1,0:T(8,128)(2,1)S(1)}, u32[]{:S(2)}, u32[]{:S(2)}) collective-permute-start(bf16[4,64,512]{2,1,0:T(8,128)(2,1)S(1)} %get-tuple-element.18), channel_id=1, source_target_pairs={{0,1},{1,2},{2,3},{3,4},{4,5},{5,6},{6,7},{7,8},{8,9},{9,10},{10,1... | collective-permute-start | bytes 786440 | tf_op jit(solution)/shard_map/ppermute | solution.py:227

commit v3 on v2

v3 whole, which is shorter than its diff:
```python
import jax
import jax.numpy as jnp
from jax import lax
from jax.experimental import pallas as pl
from jax.experimental.pallas import tpu as pltpu
from jax.sharding import Mesh
from jax.sharding import PartitionSpec as P

CHANNELS = 512
GROUPS = 32
FRAMES = 4
ROWS = 16
COLS = 2
WIDE = 2 * COLS
CLASSES = 4
CELLS = FRAMES * ROWS
MEMBERS = CHANNELS // GROUPS
QUAD = 4
SLICE = CHANNELS // QUAD
TAPS = 27
SPACE = ("zh", "zl", "c")
CHIPS = ("zh", "zl")
EPSILON = 1e-06
F32, BF16 = jnp.float32, jnp.bfloat16
HIGHEST = lax.Precision.HIGHEST


def iota(shape, dim):
    return lax.broadcasted_iota(jnp.int32, shape, dim)


def dot(a, b, precision=None):
    return jnp.dot(a, b, preferred_element_type=F32, precision=precision)


def in_pieces(v):
    high = v.astype(BF16)
    rest = v - high.astype(F32)
    middle = rest.astype(BF16)
    low = (rest - middle.astype(F32)).astype(BF16)
    lane = iota(v.shape, 1)
    return jnp.where(
        lane < GROUPS,
        high.astype(F32),
        jnp.where(lane < 2 * GROUPS, middle.astype(F32), low.astype(F32)),
    ).astype(BF16)


def pack_kernel(x_ref, y_ref, o_ref):
    rows = [ref[...].astype(F32) for ref in (x_ref, y_ref)]
    cells = x_ref.shape[0]
    gather = jnp.where(
        (iota((CHANNELS, 128), 0) // MEMBERS == iota((CHANNELS, 128), 1) % GROUPS)
        & (iota((CHANNELS, 128), 1) < 3 * GROUPS),
        1.0,
        0.0,
    )
    spread = jnp.where(iota((128, CHANNELS), 0) == iota((128, CHANNELS), 1) // MEMBERS, 1.0, 0.0)

    def totals(values):
        return jnp.broadcast_to(sum(jnp.sum(v, axis=0, keepdims=True) for v in values), (8, CHANNELS))

    mean = dot(totals(rows), gather, HIGHEST) * (1.0 / (2 * cells * MEMBERS))
    away = [v - dot(mean, spread, HIGHEST)[:1] for v in rows]
    second = dot(totals([v * v for v in away]), gather, HIGHEST)
    stats = jnp.concatenate([in_pieces(mean)[:1], in_pieces(second)[:1]], axis=0)
    for d in range(cells // WIDE):
        for j in range(WIDE):
            c = d * WIDE + j
            pair = jnp.concatenate([v[c : c + 1] for v in rows], axis=0)
            o_ref[d, :, j * CHANNELS : (j + 1) * CHANNELS] = pair.astype(BF16)
        o_ref[d, :, WIDE * CHANNELS :] = stats


def norm_kernel(r_ref, gain_ref, shift_ref, o_ref):
    r = r_ref[...].astype(F32)
    sources = r.shape[0]

    def whole(v):
        return v + pltpu.roll(v, 128 - GROUPS, 1) + pltpu.roll(v, 128 - 2 * GROUPS, 1)

    means = whole(r[:, 0, WIDE * CHANNELS :])
    seconds = whole(r[:, 1, WIDE * CHANNELS :])
    each = float(2 * sources * WIDE * MEMBERS)
    mean = jnp.sum(means, axis=0, keepdims=True) * (1.0 / sources)
    second = jnp.sum(seconds, axis=0, keepdims=True) + each * jnp.sum(
        (means - mean) * (means - mean), axis=0, keepdims=True
    )
    real = iota((1, 128), 1) < GROUPS
    mean = jnp.where(real, mean, 0.0)
    scale = lax.rsqrt(jnp.where(real, second, 0.0) * (1.0 / (each * sources)) + EPSILON)
    spread = jnp.where(iota((128, CHANNELS), 0) == iota((128, CHANNELS), 1) // MEMBERS, 1.0, 0.0)
    mean = dot(jnp.broadcast_to(mean, (8, 128)), spread, HIGHEST)[:1]
    scale = dot(jnp.broadcast_to(scale, (8, 128)), spread, HIGHEST)[:1] * gain_ref[...]
    for j in range(WIDE):
        x = r[:, :, j * CHANNELS : (j + 1) * CHANNELS].reshape(2 * sources, CHANNELS)
        v = (x - mean) * scale + shift_ref[...]
        o_ref[j] = (v / (1.0 + jnp.exp(-v))).astype(BF16)


def slice_kernel(x_ref, y_ref, o_ref):
    quarter = lax.axis_index("gq")
    lanes = pl.ds(pl.multiple_of(quarter * SLICE, SLICE), SLICE)
    share = x_ref.shape[1]
    o_ref[:, :share] = x_ref[:, :, lanes]
    o_ref[:, share:] = y_ref[:, :, lanes]


def conv_kernel(xa_ref, xl_ref, xr_ref, ya_ref, yr_ref, b_ref, *rest):
    parts = (rest[:2], rest[2:4])
    o_ref, w_ref, x_ref, p0, p1, p2, y_ref, sem = rest[4:]
    core, kind, quarter = (lax.axis_index(n) for n in ("c", "zl", "gq"))
    rows = w_ref.shape[1] // CLASSES
    away = (0, CLASSES - 1, 1, 2)

    def copies(pieces):
        made = []
        for n in range(CLASSES):
            for j in range(rows):
                part = pieces[0].at[n * rows + j] if n < CLASSES - 1 else pieces[1].at[j]
                chip = CLASSES * j + lax.rem(kind + away[n], CLASSES)
                made.append(pltpu.make_async_copy(part, w_ref.at[:, chip], sem))
        return made

    for owner in range(2):

        @pl.when(core == owner)
        def _():
            for copy in copies(parts[owner]):
                copy.start()

    half = QUAD * CELLS
    west = core == 0
    place = lax.axis_index(CHIPS)
    final = lax.axis_size(CHIPS) - 1
    for v in range(QUAD):
        inner = [jnp.where(west, xa_ref[j, v], ya_ref[COLS + j, v]) for j in range(COLS)]
        outer = jnp.where(west, jnp.where(place == 0, xa_ref[0, v], xl_ref[v]), ya_ref[1, v])
        other = jnp.where(
            west, xa_ref[COLS, v], jnp.where(place == final, ya_ref[WIDE - 1, v], yr_ref[v])
        )
        blocks = (
            (v * CELLS, outer),
            (half + v * 2 * CELLS, inner[0]),
            (half + (v * 2 + 1) * CELLS, inner[1]),
            (3 * half + v * CELLS, other),
        )
        for start, block in blocks:
            for a in range(3):
                for f in range(FRAMES):
                    g = max(f + a - 2, 0)
                    x_ref[a, start + f * ROWS : start + (f + 1) * ROWS] = block[g * ROWS : (g + 1) * ROWS]
    for copy in copies(parts[0]):
        copy.wait()

    taps = w_ref.reshape(TAPS, CHANNELS, SLICE)
    for e, (p_ref, lo, hi) in enumerate(((p0, 0, 3 * half), (p1, half, 3 * half), (p2, half, 4 * half))):
        for rows in ((0, 1), (2,)):
            total = 0.0
            for a in range(3):
                w = jnp.concatenate([taps[a * 9 + b * 3 + e] for b in rows], axis=1)
                total += dot(x_ref[a, lo:hi], w)
            for n, b in enumerate(rows):
                p_ref[b] = total[:, n * SLICE : (n + 1) * SLICE]

    bias = b_ref[pl.ds(quarter, 1)]
    row = iota((CELLS, SLICE), 0) % ROWS

    def combine(v, _):
        def own(p_ref, lead, b, j):
            return p_ref[b, pl.ds(pl.multiple_of(lead + v * 2 * CELLS + j * CELLS, CELLS), CELLS)]

        def edge(p_ref, lead, b):
            return p_ref[b, pl.ds(pl.multiple_of(lead + v * CELLS, CELLS), CELLS)]

        for j in range(COLS):
            for side in range(2):
                t = []
                for b in range(3):
                    if side == 0:
                        first = edge(p0, 0, b) if j == 0 else own(p0, half, b, 0)
                        t.append(first + own(p1, 0, b, j) + own(p2, 0, b, j))
                    else:
                        final = edge(p2, 2 * half, b) if j == 1 else own(p2, 0, b, 1)
                        t.append(own(p0, half, b, j) + own(p1, 0, b, j) + final)
                above = jnp.where(row == 0, t[0], pltpu.roll(t[0], 1, 0))
                below = jnp.where(row == ROWS - 1, t[2], pltpu.roll(t[2], CELLS - 1, 0))
                for up, value in enumerate((above + t[1] + t[2], t[0] + t[1] + below)):
                    at = up * 2 * COLS + 2 * j + side
                    y_ref[pl.ds(at, CELLS, stride=4 * COLS), :] = value + bias
        o_ref[quarter ^ v] = y_ref[...].reshape(2 * CELLS, 2 * COLS, SLICE).astype(BF16)
        return 0

    lax.fori_loop(0, QUAD, combine, 0)


def spread_kernel(i_ref, o_ref, sem):
    copies = [
        pltpu.make_async_copy(i_ref.at[q], o_ref.at[:, :, pl.ds(q * SLICE, SLICE)], sem)
        for q in range(QUAD)
    ]
    for copy in copies:
        copy.start()
    for copy in copies:
        copy.wait()


def room(mebibytes):
    return pltpu.CompilerParams(vmem_limit_bytes=mebibytes * 2**20)


def vmem(n):
    return [pl.BlockSpec(memory_space=pltpu.VMEM)] * n


def shards(hidden, norm_gain, norm_shift, conv_weight, conv_bias):
    chips = lax.axis_size(CHIPS)
    share = 2 * conv_weight.shape[3]
    weight = conv_weight.reshape(TAPS, share // 2, CHANNELS)
    rows = lax.axis_size("zh")
    width = WIDE * CHANNELS + 128
    token = lax.ppermute(hidden, "c", [(1, 0)])
    other = lax.ppermute(weight, "c", [(0, 1)])

    column = (QUAD, CELLS, CHANNELS)
    act_shape = (WIDE,) + column
    kin_shapes = tuple((n * rows, TAPS, share, SLICE) for n in (CLASSES - 1, 1))

    def blank(*shapes):
        return pl.pallas_call(
            lambda *refs: None,
            out_shape=tuple(jax.ShapeDtypeStruct(shape, BF16) for shape in shapes),
            out_specs=tuple(pl.BlockSpec(memory_space=pl.ANY) for _ in shapes),
            compiler_params=room(1),
            name="blank",
        )()

    def ring(step):
        return [(i, (i + step) % chips) for i in range(chips)]

    def activations(hidden, token, weight, other):
        packed = pl.pallas_call(
            pack_kernel,
            out_shape=jax.ShapeDtypeStruct((chips, 2, width), BF16),
            in_specs=vmem(2),
            out_specs=vmem(1)[0],
            compiler_params=room(6),
            name="pack",
        )(hidden, token)
        tiles = lax.all_to_all(packed, CHIPS, split_axis=0, concat_axis=0, tiled=True)
        active = pl.pallas_call(
            norm_kernel,
            out_shape=jax.ShapeDtypeStruct((WIDE, CELLS, CHANNELS), BF16),
            in_specs=vmem(3),
            out_specs=vmem(1)[0],
            compiler_params=room(6),
            name="norm",
        )(tiles, norm_gain[None], norm_shift[None])
        videos = [active]
        for n in range(1, QUAD):
            videos.append(lax.ppermute(active, "gq", [(i, i ^ n) for i in range(QUAD)]))
        return (jnp.stack(videos, axis=1),) + blank(*kin_shapes)

    def kernels(hidden, token, weight, other):
        mine = pl.pallas_call(
            slice_kernel,
            out_shape=jax.ShapeDtypeStruct((TAPS, share, SLICE), BF16),
            in_specs=vmem(2),
            out_specs=vmem(1)[0],
            compiler_params=room(4),
            name="slice",
        )(other, weight)
        kin = lax.all_gather(mine, "zh", axis=0)
        below = lax.ppermute(kin, CHIPS, ring(1))
        above = lax.ppermute(kin, CHIPS, ring(-1))
        low = lax.ppermute(below[: rows // 2], CHIPS, ring(1))
        high = lax.ppermute(above[rows // 2 :], CHIPS, ring(-1))
        near = jnp.concatenate([kin, below, above], axis=0)
        return blank(act_shape) + (near, jnp.concatenate([low, high], axis=0))

    core = lax.axis_index("c")
    active, near, far = lax.cond(core == 0, activations, kernels, hidden, token, weight, other)
    right = [(2 * i, 2 * i + 2) for i in range(chips - 1)]
    left = [(j, i) for i, j in right]
    before = lax.ppermute(active[WIDE - 1], SPACE, right)
    after = lax.ppermute(active[0], SPACE, left)
    given = lax.ppermute(active, "c", [(0, 1)])
    weights = (near, far)
    weights = tuple(lax.ppermute(w, "c", [(1, 0)]) for w in weights) + weights
    acts = (active, before, after, given, lax.ppermute(after, "c", [(0, 1)]))

    half = QUAD * CELLS
    out = pl.pallas_call(
        conv_kernel,
        out_shape=jax.ShapeDtypeStruct((QUAD, 2 * CELLS, 2 * COLS, SLICE), BF16),
        in_specs=vmem(6) + [pl.BlockSpec(memory_space=pltpu.HBM)] * 4,
        out_specs=vmem(1)[0],
        scratch_shapes=[
            pltpu.VMEM((TAPS, chips, share, SLICE), BF16),
            pltpu.VMEM((3, 4 * half, CHANNELS), BF16),
            pltpu.VMEM((3, 3 * half, SLICE), F32),
            pltpu.VMEM((3, 2 * half, SLICE), F32),
            pltpu.VMEM((3, 3 * half, SLICE), F32),
            pltpu.VMEM((4 * COLS * CELLS, SLICE), F32),
            pltpu.SemaphoreType.DMA,
        ],
        compiler_params=room(24),
        name="conv",
    )(*acts, conv_bias.astype(F32).reshape(QUAD, SLICE), *weights)
    out = lax.all_to_all(out, "gq", split_axis=0, concat_axis=0, tiled=True)
    out = pl.pallas_call(
        spread_kernel,
        out_shape=jax.ShapeDtypeStruct((2 * CELLS, 2 * COLS, CHANNELS), BF16),
        in_specs=vmem(1),
        out_specs=pl.BlockSpec(memory_space=pltpu.HBM),
        scratch_shapes=[pltpu.SemaphoreType.DMA],
        compiler_params=room(4),
        name="spread",
    )(out)
    return out.reshape(FRAMES, 2 * ROWS, 2 * COLS, CHANNELS)


def solution(mesh):
    groups, space = mesh.shape["groups"], mesh.shape["space"]
    torus = Mesh(
        mesh.devices.reshape(groups // QUAD, QUAD, space // (2 * CLASSES), CLASSES, 2),
        ("gh", "gq", "zh", "zl", "c"),
    )
    return jax.shard_map(
        shards,
        mesh=torus,
        in_specs=(
            P(("gh", "gq") + SPACE, None),
            P(),
            P(),
            P(None, None, None, SPACE, None),
            P(),
        ),
        out_specs=P(("gh", "gq"), None, SPACE, None),
        check_vma=False,
    )
```

time: 139 us -> 129 us (0.928)
  waiting for transfers between devices: 3.28 us -> 27.1 us
  starting transfers between devices: 55.8 us -> 35.6 us
  blocking collectives: 68.3 us -> 58.1 us
  local copies, waits for them, and re-layouts: 2.71 us -> 0.24 us
    all_to_all x1 -> x0, starting transfers between devices: 34.3 us -> none  [shards(): lax.all_to_all(packed, SPACE, split_axis=0, concat_axis=0, tiled=True)]
    ppermute x7 -> x12, waiting for transfers between devices: 3.28 us -> 27.1 us  [the longest x1 10.7 us: kernels(): above = lax.ppermute(kin, CHIPS, ring(-1))]
    ppermute x7 -> x12, starting transfers between devices: 21.4 us -> 35.6 us  [the longest x1 22.4 us: shards(): token = lax.ppermute(hidden, 'c', [(1, 0)])]
    all_gather x2 -> x1, blocking collectives: 59.4 us -> 46.6 us  [kernels(): kin = lax.all_gather(mine, 'zh', axis=0)]
    all_to_all x1, blocking collectives: 8.93 us -> 11.5 us  [shards(): out = lax.all_to_all(out, 'gq', split_axis=0, concat_axis=0, tiled=True)]
    unnamed x10 -> x2, local copies, waits for them, and re-layouts: 1.85 us -> 0.01 us
  transfers between devices with their start and end apart: 8 -> 12, of which waited for: 2 -> 5; matrix products, arithmetic and copies ran while one was open for 1% -> 0% of each run, Pallas kernels for 0% -> 0%
where the time goes in v3:
time: 129 us; the launch traced here: 128 us
  blocking collectives  58.1 us (45%)
  starting transfers between devices  35.6 us (28%)
  waiting for transfers between devices  27.1 us (21%)
  Pallas kernels  6.71 us (5%)
    all_gather x1, blocking collectives, kernels(): kin = lax.all_gather(mine, 'zh', axis=0)  46.6 us
    ppermute x1, starting transfers between devices, shards(): token = lax.ppermute(hidden, 'c', [(1, 0)])  22.4 us
    all_to_all x1, blocking collectives, shards(): out = lax.all_to_all(out, 'gq', split_axis=0, concat_axis=0, tiled=True)  11.5 us
    ppermute x1, waiting for transfers between devices, kernels(): above = lax.ppermute(kin, CHIPS, ring(-1))  10.7 us
    ppermute x1, waiting for transfers between devices, shards(): acts = (active, before, after, given, lax.ppermute(after, 'c', [(0, 1)]))  7.19 us
    ppermute x1, waiting for transfers between devices, kernels(): high = lax.ppermute(above[rows // 2:], CHIPS, ring(-1))  5.05 us
    pallas_call x1, Pallas kernels, shards(): pl.pallas_call(conv_kernel, out_shape=jax.ShapeDtypeStruct((QUAD, 2 * CEL...  4.96 us
    ppermute x2, starting transfers between devices, shards(): weights = tuple((lax.ppermute(w, 'c', [(1, 0)]) for w in weights)) + weights  4.67 us
  transfers between devices with their start and end apart: 12, of which 5 were waited for; matrix products, arithmetic and copies ran while one was open for 0% of the time, Pallas kernels for 0%

profile of v3, /device:TPU:37, one launch (start us, length us, event | category | flops | bytes accessed | tf_op | source)
XLA Modules:
  0.0 128.4 jit_solution(9827286279053594153)
XLA Ops:
  0.0 1.3 %collective-permute-start.7 = (bf16[27,8,512]{2,1,0:T(8,128)(2,1)}, bf16[27,8,512]{2,1,0:T(8,128)(2,1)S(1)}, u32[]{:S(2)}, u32[]{:S(2)}) collective-permute-start(bf16[27,8,512]{2,1,0:T(8,128)(2,1)} %bitcast.23), channel_id=1, source_target_pairs={{0,1},{2,3},{4,5},{6,7},{8,9},{10,11},{12,13},{14,15},{16,17},{18,... | collective-permute-start | bytes 663560 | tf_op jit(solution)/shard_map/ppermute | solution.py:223
  1.3 22.4 %collective-permute-start.8 = (bf16[128,512]{1,0:T(8,128)(2,1)}, bf16[128,512]{1,0:T(8,128)(2,1)S(1)}, u32[]{:S(2)}, u32[]{:S(2)}) collective-permute-start(bf16[128,512]{1,0:T(8,128)(2,1)} %param.7), channel_id=1, source_target_pairs={{1,0},{3,2},{5,4},{7,6},{9,8},{11,10},{13,12},{15,14},{17,16},{19,... | collective-permute-start | bytes 393224 | tf_op jit(solution)/shard_map/ppermute | solution.py:222
  23.7 1.2 collective-permute-done.8
  24.9 70.0 %conditional.1 = (bf16[4,4,64,512]{3,2,0,1:T(8,128)(2,1)S(1)}, bf16[24,27,16,128]{3,2,1,0:T(8,128)(2,1)S(1)}, bf16[8,27,16,128]{3,2,1,0:T(8,128)(2,1)S(1)}) conditional(s32[]{:T(128)} %convert_element_type.4, (bf16[27,8,512]{2,1,0:T(8,128)(2,1)S(1)}, bf16[27,8,512]{2,1,0:T(8,128)(2,1)}) %tuple.20, (bf16[128,512]{1,0:T(8,128)(2,1)}, ...), branch_computations={%region_0.0_spmd, %region_1.0_spmd} | conditional | flops 3096576 | bytes 22556856 | solution.py:282
  24.9 1.0 slice.21
  25.8 46.6 %all-gather = bf16[216,16,128]{2,1,0:T(8,128)(2,1)S(1)} all-gather(bf16[27,16,128]{2,1,0:T(8,128)(2,1)S(1)} %slice.21), channel_id=2, replica_groups=mesh['gh'=1,'gq'=4,'zh'=8,'zl'=4,'c'=2] {'zh'}, dimensions={0}, use_global_device_ids=true | all-gather | bytes 995328 | tf_op jit(solution)/shard_map/cond/branch_0_fun/all_gather | solution.py:273
  72.4 0.6 collective-permute-start.1
  73.0 0.8 collective-permute-start
  73.8 10.7 %collective-permute-done.1 = bf16[8,27,16,128]{3,2,1,0:T(8,128)(2,1)S(1)} collective-permute-done((bf16[8,27,16,128]{3,2,1,0:T(8,128)(2,1)S(1)}, bf16[8,27,16,128]{3,2,1,0:T(8,128)(2,1)S(1)}, u32[]{:S(2)}, u32[]{:S(2)}) %collective-permute-start.1) | collective-permute-done | bytes 884768 | tf_op jit(solution)/shard_map/cond/branch_0_fun/ppermute | solution.py:275
  84.6 1.7 %collective-permute-start.3 = (bf16[4,27,16,128]{3,2,1,0:T(8,128)(2,1)S(1)}, bf16[4,27,16,128]{3,2,1,0:T(8,128)(2,1)S(1)}, u32[]{:S(2)}, u32[]{:S(2)}) collective-permute-start(bf16[4,27,16,128]{3,2,1,0:T(8,128)(2,1)S(1)} %slice.16), channel_id=1, source_target_pairs={{0,62},{2,0},{4,2},{6,4},{8,6},{10,8},{12,10},{14,12},{16,14},{18,... | collective-permute-start | bytes 1327112 | tf_op jit(solution)/shard_map/cond/branch_0_fun/ppermute | solution.py:277
  86.3 0.1 collective-permute-start.2
  86.5 0.3 pad_maximum_fusion
  86.8 5.1 %collective-permute-done.3 = bf16[4,27,16,128]{3,2,1,0:T(8,128)(2,1)S(1)} collective-permute-done((bf16[4,27,16,128]{3,2,1,0:T(8,128)(2,1)S(1)}, bf16[4,27,16,128]{3,2,1,0:T(8,128)(2,1)S(1)}, u32[]{:S(2)}, u32[]{:S(2)}) %collective-permute-start.3) | collective-permute-done | bytes 442400 | tf_op jit(solution)/shard_map/cond/branch_0_fun/ppermute | solution.py:277
  91.9 2.9 %collective-permute-done.2 = bf16[4,27,16,128]{3,2,1,0:T(8,128)(2,1)S(1)} collective-permute-done((bf16[4,27,16,128]{3,2,1,0:T(8,128)(2,1)S(1)}, bf16[4,27,16,128]{3,2,1,0:T(8,128)(2,1)S(1)}, u32[]{:S(2)}, u32[]{:S(2)}) %collective-permute-start.2) | collective-permute-done | bytes 442400 | tf_op jit(solution)/shard_map/cond/branch_0_fun/ppermute | solution.py:276
  94.9 1.5 %collective-permute-start.13 = (bf16[24,27,16,128]{3,2,1,0:T(8,128)(2,1)S(1)}, bf16[24,27,16,128]{3,2,1,0:T(8,128)(2,1)S(1)}, u32[]{:S(2)}, u32[]{:S(2)}) collective-permute-start(bf16[24,27,16,128]{3,2,1,0:T(8,128)(2,1)S(1)} %get-tuple-element.29.rest_2_), channel_id=1, source_target_pairs={{1,0},{3,2},{5,4},{7,6},{9,8},{11,10},{13,12},{15,14},{17,16},{19,... | collective-permute-start | bytes 7962632 | tf_op jit(solution)/shard_map/ppermute | solution.py:289
  96.4 1.3 %collective-permute-start.11 = (bf16[4,4,64,512]{3,2,1,0:T(8,128)(2,1)S(1)}, bf16[4,4,64,512]{3,2,1,0:T(8,128)(2,1)S(1)}, u32[]{:S(2)}, u32[]{:S(2)}) collective-permute-start(bf16[4,4,64,512]{3,2,1,0:T(8,128)(2,1)S(1)} %copy.17.xa_ref), channel_id=1, source_target_pairs={{0,1},{2,3},{4,5},{6,7},{8,9},{10,11},{12,13},{14,15},{16,17},{18,... | collective-permute-start | bytes 3145736 | tf_op jit(solution)/shard_map/ppermute | solution.py:287
  97.7 3.2 %collective-permute-start.14 = (bf16[8,27,16,128]{3,2,1,0:T(8,128)(2,1)S(1)}, bf16[8,27,16,128]{3,2,1,0:T(8,128)(2,1)S(1)}, u32[]{:S(2)}, u32[]{:S(2)}) collective-permute-start(bf16[8,27,16,128]{3,2,1,0:T(8,128)(2,1)S(1)} %get-tuple-element.30.rest_3_), channel_id=1, source_target_pairs={{1,0},{3,2},{5,4},{7,6},{9,8},{11,10},{13,12},{15,14},{17,16},{19,... | collective-permute-start | bytes 2654216 | tf_op jit(solution)/shard_map/ppermute | solution.py:289
  101.0 0.7 collective-permute-start.10
  101.7 0.7 collective-permute-start.9
  102.4 1.3 %collective-permute-start.12 = (bf16[4,64,512]{2,1,0:T(8,128)(2,1)S(1)}, bf16[4,64,512]{2,1,0:T(8,128)(2,1)S(1)}, u32[]{:S(2)}, u32[]{:S(2)}) collective-permute-start(bf16[4,64,512]{2,1,0:T(8,128)(2,1)S(1)} %collective-permute-done.10.xr_ref), channel_id=1, source_target_pairs={{0,1},{2,3},{4,5},{6,7},{8,9},{10,11},{12,13},{14,15},{16,17},{18,... | collective-permute-start | bytes 786440 | tf_op jit(solution)/shard_map/ppermute | solution.py:290
  103.7 7.2 %collective-permute-done.12.yr_ref = bf16[4,64,512]{2,1,0:T(8,128)(2,1)S(1)} collective-permute-done((bf16[4,64,512]{2,1,0:T(8,128)(2,1)S(1)}, bf16[4,64,512]{2,1,0:T(8,128)(2,1)S(1)}, u32[]{:S(2)}, u32[]{:S(2)}) %collective-permute-start.12) | collective-permute-done | bytes 262176 | tf_op jit(solution)/shard_map/ppermute | solution.py:290
  110.9 5.0 %conv.1 = bf16[4,128,4,128]{3,2,1,0:T(4,128)(2,1)S(1)} custom-call(bf16[4,4,64,512]{3,2,1,0:T(8,128)(2,1)S(1)} %copy.17.xa_ref, bf16[4,64,512]{2,1,0:T(8,128)(2,1)S(1)} %collective-permute-done.9.xl_ref, bf16[4,64,512]{2,1,0:T(8,128)(2,1)S(1)} %collective-permute-done.10.xr_ref, bf16[4,4,64,512]{3,2,1,0:T(8,128)(2,1)S(1)} %collective-permute-done.11.ya_ref, ...), custom_call_target="tpu_custom_call" | custom-call | tf_op jit(solution)/shard_map/conv/pallas_call | solution.py:293
  115.9 11.5 %all_to_all.10.i_ref = bf16[4,128,4,128]{3,2,1,0:T(4,128)(2,1)S(1)} all-to-all(bf16[4,128,4,128]{3,2,1,0:T(4,128)(2,1)S(1)} %conv.1), channel_id=1, replica_groups=mesh['gh'=1,'gq'=4,'zh'=8,'zl'=4,'c'=2] {'gq'}, dimensions={0} | all-to-all | bytes 1048576 | tf_op jit(solution)/shard_map/all_to_all | solution.py:310
  127.4 0.8 spread.1
  (17 shorter events, 0.3 us)
Async XLA Ops:
  0.0 24.9 %collective-permute-start.7 = (bf16[27,8,512]{2,1,0:T(8,128)(2,1)}, bf16[27,8,512]{2,1,0:T(8,128)(2,1)S(1)}, u32[]{:S(2)}, u32[]{:S(2)}) collective-permute-start(bf16[27,8,512]{2,1,0:T(8,128)(2,1)} %bitcast.23), channel_id=1, source_target_pairs={{0,1},{2,3},{4,5},{6,7},{8,9},{10,11},{12,13},{14,15},{16,17},{18,... | collective-permute-start | bytes 663560 | tf_op jit(solution)/shard_map/ppermute | solution.py:223
  1.3 23.5 %collective-permute-start.8 = (bf16[128,512]{1,0:T(8,128)(2,1)}, bf16[128,512]{1,0:T(8,128)(2,1)S(1)}, u32[]{:S(2)}, u32[]{:S(2)}) collective-permute-start(bf16[128,512]{1,0:T(8,128)(2,1)} %param.7), channel_id=1, source_target_pairs={{1,0},{3,2},{5,4},{7,6},{9,8},{11,10},{13,12},{15,14},{17,16},{19,... | collective-permute-start | bytes 393224 | tf_op jit(solution)/shard_map/ppermute | solution.py:222
  72.4 12.2 %collective-permute-start.1 = (bf16[8,27,16,128]{3,2,1,0:T(8,128)(2,1)S(1)}, bf16[8,27,16,128]{3,2,1,0:T(8,128)(2,1)S(1)}, u32[]{:S(2)}, u32[]{:S(2)}) collective-permute-start(bf16[8,27,16,128]{3,2,1,0:T(8,128)(2,1)S(1)} %bitcast.17), channel_id=1, source_target_pairs={{0,62},{2,0},{4,2},{6,4},{8,6},{10,8},{12,10},{14,12},{16,14},{18,... | collective-permute-start | bytes 2654216 | tf_op jit(solution)/shard_map/cond/branch_0_fun/ppermute | solution.py:275
  73.0 13.3 %collective-permute-start = (bf16[8,27,16,128]{3,2,1,0:T(8,128)(2,1)S(1)}, bf16[8,27,16,128]{3,2,1,0:T(8,128)(2,1)S(1)}, u32[]{:S(2)}, u32[]{:S(2)}) collective-permute-start(bf16[8,27,16,128]{3,2,1,0:T(8,128)(2,1)S(1)} %bitcast.18), channel_id=1, source_target_pairs={{0,2},{2,4},{4,6},{6,8},{8,10},{10,12},{12,14},{14,16},{16,18},{18... | collective-permute-start | bytes 2654216 | tf_op jit(solution)/shard_map/cond/branch_0_fun/ppermute | solution.py:274
  84.6 7.3 %collective-permute-start.3 = (bf16[4,27,16,128]{3,2,1,0:T(8,128)(2,1)S(1)}, bf16[4,27,16,128]{3,2,1,0:T(8,128)(2,1)S(1)}, u32[]{:S(2)}, u32[]{:S(2)}) collective-permute-start(bf16[4,27,16,128]{3,2,1,0:T(8,128)(2,1)S(1)} %slice.16), channel_id=1, source_target_pairs={{0,62},{2,0},{4,2},{6,4},{8,6},{10,8},{12,10},{14,12},{16,14},{18,... | collective-permute-start | bytes 1327112 | tf_op jit(solution)/shard_map/cond/branch_0_fun/ppermute | solution.py:277
  86.3 8.5 %collective-permute-start.2 = (bf16[4,27,16,128]{3,2,1,0:T(8,128)(2,1)S(1)}, bf16[4,27,16,128]{3,2,1,0:T(8,128)(2,1)S(1)}, u32[]{:S(2)}, u32[]{:S(2)}) collective-permute-start(bf16[4,27,16,128]{3,2,1,0:T(8,128)(2,1)S(1)} %slice.15), channel_id=1, source_target_pairs={{0,2},{2,4},{4,6},{6,8},{8,10},{10,12},{12,14},{14,16},{16,18},{18... | collective-permute-start | bytes 1327112 | tf_op jit(solution)/shard_map/cond/branch_0_fun/ppermute | solution.py:276
  94.9 8.8 %copy-start = (bf16[512]{0:T(512)(128)(2,1)S(1)}, bf16[512]{0:T(512)(128)(2,1)}, u32[]{:S(2)}) copy-start(bf16[512]{0:T(512)(128)(2,1)} %param.11) | copy-start | bytes 3076
  94.9 16.1 %collective-permute-start.13 = (bf16[24,27,16,128]{3,2,1,0:T(8,128)(2,1)S(1)}, bf16[24,27,16,128]{3,2,1,0:T(8,128)(2,1)S(1)}, u32[]{:S(2)}, u32[]{:S(2)}) collective-permute-start(bf16[24,27,16,128]{3,2,1,0:T(8,128)(2,1)S(1)} %get-tuple-element.29.rest_2_), channel_id=1, source_target_pairs={{1,0},{3,2},{5,4},{7,6},{9,8},{11,10},{13,12},{15,14},{17,16},{19,... | collective-permute-start | bytes 7962632 | tf_op jit(solution)/shard_map/ppermute | solution.py:289
  96.4 14.5 %collective-permute-start.11 = (bf16[4,4,64,512]{3,2,1,0:T(8,128)(2,1)S(1)}, bf16[4,4,64,512]{3,2,1,0:T(8,128)(2,1)S(1)}, u32[]{:S(2)}, u32[]{:S(2)}) collective-permute-start(bf16[4,4,64,512]{3,2,1,0:T(8,128)(2,1)S(1)} %copy.17.xa_ref), channel_id=1, source_target_pairs={{0,1},{2,3},{4,5},{6,7},{8,9},{10,11},{12,13},{14,15},{16,17},{18,... | collective-permute-start | bytes 3145736 | tf_op jit(solution)/shard_map/ppermute | solution.py:287
  97.7 13.2 %collective-permute-start.14 = (bf16[8,27,16,128]{3,2,1,0:T(8,128)(2,1)S(1)}, bf16[8,27,16,128]{3,2,1,0:T(8,128)(2,1)S(1)}, u32[]{:S(2)}, u32[]{:S(2)}) collective-permute-start(bf16[8,27,16,128]{3,2,1,0:T(8,128)(2,1)S(1)} %get-tuple-element.30.rest_3_), channel_id=1, source_target_pairs={{1,0},{3,2},{5,4},{7,6},{9,8},{11,10},{13,12},{15,14},{17,16},{19,... | collective-permute-start | bytes 2654216 | tf_op jit(solution)/shard_map/ppermute | solution.py:289
  101.0 1.4 %collective-permute-start.10 = (bf16[4,64,512]{2,1,0:T(8,128)(2,1)S(1)}, bf16[4,64,512]{2,1,0:T(8,128)(2,1)S(1)}, u32[]{:S(2)}, u32[]{:S(2)}) collective-permute-start(bf16[4,64,512]{2,1,0:T(8,128)(2,1)S(1)} %get-tuple-element.41), channel_id=1, source_target_pairs={{2,0},{4,2},{6,4},{8,6},{10,8},{12,10},{14,12},{16,14},{18,16},{20... | collective-permute-start | bytes 786440 | tf_op jit(solution)/shard_map/ppermute | solution.py:286
  101.7 2.0 %collective-permute-start.9 = (bf16[4,64,512]{2,1,0:T(8,128)(2,1)S(1)}, bf16[4,64,512]{2,1,0:T(8,128)(2,1)S(1)}, u32[]{:S(2)}, u32[]{:S(2)}) collective-permute-start(bf16[4,64,512]{2,1,0:T(8,128)(2,1)S(1)} %get-tuple-element.42), channel_id=1, source_target_pairs={{0,2},{2,4},{4,6},{6,8},{8,10},{10,12},{12,14},{14,16},{16,18},{18... | collective-permute-start | bytes 786440 | tf_op jit(solution)/shard_map/ppermute | solution.py:285
  102.4 8.5 %collective-permute-start.12 = (bf16[4,64,512]{2,1,0:T(8,128)(2,1)S(1)}, bf16[4,64,512]{2,1,0:T(8,128)(2,1)S(1)}, u32[]{:S(2)}, u32[]{:S(2)}) collective-permute-start(bf16[4,64,512]{2,1,0:T(8,128)(2,1)S(1)} %collective-permute-done.10.xr_ref), channel_id=1, source_target_pairs={{0,1},{2,3},{4,5},{6,7},{8,9},{10,11},{12,13},{14,15},{16,17},{18,... | collective-permute-start | bytes 786440 | tf_op jit(solution)/shard_map/ppermute | solution.py:290

commit v4 on v3

--- a/solution.py
+++ b/solution.py
@@ -46,9 +46,51 @@
     ).astype(BF16)
 
 
+def parcel_kernel(x_ref, w_ref, p_ref, s_ref, r_ref, sem):
+    core, quarter = lax.axis_index("c"), lax.axis_index("gq")
+    lanes = pl.ds(pl.multiple_of(quarter * SLICE, SLICE), SLICE)
+    tiles = x_ref.shape[0]
+
+    def token_copies():
+        return [
+            pltpu.make_async_copy(
+                x_ref.at[:, :, pl.ds(n * SLICE, SLICE)], p_ref.at[pl.ds(n * tiles, tiles)], sem.at[2 + n]
+            )
+            for n in range(CHANNELS // SLICE)
+        ]
+
+    def slice_copy():
+        return pltpu.make_async_copy(w_ref.at[:, :, lanes], p_ref.at[pl.ds(0, TAPS)], sem.at[2])
+
+    own = pltpu.make_async_copy(w_ref.at[:, :, lanes], s_ref, sem.at[0])
+    row = pltpu.make_async_copy(x_ref, r_ref, sem.at[1])
+
+    @pl.when(core == 0)
+    def _():
+        slice_copy().start()
+        row.start()
+        slice_copy().wait()
+        row.wait()
+
+    @pl.when(core == 1)
+    def _():
+        for copy in token_copies():
+            copy.start()
+        own.start()
+        for copy in token_copies():
+            copy.wait()
+        own.wait()
+
+
 def pack_kernel(x_ref, y_ref, o_ref):
-    rows = [ref[...].astype(F32) for ref in (x_ref, y_ref)]
-    cells = x_ref.shape[0]
+    cells = x_ref.shape[0] * x_ref.shape[1]
+    tiles = x_ref.shape[0]
+    own = x_ref[...].astype(F32).reshape(cells, CHANNELS)
+    given = [
+        y_ref[n * tiles : (n + 1) * tiles].astype(F32).reshape(cells, SLICE)
+        for n in range(CHANNELS // SLICE)
+    ]
+    rows = [own, jnp.concatenate(given, axis=1)]
     gather = jnp.where(
         (iota((CHANNELS, 128), 0) // MEMBERS == iota((CHANNELS, 128), 1) % GROUPS)
         & (iota((CHANNELS, 128), 1) < 3 * GROUPS),
@@ -98,15 +140,7 @@
         o_ref[j] = (v / (1.0 + jnp.exp(-v))).astype(BF16)
 
 
-def slice_kernel(x_ref, y_ref, o_ref):
-    quarter = lax.axis_index("gq")
-    lanes = pl.ds(pl.multiple_of(quarter * SLICE, SLICE), SLICE)
-    share = x_ref.shape[1]
-    o_ref[:, :share] = x_ref[:, :, lanes]
-    o_ref[:, share:] = y_ref[:, :, lanes]
-
-
-def conv_kernel(xa_ref, xl_ref, xr_ref, ya_ref, yr_ref, b_ref, *rest):
+def conv_kernel(x0_ref, l0_ref, x1_ref, r1_ref, b_ref, *rest):
     parts = (rest[:2], rest[2:4])
     o_ref, w_ref, x_ref, p0, p1, p2, y_ref, sem = rest[4:]
     core, kind, quarter = (lax.axis_index(n) for n in ("c", "zl", "gq"))
@@ -130,19 +164,18 @@
                 copy.start()
 
     half = QUAD * CELLS
-    west = core == 0
     place = lax.axis_index(CHIPS)
     final = lax.axis_size(CHIPS) - 1
     for v in range(QUAD):
-        inner = [jnp.where(west, xa_ref[j, v], ya_ref[COLS + j, v]) for j in range(COLS)]
-        outer = jnp.where(west, jnp.where(place == 0, xa_ref[0, v], xl_ref[v]), ya_ref[1, v])
-        other = jnp.where(
-            west, xa_ref[COLS, v], jnp.where(place == final, ya_ref[WIDE - 1, v], yr_ref[v])
+        sides = (
+            [jnp.where(place == 0, x0_ref[v, 0], l0_ref[v])] + [x0_ref[v, j] for j in range(WIDE - 1)],
+            [x1_ref[v, j] for j in range(WIDE - 1)] + [jnp.where(place == final, x1_ref[v, WIDE - 2], r1_ref[v])],
         )
+        outer, first, second, other = (jnp.where(core == 0, x, y) for x, y in zip(*sides))
         blocks = (
             (v * CELLS, outer),
-            (half + v * 2 * CELLS, inner[0]),
-            (half + (v * 2 + 1) * CELLS, inner[1]),
+            (half + v * 2 * CELLS, first),
+            (half + (v * 2 + 1) * CELLS, second),
             (3 * half + v * CELLS, other),
         )
         for start, block in blocks:
@@ -219,11 +252,23 @@
     weight = conv_weight.reshape(TAPS, share // 2, CHANNELS)
     rows = lax.axis_size("zh")
     width = WIDE * CHANNELS + 128
-    token = lax.ppermute(hidden, "c", [(1, 0)])
-    other = lax.ppermute(weight, "c", [(0, 1)])
-
-    column = (QUAD, CELLS, CHANNELS)
-    act_shape = (WIDE,) + column
+    tiles = hidden.shape[0] // 8
+    parcel, mine, row = pl.pallas_call(
+        parcel_kernel,
+        out_shape=(
+            jax.ShapeDtypeStruct((tiles * CHANNELS // SLICE, 8, SLICE), BF16),
+            jax.ShapeDtypeStruct((TAPS, share // 2, SLICE), BF16),
+            jax.ShapeDtypeStruct((tiles, 8, CHANNELS), BF16),
+        ),
+        in_specs=[pl.BlockSpec(memory_space=pltpu.HBM)] * 2,
+        out_specs=tuple(vmem(3)),
+        scratch_shapes=[pltpu.SemaphoreType.DMA((2 + CHANNELS // SLICE,))],
+        compiler_params=room(2),
+        name="parcel",
+    )(hidden.reshape(tiles, 8, CHANNELS), weight)
+    parcel = lax.ppermute(parcel, "c", [(0, 1), (1, 0)])
+
+    act_shape = (QUAD, WIDE, CELLS, CHANNELS)
     kin_shapes = tuple((n * rows, TAPS, share, SLICE) for n in (CLASSES - 1, 1))
 
     def blank(*shapes):
@@ -238,7 +283,7 @@
     def ring(step):
         return [(i, (i + step) % chips) for i in range(chips)]
 
-    def activations(hidden, token, weight, other):
+    def activations(parcel, mine, row):
         packed = pl.pallas_call(
             pack_kernel,
             out_shape=jax.ShapeDtypeStruct((chips, 2, width), BF16),
@@ -246,7 +291,7 @@
             out_specs=vmem(1)[0],
             compiler_params=room(6),
             name="pack",
-        )(hidden, token)
+        )(row, parcel)
         tiles = lax.all_to_all(packed, CHIPS, split_axis=0, concat_axis=0, tiled=True)
         active = pl.pallas_call(
             norm_kernel,
@@ -256,44 +301,40 @@
             compiler_params=room(6),
             name="norm",
         )(tiles, norm_gain[None], norm_shift[None])
-        videos = [active]
-        for n in range(1, QUAD):
-            videos.append(lax.ppermute(active, "gq", [(i, i ^ n) for i in range(QUAD)]))
-        return (jnp.stack(videos, axis=1),) + blank(*kin_shapes)
-
-    def kernels(hidden, token, weight, other):
-        mine = pl.pallas_call(
-            slice_kernel,
-            out_shape=jax.ShapeDtypeStruct((TAPS, share, SLICE), BF16),
-            in_specs=vmem(2),
-            out_specs=vmem(1)[0],
-            compiler_params=room(4),
-            name="slice",
-        )(other, weight)
+        hops = [[(i, i ^ n) for i in range(QUAD)] for n in range(1, QUAD)]
+        videos = [active] + [lax.ppermute(active, "gq", hop) for hop in hops]
+        return (jnp.stack(videos),) + blank(*kin_shapes)
+
+    def kernels(parcel, mine, row):
+        mine = jnp.concatenate([parcel[:TAPS], mine], axis=1)
         kin = lax.all_gather(mine, "zh", axis=0)
-        below = lax.ppermute(kin, CHIPS, ring(1))
-        above = lax.ppermute(kin, CHIPS, ring(-1))
-        low = lax.ppermute(below[: rows // 2], CHIPS, ring(1))
-        high = lax.ppermute(above[rows // 2 :], CHIPS, ring(-1))
-        near = jnp.concatenate([kin, below, above], axis=0)
+        front, back = kin[: rows // 2], kin[rows // 2 :]
+        below = [lax.ppermute(front, CHIPS, ring(1))]
+        above = [lax.ppermute(back, CHIPS, ring(-1))]
+        below += [lax.ppermute(back, CHIPS, ring(1))]
+        above = [lax.ppermute(front, CHIPS, ring(-1))] + above
+        low = lax.ppermute(below[0], CHIPS, ring(1))
+        high = lax.ppermute(above[1], CHIPS, ring(-1))
+        below, above = lax.optimization_barrier([jnp.concatenate(x) for x in (below, above)])
+        near = jnp.concatenate([kin, below, above])
         return blank(act_shape) + (near, jnp.concatenate([low, high], axis=0))
 
     core = lax.axis_index("c")
-    active, near, far = lax.cond(core == 0, activations, kernels, hidden, token, weight, other)
+    active, near, far = lax.cond(core == 0, activations, kernels, parcel, mine, row)
     right = [(2 * i, 2 * i + 2) for i in range(chips - 1)]
     left = [(j, i) for i, j in right]
-    before = lax.ppermute(active[WIDE - 1], SPACE, right)
-    after = lax.ppermute(active[0], SPACE, left)
-    given = lax.ppermute(active, "c", [(0, 1)])
+    before = lax.ppermute(active[:, WIDE - 1], SPACE, right)
+    after = lax.ppermute(active[:, 0], SPACE, left)
+    given = lax.ppermute(active[:, 1:], "c", [(0, 1)])
     weights = (near, far)
     weights = tuple(lax.ppermute(w, "c", [(1, 0)]) for w in weights) + weights
-    acts = (active, before, after, given, lax.ppermute(after, "c", [(0, 1)]))
+    acts = (active, before, given, lax.ppermute(after, "c", [(0, 1)]))
 
     half = QUAD * CELLS
     out = pl.pallas_call(
         conv_kernel,
         out_shape=jax.ShapeDtypeStruct((QUAD, 2 * CELLS, 2 * COLS, SLICE), BF16),
-        in_specs=vmem(6) + [pl.BlockSpec(memory_space=pltpu.HBM)] * 4,
+        in_specs=vmem(5) + [pl.BlockSpec(memory_space=pltpu.HBM)] * 4,
         out_specs=vmem(1)[0],
         scratch_shapes=[
             pltpu.VMEM((TAPS, chips, share, SLICE), BF16),

time: 129 us -> 123 us (0.953)
  waiting for transfers between devices: 27.1 us -> 22.8 us
  starting transfers between devices: 35.6 us -> 33.1 us
  local copies, waits for them, and re-layouts: 0.24 us -> 2.09 us
    ppermute x10 -> x11, waiting for transfers between devices: 27 us -> 22.8 us  [the longest x1 9.06 us: shards(): acts = (active, before, given, lax.ppermute(after, 'c', [(0, 1)]))]
    unnamed x2 -> x6, local copies, waits for them, and re-layouts: 0.01 us -> 1.84 us
    ppermute x2, starting transfers between devices: 4.67 us -> 3.02 us  [shards(): weights = tuple((lax.ppermute(w, 'c', [(1, 0)]) for w in weights)) + weights]
    ppermute x10 -> x11, starting transfers between devices: 30.9 us -> 30.1 us  [the longest x1 20.7 us: shards(): parcel = lax.ppermute(parcel, 'c', [(0, 1), (1, 0)])]
  transfers between devices with their start and end apart: 12 -> 13, of which waited for: 5 -> 7; matrix products, arithmetic and copies ran while one was open for 0% -> 0% of each run, Pallas kernels for 0% -> 0%
where the time goes in v4:
time: 123 us; the launch traced here: 122 us
  blocking collectives  57.8 us (47%)
  starting transfers between devices  33.1 us (27%)
  waiting for transfers between devices  22.8 us (19%)
  Pallas kernels  5.68 us (5%)
  local copies, waits for them, and re-layouts  2.09 us (2%)
    all_gather x1, blocking collectives, kernels(): kin = lax.all_gather(mine, 'zh', axis=0)  45.9 us
    ppermute x1, starting transfers between devices, shards(): parcel = lax.ppermute(parcel, 'c', [(0, 1), (1, 0)])  20.7 us
    all_to_all x1, blocking collectives, shards(): out = lax.all_to_all(out, 'gq', split_axis=0, concat_axis=0, tiled=True)  11.9 us
    ppermute x1, waiting for transfers between devices, shards(): acts = (active, before, given, lax.ppermute(after, 'c', [(0, 1)]))  9.06 us
    pallas_call x1, Pallas kernels, shards(): pl.pallas_call(conv_kernel, out_shape=jax.ShapeDtypeStruct((QUAD, 2 * CEL...  4.79 us
    ppermute x1, waiting for transfers between devices, kernels(): above = [lax.ppermute(back, CHIPS, ring(-1))]  3.73 us
    ppermute x1, waiting for transfers between devices, kernels(): above = [lax.ppermute(front, CHIPS, ring(-1))] + above  3.08 us
    ppermute x2, starting transfers between devices, shards(): weights = tuple((lax.ppermute(w, 'c', [(1, 0)]) for w in weights)) + weights  3.02 us
  transfers between devices with their start and end apart: 13, of which 7 were waited for; matrix products, arithmetic and copies ran while one was open for 0% of the time, Pallas kernels for 0%

profile of v4, /device:TPU:37, one launch (start us, length us, event | category | flops | bytes accessed | tf_op | source)
XLA Modules:
  0.0 122.4 jit_solution(5138212263114600256)
XLA Ops:
  0.0 0.9 copy-done
  0.9 0.9 copy-done.1
  1.9 20.7 %collective-permute-start.9 = (bf16[64,8,128]{2,1,0:T(8,128)(2,1)S(1)}, bf16[64,8,128]{2,1,0:T(8,128)(2,1)S(1)}, u32[]{:S(2)}, u32[]{:S(2)}) collective-permute-start(bf16[64,8,128]{2,1,0:T(8,128)(2,1)S(1)} %get-tuple-element.33), channel_id=1, source_target_pairs={{0,1},{1,0},{2,3},{3,2},{4,5},{5,4},{6,7},{7,6},{8,9},{9,8},{10,11... | collective-permute-start | bytes 393224 | tf_op jit(solution)/shard_map/ppermute | solution.py:269
  22.6 1.0 collective-permute-done.9
  23.6 64.9 %conditional.1 = (bf16[4,4,64,512]{3,2,1,0:T(8,128)(2,1)S(1)}, bf16[24,27,16,128]{3,2,1,0:T(8,128)(2,1)S(1)}, bf16[8,27,16,128]{3,2,1,0:T(8,128)(2,1)S(1)}) conditional(s32[]{:T(128)} %convert_element_type.4, (bf16[64,8,128]{2,1,0:T(8,128)(2,1)S(1)}, bf16[27,8,128]{2,1,0:T(8,128)(2,1)S(1)}) %tuple.14, (bf16[16,8,512]{2,1,0:T(8,128)(2,1)S(1)}, ...), branch_computations={%region_0.0_spmd, %region_1.0_spmd} | conditional | flops 4202496 | bytes 24330504 | solution.py:323
  23.6 45.9 %all-gather = bf16[216,16,128]{2,1,0:T(8,128)(2,1)S(1)} all-gather(bf16[27,16,128]{2,1,0:T(8,128)(2,1)S(1)} %pad_maximum_fusion.4), channel_id=2, replica_groups=mesh['gh'=1,'gq'=4,'zh'=8,'zl'=4,'c'=2] {'zh'}, dimensions={0}, use_global_device_ids=true | all-gather | bytes 995328 | tf_op jit(solution)/shard_map/cond/branch_0_fun/all_gather | solution.py:310
  69.7 0.9 collective-permute-start.6
  70.5 0.7 collective-permute-start.3
  71.3 2.0 %collective-permute-start.5 = (bf16[4,27,16,128]{3,2,1,0:T(8,128)(2,1)S(1)}, bf16[4,27,16,128]{3,2,1,0:T(8,128)(2,1)S(1)}, u32[]{:S(2)}, u32[]{:S(2)}) collective-permute-start(bf16[4,27,16,128]{3,2,1,0:T(8,128)(2,1)S(1)} %bitcast.26), channel_id=1, source_target_pairs={{0,62},{2,0},{4,2},{6,4},{8,6},{10,8},{12,10},{14,12},{16,14},{18,... | collective-permute-start | bytes 1327112 | tf_op jit(solution)/shard_map/cond/branch_0_fun/ppermute | solution.py:315
  73.2 3.7 %collective-permute-done.6 = bf16[4,27,16,128]{3,2,1,0:T(8,128)(2,1)S(1)} collective-permute-done((bf16[4,27,16,128]{3,2,1,0:T(8,128)(2,1)S(1)}, bf16[4,27,16,128]{3,2,1,0:T(8,128)(2,1)S(1)}, u32[]{:S(2)}, u32[]{:S(2)}) %collective-permute-start.6) | collective-permute-done | bytes 442400 | tf_op jit(solution)/shard_map/cond/branch_0_fun/ppermute | solution.py:313
  77.0 2.0 %collective-permute-start.8 = (bf16[4,27,16,128]{3,2,1,0:T(8,128)(2,1)S(1)}, bf16[4,27,16,128]{3,2,1,0:T(8,128)(2,1)S(1)}, u32[]{:S(2)}, u32[]{:S(2)}) collective-permute-start(bf16[4,27,16,128]{3,2,1,0:T(8,128)(2,1)S(1)} %collective-permute-done.6), channel_id=1, source_target_pairs={{0,62},{2,0},{4,2},{6,4},{8,6},{10,8},{12,10},{14,12},{16,14},{18,... | collective-permute-start | bytes 1327112 | tf_op jit(solution)/shard_map/cond/branch_0_fun/ppermute | solution.py:317
  78.9 3.1 %collective-permute-done.5 = bf16[4,27,16,128]{3,2,1,0:T(8,128)(2,1)S(1)} collective-permute-done((bf16[4,27,16,128]{3,2,1,0:T(8,128)(2,1)S(1)}, bf16[4,27,16,128]{3,2,1,0:T(8,128)(2,1)S(1)}, u32[]{:S(2)}, u32[]{:S(2)}) %collective-permute-start.5) | collective-permute-done | bytes 442400 | tf_op jit(solution)/shard_map/cond/branch_0_fun/ppermute | solution.py:315
  82.1 1.6 %collective-permute-done.4 = bf16[4,27,16,128]{3,2,1,0:T(8,128)(2,1)S(1)} collective-permute-done((bf16[4,27,16,128]{3,2,1,0:T(8,128)(2,1)S(1)}, bf16[4,27,16,128]{3,2,1,0:T(8,128)(2,1)S(1)}, u32[]{:S(2)}, u32[]{:S(2)}) %collective-permute-start.4) | collective-permute-done | bytes 442400 | tf_op jit(solution)/shard_map/cond/branch_0_fun/ppermute | solution.py:314
  84.0 2.4 %collective-permute-done.8 = bf16[4,27,16,128]{3,2,1,0:T(8,128)(2,1)S(1)} collective-permute-done((bf16[4,27,16,128]{3,2,1,0:T(8,128)(2,1)S(1)}, bf16[4,27,16,128]{3,2,1,0:T(8,128)(2,1)S(1)}, u32[]{:S(2)}, u32[]{:S(2)}) %collective-permute-start.8) | collective-permute-done | bytes 442400 | tf_op jit(solution)/shard_map/cond/branch_0_fun/ppermute | solution.py:317
  86.4 2.0 %collective-permute-done.7 = bf16[4,27,16,128]{3,2,1,0:T(8,128)(2,1)S(1)} collective-permute-done((bf16[4,27,16,128]{3,2,1,0:T(8,128)(2,1)S(1)}, bf16[4,27,16,128]{3,2,1,0:T(8,128)(2,1)S(1)}, u32[]{:S(2)}, u32[]{:S(2)}) %collective-permute-start.7) | collective-permute-done | bytes 442400 | tf_op jit(solution)/shard_map/cond/branch_0_fun/ppermute | solution.py:316
  88.5 1.5 %collective-permute-start.14 = (bf16[24,27,16,128]{3,2,1,0:T(8,128)(2,1)S(1)}, bf16[24,27,16,128]{3,2,1,0:T(8,128)(2,1)S(1)}, u32[]{:S(2)}, u32[]{:S(2)}) collective-permute-start(bf16[24,27,16,128]{3,2,1,0:T(8,128)(2,1)S(1)} %get-tuple-element.37.rest_2_), channel_id=1, source_target_pairs={{1,0},{3,2},{5,4},{7,6},{9,8},{11,10},{13,12},{15,14},{17,16},{19,... | collective-permute-start | bytes 7962632 | tf_op jit(solution)/shard_map/ppermute | solution.py:330
  90.0 1.5 %collective-permute-start.15 = (bf16[8,27,16,128]{3,2,1,0:T(8,128)(2,1)S(1)}, bf16[8,27,16,128]{3,2,1,0:T(8,128)(2,1)S(1)}, u32[]{:S(2)}, u32[]{:S(2)}) collective-permute-start(bf16[8,27,16,128]{3,2,1,0:T(8,128)(2,1)S(1)} %get-tuple-element.38.rest_3_), channel_id=1, source_target_pairs={{1,0},{3,2},{5,4},{7,6},{9,8},{11,10},{13,12},{15,14},{17,16},{19,... | collective-permute-start | bytes 2654216 | tf_op jit(solution)/shard_map/ppermute | solution.py:330
  91.6 1.3 %collective-permute-start.11 = (bf16[4,3,64,512]{3,2,1,0:T(8,128)(2,1)S(1)}, bf16[4,3,64,512]{3,2,1,0:T(8,128)(2,1)S(1)}, u32[]{:S(2)}, u32[]{:S(2)}) collective-permute-start(bf16[4,3,64,512]{3,2,1,0:T(8,128)(2,1)S(1)} %slice.19), channel_id=1, source_target_pairs={{0,1},{2,3},{4,5},{6,7},{8,9},{10,11},{12,13},{14,15},{16,17},{18,... | collective-permute-start | bytes 2359304 | tf_op jit(solution)/shard_map/ppermute | solution.py:328
  92.9 0.7 collective-permute-start.12
  94.3 1.3 %collective-permute-start.13 = (bf16[4,64,512]{2,1,0:T(8,128)(2,1)S(1)}, bf16[4,64,512]{2,1,0:T(8,128)(2,1)S(1)}, u32[]{:S(2)}, u32[]{:S(2)}) collective-permute-start(bf16[4,64,512]{2,1,0:T(8,128)(2,1)S(1)} %collective-permute-done.12), channel_id=1, source_target_pairs={{0,1},{2,3},{4,5},{6,7},{8,9},{10,11},{12,13},{14,15},{16,17},{18,... | collective-permute-start | bytes 786440 | tf_op jit(solution)/shard_map/ppermute | solution.py:331
  95.7 9.1 %collective-permute-done.13.r1_ref = bf16[4,64,512]{2,1,0:T(8,128)(2,1)S(1)} collective-permute-done((bf16[4,64,512]{2,1,0:T(8,128)(2,1)S(1)}, bf16[4,64,512]{2,1,0:T(8,128)(2,1)S(1)}, u32[]{:S(2)}, u32[]{:S(2)}) %collective-permute-start.13) | collective-permute-done | bytes 262176 | tf_op jit(solution)/shard_map/ppermute | solution.py:331
  104.7 4.8 %conv.1 = bf16[4,128,4,128]{3,2,1,0:T(4,128)(2,1)S(1)} custom-call(bf16[4,4,64,512]{3,2,1,0:T(8,128)(2,1)S(1)} %get-tuple-element.36.x0_ref, bf16[4,64,512]{2,1,0:T(8,128)(2,1)S(1)} %collective-permute-done.10.l0_ref, bf16[4,3,64,512]{3,2,1,0:T(8,128)(2,1)S(1)} %collective-permute-done.11.x1_ref, bf16[4,64,512]{2,1,0:T(8,128)(2,1)S(1)} %collective-permute-done.13.r1_ref, ...), custom_call_target="tpu_custom_call" | custom-call | tf_op jit(solution)/shard_map/conv/pallas_call | solution.py:334
  109.5 11.9 %all_to_all.10.i_ref = bf16[4,128,4,128]{3,2,1,0:T(4,128)(2,1)S(1)} all-to-all(bf16[4,128,4,128]{3,2,1,0:T(4,128)(2,1)S(1)} %conv.1), channel_id=1, replica_groups=mesh['gh'=1,'gq'=4,'zh'=8,'zl'=4,'c'=2] {'gq'}, dimensions={0} | all-to-all | bytes 1048576 | tf_op jit(solution)/shard_map/all_to_all | solution.py:351
  121.5 0.8 spread.1
  (25 shorter events, 1.6 us)
Async XLA Ops:
  0.0 0.9 copy-start
  0.9 0.9 copy-start.1
  1.9 21.7 %collective-permute-start.9 = (bf16[64,8,128]{2,1,0:T(8,128)(2,1)S(1)}, bf16[64,8,128]{2,1,0:T(8,128)(2,1)S(1)}, u32[]{:S(2)}, u32[]{:S(2)}) collective-permute-start(bf16[64,8,128]{2,1,0:T(8,128)(2,1)S(1)} %get-tuple-element.33), channel_id=1, source_target_pairs={{0,1},{1,0},{2,3},{3,2},{4,5},{5,4},{6,7},{7,6},{8,9},{9,8},{10,11... | collective-permute-start | bytes 393224 | tf_op jit(solution)/shard_map/ppermute | solution.py:269
  23.6 72.0 %copy-start.2 = (bf16[512]{0:T(512)(128)(2,1)S(1)}, bf16[512]{0:T(512)(128)(2,1)}, u32[]{:S(2)}) copy-start(bf16[512]{0:T(512)(128)(2,1)} %param.11) | copy-start | bytes 3076
  69.7 7.3 %collective-permute-start.6 = (bf16[4,27,16,128]{3,2,1,0:T(8,128)(2,1)S(1)}, bf16[4,27,16,128]{3,2,1,0:T(8,128)(2,1)S(1)}, u32[]{:S(2)}, u32[]{:S(2)}) collective-permute-start(bf16[4,27,16,128]{3,2,1,0:T(8,128)(2,1)S(1)} %bitcast.23), channel_id=1, source_target_pairs={{0,62},{2,0},{4,2},{6,4},{8,6},{10,8},{12,10},{14,12},{16,14},{18,... | collective-permute-start | bytes 1327112 | tf_op jit(solution)/shard_map/cond/branch_0_fun/ppermute | solution.py:313
  70.5 8.4 %collective-permute-start.3 = (bf16[4,27,16,128]{3,2,1,0:T(8,128)(2,1)S(1)}, bf16[4,27,16,128]{3,2,1,0:T(8,128)(2,1)S(1)}, u32[]{:S(2)}, u32[]{:S(2)}) collective-permute-start(bf16[4,27,16,128]{3,2,1,0:T(8,128)(2,1)S(1)} %bitcast.25), channel_id=1, source_target_pairs={{0,2},{2,4},{4,6},{6,8},{8,10},{10,12},{12,14},{14,16},{16,18},{18... | collective-permute-start | bytes 1327112 | tf_op jit(solution)/shard_map/cond/branch_0_fun/ppermute | solution.py:312
  71.3 10.7 %collective-permute-start.5 = (bf16[4,27,16,128]{3,2,1,0:T(8,128)(2,1)S(1)}, bf16[4,27,16,128]{3,2,1,0:T(8,128)(2,1)S(1)}, u32[]{:S(2)}, u32[]{:S(2)}) collective-permute-start(bf16[4,27,16,128]{3,2,1,0:T(8,128)(2,1)S(1)} %bitcast.26), channel_id=1, source_target_pairs={{0,62},{2,0},{4,2},{6,4},{8,6},{10,8},{12,10},{14,12},{16,14},{18,... | collective-permute-start | bytes 1327112 | tf_op jit(solution)/shard_map/cond/branch_0_fun/ppermute | solution.py:315
  73.2 10.4 %collective-permute-start.4 = (bf16[4,27,16,128]{3,2,1,0:T(8,128)(2,1)S(1)}, bf16[4,27,16,128]{3,2,1,0:T(8,128)(2,1)S(1)}, u32[]{:S(2)}, u32[]{:S(2)}) collective-permute-start(bf16[4,27,16,128]{3,2,1,0:T(8,128)(2,1)S(1)} %bitcast.24), channel_id=1, source_target_pairs={{0,2},{2,4},{4,6},{6,8},{8,10},{10,12},{12,14},{14,16},{16,18},{18... | collective-permute-start | bytes 1327112 | tf_op jit(solution)/shard_map/cond/branch_0_fun/ppermute | solution.py:314
  77.0 9.5 %collective-permute-start.8 = (bf16[4,27,16,128]{3,2,1,0:T(8,128)(2,1)S(1)}, bf16[4,27,16,128]{3,2,1,0:T(8,128)(2,1)S(1)}, u32[]{:S(2)}, u32[]{:S(2)}) collective-permute-start(bf16[4,27,16,128]{3,2,1,0:T(8,128)(2,1)S(1)} %collective-permute-done.6), channel_id=1, source_target_pairs={{0,62},{2,0},{4,2},{6,4},{8,6},{10,8},{12,10},{14,12},{16,14},{18,... | collective-permute-start | bytes 1327112 | tf_op jit(solution)/shard_map/cond/branch_0_fun/ppermute | solution.py:317
  78.9 9.5 %collective-permute-start.7 = (bf16[4,27,16,128]{3,2,1,0:T(8,128)(2,1)S(1)}, bf16[4,27,16,128]{3,2,1,0:T(8,128)(2,1)S(1)}, u32[]{:S(2)}, u32[]{:S(2)}) collective-permute-start(bf16[4,27,16,128]{3,2,1,0:T(8,128)(2,1)S(1)} %collective-permute-done.3), channel_id=1, source_target_pairs={{0,2},{2,4},{4,6},{6,8},{8,10},{10,12},{12,14},{14,16},{16,18},{18... | collective-permute-start | bytes 1327112 | tf_op jit(solution)/shard_map/cond/branch_0_fun/ppermute | solution.py:316
  88.5 16.3 %collective-permute-start.14 = (bf16[24,27,16,128]{3,2,1,0:T(8,128)(2,1)S(1)}, bf16[24,27,16,128]{3,2,1,0:T(8,128)(2,1)S(1)}, u32[]{:S(2)}, u32[]{:S(2)}) collective-permute-start(bf16[24,27,16,128]{3,2,1,0:T(8,128)(2,1)S(1)} %get-tuple-element.37.rest_2_), channel_id=1, source_target_pairs={{1,0},{3,2},{5,4},{7,6},{9,8},{11,10},{13,12},{15,14},{17,16},{19,... | collective-permute-start | bytes 7962632 | tf_op jit(solution)/shard_map/ppermute | solution.py:330
  90.0 14.8 %collective-permute-start.15 = (bf16[8,27,16,128]{3,2,1,0:T(8,128)(2,1)S(1)}, bf16[8,27,16,128]{3,2,1,0:T(8,128)(2,1)S(1)}, u32[]{:S(2)}, u32[]{:S(2)}) collective-permute-start(bf16[8,27,16,128]{3,2,1,0:T(8,128)(2,1)S(1)} %get-tuple-element.38.rest_3_), channel_id=1, source_target_pairs={{1,0},{3,2},{5,4},{7,6},{9,8},{11,10},{13,12},{15,14},{17,16},{19,... | collective-permute-start | bytes 2654216 | tf_op jit(solution)/shard_map/ppermute | solution.py:330
  91.6 13.2 %collective-permute-start.11 = (bf16[4,3,64,512]{3,2,1,0:T(8,128)(2,1)S(1)}, bf16[4,3,64,512]{3,2,1,0:T(8,128)(2,1)S(1)}, u32[]{:S(2)}, u32[]{:S(2)}) collective-permute-start(bf16[4,3,64,512]{3,2,1,0:T(8,128)(2,1)S(1)} %slice.19), channel_id=1, source_target_pairs={{0,1},{2,3},{4,5},{6,7},{8,9},{10,11},{12,13},{14,15},{16,17},{18,... | collective-permute-start | bytes 2359304 | tf_op jit(solution)/shard_map/ppermute | solution.py:328
  92.9 1.4 %collective-permute-start.12 = (bf16[4,64,512]{2,1,0:T(8,128)(2,1)S(1)}, bf16[4,64,512]{2,1,0:T(8,128)(2,1)S(1)}, u32[]{:S(2)}, u32[]{:S(2)}) collective-permute-start(bf16[4,64,512]{2,1,0:T(8,128)(2,1)S(1)} %get-tuple-element.45), channel_id=1, source_target_pairs={{2,0},{4,2},{6,4},{8,6},{10,8},{12,10},{14,12},{16,14},{18,16},{20... | collective-permute-start | bytes 786440 | tf_op jit(solution)/shard_map/ppermute | solution.py:327
  93.6 2.0 %collective-permute-start.10 = (bf16[4,64,512]{2,1,0:T(8,128)(2,1)S(1)}, bf16[4,64,512]{2,1,0:T(8,128)(2,1)S(1)}, u32[]{:S(2)}, u32[]{:S(2)}) collective-permute-start(bf16[4,64,512]{2,1,0:T(8,128)(2,1)S(1)} %get-tuple-element.46), channel_id=1, source_target_pairs={{0,2},{2,4},{4,6},{6,8},{8,10},{10,12},{12,14},{14,16},{16,18},{18... | collective-permute-start | bytes 786440 | tf_op jit(solution)/shard_map/ppermute | solution.py:326
  94.3 10.4 %collective-permute-start.13 = (bf16[4,64,512]{2,1,0:T(8,128)(2,1)S(1)}, bf16[4,64,512]{2,1,0:T(8,128)(2,1)S(1)}, u32[]{:S(2)}, u32[]{:S(2)}) collective-permute-start(bf16[4,64,512]{2,1,0:T(8,128)(2,1)S(1)} %collective-permute-done.12), channel_id=1, source_target_pairs={{0,1},{2,3},{4,5},{6,7},{8,9},{10,11},{12,13},{14,15},{16,17},{18,... | collective-permute-start | bytes 786440 | tf_op jit(solution)/shard_map/ppermute | solution.py:331

commit v5 on v4

--- a/solution.py
+++ b/solution.py
@@ -1,3 +1,5 @@
+import functools
+
 import jax
 import jax.numpy as jnp
 from jax import lax
@@ -46,7 +48,7 @@
     ).astype(BF16)
 
 
-def parcel_kernel(x_ref, w_ref, p_ref, s_ref, r_ref, sem):
+def parcel_kernel(x_ref, w_ref, g_ref, h_ref, p_ref, s_ref, r_ref, u_ref, v_ref, sem):
     core, quarter = lax.axis_index("c"), lax.axis_index("gq")
     lanes = pl.ds(pl.multiple_of(quarter * SLICE, SLICE), SLICE)
     tiles = x_ref.shape[0]
@@ -64,13 +66,16 @@
 
     own = pltpu.make_async_copy(w_ref.at[:, :, lanes], s_ref, sem.at[0])
     row = pltpu.make_async_copy(x_ref, r_ref, sem.at[1])
+    gain = pltpu.make_async_copy(g_ref, u_ref, sem.at[3])
+    shift = pltpu.make_async_copy(h_ref, v_ref, sem.at[4])
 
     @pl.when(core == 0)
     def _():
-        slice_copy().start()
-        row.start()
-        slice_copy().wait()
-        row.wait()
+        moves = (slice_copy(), row, gain, shift)
+        for copy in moves:
+            copy.start()
+        for copy in moves:
+            copy.wait()
 
     @pl.when(core == 1)
     def _():
@@ -140,98 +145,102 @@
         o_ref[j] = (v / (1.0 + jnp.exp(-v))).astype(BF16)
 
 
-def conv_kernel(x0_ref, l0_ref, x1_ref, r1_ref, b_ref, *rest):
-    parts = (rest[:2], rest[2:4])
-    o_ref, w_ref, x_ref, p0, p1, p2, y_ref, sem = rest[4:]
+PASSES = (
+    (((0, 0), (0, 1)), 0, 3),
+    (((0, 2), (1, 0)), 0, 3),
+    (((1, 1), (1, 2)), 1, 3),
+    (((2, 0), (2, 1)), 1, 4),
+    (((2, 2),), 1, 4),
+)
+
+
+def conv_kernel(videos, c_ref, w_ref, b_ref, *refs):
+    outs, (x_ref, p0, p1, p2, y_ref) = refs[: len(videos)], refs[len(videos) :]
     core, kind, quarter = (lax.axis_index(n) for n in ("c", "zl", "gq"))
-    rows = w_ref.shape[1] // CLASSES
-    away = (0, CLASSES - 1, 1, 2)
-
-    def copies(pieces):
-        made = []
-        for n in range(CLASSES):
-            for j in range(rows):
-                part = pieces[0].at[n * rows + j] if n < CLASSES - 1 else pieces[1].at[j]
-                chip = CLASSES * j + lax.rem(kind + away[n], CLASSES)
-                made.append(pltpu.make_async_copy(part, w_ref.at[:, chip], sem))
-        return made
-
-    for owner in range(2):
-
-        @pl.when(core == owner)
-        def _():
-            for copy in copies(parts[owner]):
-                copy.start()
-
-    half = QUAD * CELLS
     place = lax.axis_index(CHIPS)
     final = lax.axis_size(CHIPS) - 1
-    for v in range(QUAD):
-        sides = (
-            [jnp.where(place == 0, x0_ref[v, 0], l0_ref[v])] + [x0_ref[v, j] for j in range(WIDE - 1)],
-            [x1_ref[v, j] for j in range(WIDE - 1)] + [jnp.where(place == final, x1_ref[v, WIDE - 2], r1_ref[v])],
-        )
-        outer, first, second, other = (jnp.where(core == 0, x, y) for x, y in zip(*sides))
-        blocks = (
-            (v * CELLS, outer),
-            (half + v * 2 * CELLS, first),
-            (half + (v * 2 + 1) * CELLS, second),
-            (3 * half + v * CELLS, other),
-        )
-        for start, block in blocks:
+    rows = w_ref.shape[0] // CLASSES
+    count = len(videos)
+    half = count * CELLS
+    for n, v in enumerate(videos):
+        block = [c_ref[v, j] for j in range(COLS + 2)]
+        block[0] = jnp.where((core == 0) & (place == 0), block[1], block[0])
+        block[3] = jnp.where((core == 1) & (place == final), block[2], block[3])
+        for j in range(COLS + 2):
             for a in range(3):
                 for f in range(FRAMES):
                     g = max(f + a - 2, 0)
-                    x_ref[a, start + f * ROWS : start + (f + 1) * ROWS] = block[g * ROWS : (g + 1) * ROWS]
-    for copy in copies(parts[0]):
-        copy.wait()
-
-    taps = w_ref.reshape(TAPS, CHANNELS, SLICE)
-    for e, (p_ref, lo, hi) in enumerate(((p0, 0, 3 * half), (p1, half, 3 * half), (p2, half, 4 * half))):
-        for rows in ((0, 1), (2,)):
-            total = 0.0
-            for a in range(3):
-                w = jnp.concatenate([taps[a * 9 + b * 3 + e] for b in rows], axis=1)
-                total += dot(x_ref[a, lo:hi], w)
-            for n, b in enumerate(rows):
-                p_ref[b] = total[:, n * SLICE : (n + 1) * SLICE]
+                    start = j * half + n * CELLS + f * ROWS
+                    x_ref[a, start : start + ROWS] = block[j][g * ROWS : (g + 1) * ROWS]
+
+    lead = []
+    for k in range(CLASSES):
+        away = lax.rem(k + CLASSES - kind, CLASSES)
+        lead.append(rows * jnp.where(away == 1, 2, jnp.where(away == 2, 3, jnp.where(away == 3, 1, 0))))
+
+    def tap(t):
+        return jnp.concatenate([w_ref[lead[k] + j, t] for j in range(rows) for k in range(CLASSES)], axis=0)
+
+    store = (p0, p1, p2)
+    offset = (0, 1, 1)
+    for pair, lo, hi in PASSES:
+        total = 0.0
+        for a in range(3):
+            w = [tap(a * 9 + b * 3 + e) for e, b in pair]
+            w = jnp.concatenate(w, axis=1) if len(w) > 1 else w[0]
+            total += dot(x_ref[a, lo * half : hi * half], w)
+        for n, (e, b) in enumerate(pair):
+            skip = (max(lo, offset[e]) - lo) * half
+            store[e][b] = total[skip:, n * SLICE : (n + 1) * SLICE]
 
     bias = b_ref[pl.ds(quarter, 1)]
     row = iota((CELLS, SLICE), 0) % ROWS
 
-    def combine(v, _):
-        def own(p_ref, lead, b, j):
-            return p_ref[b, pl.ds(pl.multiple_of(lead + v * 2 * CELLS + j * CELLS, CELLS), CELLS)]
-
-        def edge(p_ref, lead, b):
-            return p_ref[b, pl.ds(pl.multiple_of(lead + v * CELLS, CELLS), CELLS)]
-
-        for j in range(COLS):
+    for n, o_ref in enumerate(outs):
+
+        def part(e, b, j):
+            start = (j - offset[e]) * half + n * CELLS
+            return store[e][b, start : start + CELLS]
+
+        for j in range(1, COLS + 1):
             for side in range(2):
-                t = []
-                for b in range(3):
-                    if side == 0:
-                        first = edge(p0, 0, b) if j == 0 else own(p0, half, b, 0)
-                        t.append(first + own(p1, 0, b, j) + own(p2, 0, b, j))
-                    else:
-                        final = edge(p2, 2 * half, b) if j == 1 else own(p2, 0, b, 1)
-                        t.append(own(p0, half, b, j) + own(p1, 0, b, j) + final)
+                t = [
+                    part(0, b, j - 1 + side) + part(1, b, j) + part(2, b, j + side) for b in range(3)
+                ]
                 above = jnp.where(row == 0, t[0], pltpu.roll(t[0], 1, 0))
                 below = jnp.where(row == ROWS - 1, t[2], pltpu.roll(t[2], CELLS - 1, 0))
                 for up, value in enumerate((above + t[1] + t[2], t[0] + t[1] + below)):
-                    at = up * 2 * COLS + 2 * j + side
+                    at = up * 2 * COLS + 2 * (j - 1) + side
                     y_ref[pl.ds(at, CELLS, stride=4 * COLS), :] = value + bias
-        o_ref[quarter ^ v] = y_ref[...].reshape(2 * CELLS, 2 * COLS, SLICE).astype(BF16)
-        return 0
-
-    lax.fori_loop(0, QUAD, combine, 0)
-
-
-def spread_kernel(i_ref, o_ref, sem):
-    copies = [
-        pltpu.make_async_copy(i_ref.at[q], o_ref.at[:, :, pl.ds(q * SLICE, SLICE)], sem)
-        for q in range(QUAD)
-    ]
+        o_ref[...] = y_ref[...].reshape(2 * CELLS, 2 * COLS, SLICE).astype(BF16)
+
+
+def convolve(videos, columns, weights, bias):
+    half = len(videos) * CELLS
+    return pl.pallas_call(
+        functools.partial(conv_kernel, videos),
+        out_shape=(jax.ShapeDtypeStruct((2 * CELLS, 2 * COLS, SLICE), BF16),) * len(videos),
+        in_specs=vmem(3),
+        out_specs=tuple(vmem(len(videos))),
+        scratch_shapes=[
+            pltpu.VMEM((3, 4 * half, CHANNELS), BF16),
+            pltpu.VMEM((3, 3 * half, SLICE), F32),
+            pltpu.VMEM((3, 2 * half, SLICE), F32),
+            pltpu.VMEM((3, 3 * half, SLICE), F32),
+            pltpu.VMEM((4 * COLS * CELLS, SLICE), F32),
+        ],
+        compiler_params=room(16),
+        name="conv",
+    )(columns, weights, bias)
+
+
+def spread_kernel(*refs):
+    o_ref, sem = refs[QUAD:]
+    quarter = lax.axis_index("gq")
+    copies = []
+    for n in range(QUAD):
+        lanes = pl.ds(pl.multiple_of((quarter ^ n) * SLICE, SLICE), SLICE)
+        copies.append(pltpu.make_async_copy(refs[n], o_ref.at[:, :, lanes], sem.at[n]))
     for copy in copies:
         copy.start()
     for copy in copies:
@@ -253,23 +262,25 @@
     rows = lax.axis_size("zh")
     width = WIDE * CHANNELS + 128
     tiles = hidden.shape[0] // 8
-    parcel, mine, row = pl.pallas_call(
+    parcel, mine, row, gain, shift = pl.pallas_call(
         parcel_kernel,
         out_shape=(
             jax.ShapeDtypeStruct((tiles * CHANNELS // SLICE, 8, SLICE), BF16),
             jax.ShapeDtypeStruct((TAPS, share // 2, SLICE), BF16),
             jax.ShapeDtypeStruct((tiles, 8, CHANNELS), BF16),
+            jax.ShapeDtypeStruct((1, CHANNELS), F32),
+            jax.ShapeDtypeStruct((1, CHANNELS), F32),
         ),
-        in_specs=[pl.BlockSpec(memory_space=pltpu.HBM)] * 2,
-        out_specs=tuple(vmem(3)),
+        in_specs=[pl.BlockSpec(memory_space=pltpu.HBM)] * 4,
+        out_specs=tuple(vmem(5)),
         scratch_shapes=[pltpu.SemaphoreType.DMA((2 + CHANNELS // SLICE,))],
-        compiler_params=room(2),
+        compiler_params=pltpu.CompilerParams(vmem_limit_bytes=66563328),
         name="parcel",
-    )(hidden.reshape(tiles, 8, CHANNELS), weight)
+    )(hidden.reshape(tiles, 8, CHANNELS), weight, norm_gain[None], norm_shift[None])
     parcel = lax.ppermute(parcel, "c", [(0, 1), (1, 0)])
 
     act_shape = (QUAD, WIDE, CELLS, CHANNELS)
-    kin_shapes = tuple((n * rows, TAPS, share, SLICE) for n in (CLASSES - 1, 1))
+    kin_shape = (CLASSES * rows, TAPS, share, SLICE)
 
     def blank(*shapes):
         return pl.pallas_call(
@@ -283,7 +294,7 @@
     def ring(step):
         return [(i, (i + step) % chips) for i in range(chips)]
 
-    def activations(parcel, mine, row):
+    def activations(parcel, mine, row, gain, shift):
         packed = pl.pallas_call(
             pack_kernel,
             out_shape=jax.ShapeDtypeStruct((chips, 2, width), BF16),
@@ -300,12 +311,12 @@
             out_specs=vmem(1)[0],
             compiler_params=room(6),
             name="norm",
-        )(tiles, norm_gain[None], norm_shift[None])
+        )(tiles, gain, shift)
         hops = [[(i, i ^ n) for i in range(QUAD)] for n in range(1, QUAD)]
         videos = [active] + [lax.ppermute(active, "gq", hop) for hop in hops]
-        return (jnp.stack(videos),) + blank(*kin_shapes)
-
-    def kernels(parcel, mine, row):
+        return (jnp.stack(videos),) + blank(kin_shape)
+
+    def kernels(parcel, mine, row, gain, shift):
         mine = jnp.concatenate([parcel[:TAPS], mine], axis=1)
         kin = lax.all_gather(mine, "zh", axis=0)
         front, back = kin[: rows // 2], kin[rows // 2 :]
@@ -317,47 +328,35 @@
         high = lax.ppermute(above[1], CHIPS, ring(-1))
         below, above = lax.optimization_barrier([jnp.concatenate(x) for x in (below, above)])
         near = jnp.concatenate([kin, below, above])
-        return blank(act_shape) + (near, jnp.concatenate([low, high], axis=0))
+        far = jnp.concatenate([low, high])
+        near, far = lax.optimization_barrier((near, far))
+        return blank(act_shape) + (jnp.concatenate([near, far]),)
 
     core = lax.axis_index("c")
-    active, near, far = lax.cond(core == 0, activations, kernels, parcel, mine, row)
+    active, weights = lax.cond(core == 0, activations, kernels, parcel, mine, row, gain, shift)
     right = [(2 * i, 2 * i + 2) for i in range(chips - 1)]
     left = [(j, i) for i, j in right]
     before = lax.ppermute(active[:, WIDE - 1], SPACE, right)
     after = lax.ppermute(active[:, 0], SPACE, left)
-    given = lax.ppermute(active[:, 1:], "c", [(0, 1)])
-    weights = (near, far)
-    weights = tuple(lax.ppermute(w, "c", [(1, 0)]) for w in weights) + weights
-    acts = (active, before, given, lax.ppermute(after, "c", [(0, 1)]))
-
-    half = QUAD * CELLS
-    out = pl.pallas_call(
-        conv_kernel,
-        out_shape=jax.ShapeDtypeStruct((QUAD, 2 * CELLS, 2 * COLS, SLICE), BF16),
-        in_specs=vmem(5) + [pl.BlockSpec(memory_space=pltpu.HBM)] * 4,
-        out_specs=vmem(1)[0],
-        scratch_shapes=[
-            pltpu.VMEM((TAPS, chips, share, SLICE), BF16),
-            pltpu.VMEM((3, 4 * half, CHANNELS), BF16),
-            pltpu.VMEM((3, 3 * half, SLICE), F32),
-            pltpu.VMEM((3, 2 * half, SLICE), F32),
-            pltpu.VMEM((3, 3 * half, SLICE), F32),
-            pltpu.VMEM((4 * COLS * CELLS, SLICE), F32),
-            pltpu.SemaphoreType.DMA,
-        ],
-        compiler_params=room(24),
-        name="conv",
-    )(*acts, conv_bias.astype(F32).reshape(QUAD, SLICE), *weights)
-    out = lax.all_to_all(out, "gq", split_axis=0, concat_axis=0, tiled=True)
+    brought = lax.ppermute(weights, "c", [(1, 0)])
+    given = lax.ppermute(jnp.concatenate([active[:, 1:], after[:, None]], axis=1), "c", [(0, 1)])
+    columns = jnp.concatenate([before[:, None], active[:, :WIDE - 1]], axis=1)
+    bias = conv_bias.astype(F32).reshape(QUAD, SLICE)
+
+    columns = jnp.where(core == 0, columns, given)
+    weights = jnp.where(core == 0, brought, weights)
+    outs = list(convolve(tuple(range(QUAD)), columns, weights, bias))
+    for n in range(1, QUAD):
+        outs[n] = lax.ppermute(outs[n], "gq", [(i, i ^ n) for i in range(QUAD)])
     out = pl.pallas_call(
         spread_kernel,
         out_shape=jax.ShapeDtypeStruct((2 * CELLS, 2 * COLS, CHANNELS), BF16),
-        in_specs=vmem(1),
+        in_specs=vmem(QUAD),
         out_specs=pl.BlockSpec(memory_space=pltpu.HBM),
-        scratch_shapes=[pltpu.SemaphoreType.DMA],
+        scratch_shapes=[pltpu.SemaphoreType.DMA((QUAD,))],
         compiler_params=room(4),
         name="spread",
-    )(out)
+    )(*outs)
     return out.reshape(FRAMES, 2 * ROWS, 2 * COLS, CHANNELS)
 
 

time: 123 us -> 116 us (0.943)
  the two profiles are of different devices: /device:TPU:37 before, /device:TPU:108 now
where the time goes in v5:
time: 116 us
  blocking collectives  65.1 us (56%)
  waiting for transfers between devices  21.9 us (19%)
  starting transfers between devices  19.1 us (16%)
  Pallas kernels  8.42 us (7%)
    all_to_all x1, blocking collectives, activations(): lax.all_to_all(packed, CHIPS, split_axis=0, concat_axis=0, tiled=True)  65.1 us
    ppermute x3, waiting for transfers between devices, activations(): videos = [active] + [lax.ppermute(active, 'gq', hop) for hop in hops]  6.37 us
    ppermute x1, waiting for transfers between devices, shards(): before = lax.ppermute(active[:, WIDE - 1], SPACE, right)  5.22 us
    ppermute x3, waiting for transfers between devices, shards(): outs[n] = lax.ppermute(outs[n], 'gq', [(i, i ^ n) for i in range(QUAD)])  5.01 us
    ppermute x3, starting transfers between devices, activations(): videos = [active] + [lax.ppermute(active, 'gq', hop) for hop in hops]  4.77 us
    ppermute x1, starting transfers between devices, shards(): after = lax.ppermute(active[:, 0], SPACE, left)  4.64 us
    ppermute x1, waiting for transfers between devices, shards(): after = lax.ppermute(active[:, 0], SPACE, left)  3.74 us
    ppermute x3, starting transfers between devices, shards(): outs[n] = lax.ppermute(outs[n], 'gq', [(i, i ^ n) for i in range(QUAD)])  3.61 us
  transfers between devices with their start and end apart: 11, of which 9 were waited for; matrix products, arithmetic and copies ran while one was open for 0% of the time, Pallas kernels for 0%

profile of v5, /device:TPU:108, one launch (start us, length us, event | category | flops | bytes accessed | tf_op | source)
XLA Modules:
  0.0 115.8 jit_solution(5561110375239664436)
XLA Ops:
  0.0 1.7 %parcel.1 = (bf16[64,8,128]{2,1,0:T(8,128)(2,1)}, bf16[27,8,128]{2,1,0:T(8,128)(2,1)S(1)}, bf16[16,8,512]{2,1,0:T(8,128)(2,1)}, f32[1,512]{1,0:T(1,128)S(1)}, f32[1,512]{1,0:T(1,128)S(1)}) custom-call(bf16[16,8,512]{2,1,0:T(8,128)(2,1)} %bitcast.33, bf16[27,8,512]{2,1,0:T(8,128)(2,1)} %bitcast.32, f32[1,512]{1,0:T(1,128)} %bitcast.34, f32[1,512]{1,0:T(1,128)} %bitcast.35), custom_call_target="tpu_custom_call" | custom-call | tf_op jit(solution)/shard_map/parcel/pallas_call | solution.py:265
  1.8 1.5 %collective-permute-done.9 = bf16[64,8,128]{2,1,0:T(8,128)(2,1)S(1)} collective-permute-done((bf16[64,8,128]{2,1,0:T(8,128)(2,1)}, bf16[64,8,128]{2,1,0:T(8,128)(2,1)S(1)}, u32[]{:S(2)}, u32[]{:S(2)}) %collective-permute-start.9) | collective-permute-done | bytes 131104 | tf_op jit(solution)/shard_map/ppermute | solution.py:280
  3.4 79.0 %conditional.1 = (bf16[4,4,64,512]{3,2,1,0:T(8,128)(2,1)S(1)}, bf16[32,27,16,128]{3,2,1,0:T(8,128)(2,1)S(1)}) conditional(s32[]{:T(128)} %convert_element_type.4, (bf16[64,8,128]{2,1,0:T(8,128)(2,1)S(1)}, bf16[27,8,128]{2,1,0:T(8,128)(2,1)S(1)}) %tuple.15, (bf16[16,8,512]{2,1,0:T(8,128)(2,1)}, bf16[64,8,128]{2,1,0:T(8,128)(2,1)S(1)}, ...), branch_computations={%region_0.0_spmd, %region_1.0_spmd} | conditional | flops 5971968 | bytes 31408384 | solution.py:336
  3.4 2.0 %pack.1 = bf16[32,2,2176]{2,1,0:T(2,128)(2,1)S(1)} custom-call(bf16[16,8,512]{2,1,0:T(8,128)(2,1)} %get-tuple-element.23.x_ref, bf16[64,8,128]{2,1,0:T(8,128)(2,1)S(1)} %get-tuple-element.24.y_ref), custom_call_target="tpu_custom_call" | custom-call | tf_op jit(solution)/shard_map/cond/branch_1_fun/pack/pallas_call | solution.py:298
  5.4 65.1 %all_to_all.4.r_ref = bf16[32,2,2176]{2,1,0:T(2,128)(2,1)S(1)} all-to-all(bf16[32,2,2176]{2,1,0:T(2,128)(2,1)S(1)} %pack.1), channel_id=1, replica_groups=mesh['gh'=1,'gq'=4,'zh'=8,'zl'=4,'c'=2] {'zh','zl'}, dimensions={0} | all-to-all | bytes 557056 | tf_op jit(solution)/shard_map/cond/branch_1_fun/all_to_all | solution.py:306
  71.1 1.4 %collective-permute-start.2 = (bf16[4,64,512]{2,1,0:T(8,128)(2,1)S(1)}, bf16[4,64,512]{2,1,0:T(8,128)(2,1)S(1)}, u32[]{:S(2)}, u32[]{:S(2)}) collective-permute-start(bf16[4,64,512]{2,1,0:T(8,128)(2,1)S(1)} %norm.1), channel_id=1, source_target_pairs={{0,192},{64,128},{128,64},{192,0},{1,193},{65,129},{129,65},{193,1... | collective-permute-start | bytes 786440 | tf_op jit(solution)/shard_map/cond/branch_1_fun/ppermute | solution.py:316
  72.5 3.3 %collective-permute-start.1 = (bf16[4,64,512]{2,1,0:T(8,128)(2,1)S(1)}, bf16[4,64,512]{2,1,0:T(8,128)(2,1)S(1)}, u32[]{:S(2)}, u32[]{:S(2)}) collective-permute-start(bf16[4,64,512]{2,1,0:T(8,128)(2,1)S(1)} %norm.1), channel_id=1, source_target_pairs={{0,128},{64,192},{128,0},{192,64},{1,129},{65,193},{129,1},{193,65... | collective-permute-start | bytes 786440 | tf_op jit(solution)/shard_map/cond/branch_1_fun/ppermute | solution.py:316
  75.9 2.7 %collective-permute-done.2 = bf16[4,64,512]{2,1,0:T(8,128)(2,1)S(1)} collective-permute-done((bf16[4,64,512]{2,1,0:T(8,128)(2,1)S(1)}, bf16[4,64,512]{2,1,0:T(8,128)(2,1)S(1)}, u32[]{:S(2)}, u32[]{:S(2)}) %collective-permute-start.2) | collective-permute-done | bytes 262176 | tf_op jit(solution)/shard_map/cond/branch_1_fun/ppermute | solution.py:316
  78.6 2.7 %collective-permute-done.1 = bf16[4,64,512]{2,1,0:T(8,128)(2,1)S(1)} collective-permute-done((bf16[4,64,512]{2,1,0:T(8,128)(2,1)S(1)}, bf16[4,64,512]{2,1,0:T(8,128)(2,1)S(1)}, u32[]{:S(2)}, u32[]{:S(2)}) %collective-permute-start.1) | collective-permute-done | bytes 262176 | tf_op jit(solution)/shard_map/cond/branch_1_fun/ppermute | solution.py:316
  81.3 0.9 collective-permute-done
  82.4 1.5 %collective-permute-start.13 = (bf16[32,27,16,128]{3,2,1,0:T(8,128)(2,1)S(1)}, bf16[32,27,16,128]{3,2,1,0:T(8,128)(2,1)S(1)}, u32[]{:S(2)}, u32[]{:S(2)}) collective-permute-start(bf16[32,27,16,128]{3,2,1,0:T(8,128)(2,1)S(1)} %get-tuple-element.44), channel_id=1, source_target_pairs={{1,0},{3,2},{5,4},{7,6},{9,8},{11,10},{13,12},{15,14},{17,16},{19,... | collective-permute-start | bytes 10616840 | tf_op jit(solution)/shard_map/ppermute | solution.py:341
  83.9 4.6 %collective-permute-start.11 = (bf16[4,64,512]{2,1,0:T(8,128)(2,1)S(1)}, bf16[4,64,512]{2,1,0:T(8,128)(2,1)S(1)}, u32[]{:S(2)}, u32[]{:S(2)}) collective-permute-start(bf16[4,64,512]{2,1,0:T(8,128)(2,1)S(1)} %get-tuple-element.52), channel_id=1, source_target_pairs={{2,0},{4,2},{6,4},{8,6},{10,8},{12,10},{14,12},{16,14},{18,16},{20... | collective-permute-start | bytes 786440 | tf_op jit(solution)/shard_map/ppermute | solution.py:340
  88.7 3.7 %collective-permute-done.11 = bf16[4,64,512]{2,1,0:T(8,128)(2,1)S(1)} collective-permute-done((bf16[4,64,512]{2,1,0:T(8,128)(2,1)S(1)}, bf16[4,64,512]{2,1,0:T(8,128)(2,1)S(1)}, u32[]{:S(2)}, u32[]{:S(2)}) %collective-permute-start.11) | collective-permute-done | bytes 262176 | tf_op jit(solution)/shard_map/ppermute | solution.py:340
  92.5 1.4 %collective-permute-start.12 = (bf16[4,4,64,512]{3,2,1,0:T(8,128)(2,1)S(1)}, bf16[4,4,64,512]{3,2,1,0:T(8,128)(2,1)S(1)}, u32[]{:S(2)}, u32[]{:S(2)}) collective-permute-start(bf16[4,4,64,512]{3,2,1,0:T(8,128)(2,1)S(1)} %pad_maximum_fusion.7), channel_id=1, source_target_pairs={{0,1},{2,3},{4,5},{6,7},{8,9},{10,11},{12,13},{14,15},{16,17},{18,... | collective-permute-start | bytes 3145736 | tf_op jit(solution)/shard_map/ppermute | solution.py:342
  93.9 3.0 %collective-permute-start.10 = (bf16[4,64,512]{2,1,0:T(8,128)(2,1)S(1)}, bf16[4,64,512]{2,1,0:T(8,128)(2,1)S(1)}, u32[]{:S(2)}, u32[]{:S(2)}) collective-permute-start(bf16[4,64,512]{2,1,0:T(8,128)(2,1)S(1)} %get-tuple-element.51), channel_id=1, source_target_pairs={{0,2},{2,4},{4,6},{6,8},{8,10},{10,12},{12,14},{14,16},{16,18},{18... | collective-permute-start | bytes 786440 | tf_op jit(solution)/shard_map/ppermute | solution.py:339
  97.0 5.2 %collective-permute-done.10 = bf16[4,64,512]{2,1,0:T(8,128)(2,1)S(1)} collective-permute-done((bf16[4,64,512]{2,1,0:T(8,128)(2,1)S(1)}, bf16[4,64,512]{2,1,0:T(8,128)(2,1)S(1)}, u32[]{:S(2)}, u32[]{:S(2)}) %collective-permute-start.10) | collective-permute-done | bytes 262176 | tf_op jit(solution)/shard_map/ppermute | solution.py:339
  102.8 3.4 %conv.1 = (bf16[128,4,128]{2,1,0:T(4,128)(2,1)S(1)}, bf16[128,4,128]{2,1,0:T(4,128)(2,1)S(1)}, bf16[128,4,128]{2,1,0:T(4,128)(2,1)S(1)}, bf16[128,4,128]{2,1,0:T(4,128)(2,1)S(1)}) custom-call(bf16[4,4,64,512]{3,2,1,0:T(8,128)(2,1)S(1)} %maximum_select_fusion.c_ref, bf16[32,27,16,128]{3,2,1,0:T(8,128)(2,1)S(1)} %broadcast_select_fusion.w_ref, ...), custom_call_target="tpu_custom_call" | custom-call | tf_op jit(solution)/shard_map/conv/pallas_call | solution.py:220
  106.2 1.4 %collective-permute-start.14 = (bf16[128,4,128]{2,1,0:T(4,128)(2,1)S(1)}, bf16[128,4,128]{2,1,0:T(4,128)(2,1)S(1)}, u32[]{:S(2)}, u32[]{:S(2)}) collective-permute-start(bf16[128,4,128]{2,1,0:T(4,128)(2,1)S(1)} %get-tuple-element.46), channel_id=1, source_target_pairs={{0,64},{64,0},{128,192},{192,128},{1,65},{65,1},{129,193},{193,129... | collective-permute-start | bytes 393224 | tf_op jit(solution)/shard_map/ppermute | solution.py:350
  107.6 1.4 %collective-permute-start.15 = (bf16[128,4,128]{2,1,0:T(4,128)(2,1)S(1)}, bf16[128,4,128]{2,1,0:T(4,128)(2,1)S(1)}, u32[]{:S(2)}, u32[]{:S(2)}) collective-permute-start(bf16[128,4,128]{2,1,0:T(4,128)(2,1)S(1)} %get-tuple-element.47), channel_id=1, source_target_pairs={{0,128},{64,192},{128,0},{192,64},{1,129},{65,193},{129,1},{193,65... | collective-permute-start | bytes 393224 | tf_op jit(solution)/shard_map/ppermute | solution.py:350
  108.9 0.9 collective-permute-start.16
  109.8 1.5 %collective-permute-done.14.refs_1_ = bf16[128,4,128]{2,1,0:T(4,128)(2,1)S(1)} collective-permute-done((bf16[128,4,128]{2,1,0:T(4,128)(2,1)S(1)}, bf16[128,4,128]{2,1,0:T(4,128)(2,1)S(1)}, u32[]{:S(2)}, u32[]{:S(2)}) %collective-permute-start.14) | collective-permute-done | bytes 131104 | tf_op jit(solution)/shard_map/ppermute | solution.py:350
  111.3 1.3 %collective-permute-done.15.refs_2_ = bf16[128,4,128]{2,1,0:T(4,128)(2,1)S(1)} collective-permute-done((bf16[128,4,128]{2,1,0:T(4,128)(2,1)S(1)}, bf16[128,4,128]{2,1,0:T(4,128)(2,1)S(1)}, u32[]{:S(2)}, u32[]{:S(2)}) %collective-permute-start.15) | collective-permute-done | bytes 131104 | tf_op jit(solution)/shard_map/ppermute | solution.py:350
  112.6 2.3 %collective-permute-done.16.refs_3_ = bf16[128,4,128]{2,1,0:T(4,128)(2,1)S(1)} collective-permute-done((bf16[128,4,128]{2,1,0:T(4,128)(2,1)S(1)}, bf16[128,4,128]{2,1,0:T(4,128)(2,1)S(1)}, u32[]{:S(2)}, u32[]{:S(2)}) %collective-permute-start.16) | collective-permute-done | bytes 131104 | tf_op jit(solution)/shard_map/ppermute | solution.py:350
  114.8 0.8 spread.1
  (15 shorter events, 1.7 us)
Async XLA Ops:
  1.7 1.7 %collective-permute-start.9 = (bf16[64,8,128]{2,1,0:T(8,128)(2,1)}, bf16[64,8,128]{2,1,0:T(8,128)(2,1)S(1)}, u32[]{:S(2)}, u32[]{:S(2)}) collective-permute-start(bf16[64,8,128]{2,1,0:T(8,128)(2,1)} %get-tuple-element.38), channel_id=1, source_target_pairs={{0,1},{1,0},{2,3},{3,2},{4,5},{5,4},{6,7},{7,6},{8,9},{9,8},{10,11... | collective-permute-start | bytes 393224 | tf_op jit(solution)/shard_map/ppermute | solution.py:280
  71.1 7.5 %collective-permute-start.2 = (bf16[4,64,512]{2,1,0:T(8,128)(2,1)S(1)}, bf16[4,64,512]{2,1,0:T(8,128)(2,1)S(1)}, u32[]{:S(2)}, u32[]{:S(2)}) collective-permute-start(bf16[4,64,512]{2,1,0:T(8,128)(2,1)S(1)} %norm.1), channel_id=1, source_target_pairs={{0,192},{64,128},{128,64},{192,0},{1,193},{65,129},{129,65},{193,1... | collective-permute-start | bytes 786440 | tf_op jit(solution)/shard_map/cond/branch_1_fun/ppermute | solution.py:316
  72.5 8.8 %collective-permute-start.1 = (bf16[4,64,512]{2,1,0:T(8,128)(2,1)S(1)}, bf16[4,64,512]{2,1,0:T(8,128)(2,1)S(1)}, u32[]{:S(2)}, u32[]{:S(2)}) collective-permute-start(bf16[4,64,512]{2,1,0:T(8,128)(2,1)S(1)} %norm.1), channel_id=1, source_target_pairs={{0,128},{64,192},{128,0},{192,64},{1,129},{65,193},{129,1},{193,65... | collective-permute-start | bytes 786440 | tf_op jit(solution)/shard_map/cond/branch_1_fun/ppermute | solution.py:316
  75.9 6.4 %collective-permute-start = (bf16[4,64,512]{2,1,0:T(8,128)(2,1)S(1)}, bf16[4,64,512]{2,1,0:T(8,128)(2,1)S(1)}, u32[]{:S(2)}, u32[]{:S(2)}) collective-permute-start(bf16[4,64,512]{2,1,0:T(8,128)(2,1)S(1)} %norm.1), channel_id=1, source_target_pairs={{0,64},{64,0},{128,192},{192,128},{1,65},{65,1},{129,193},{193,129... | collective-permute-start | bytes 786440 | tf_op jit(solution)/shard_map/cond/branch_1_fun/ppermute | solution.py:316
  82.4 14.6 %copy-start = (bf16[512]{0:T(512)(128)(2,1)S(1)}, bf16[512]{0:T(512)(128)(2,1)}, u32[]{:S(2)}) copy-start(bf16[512]{0:T(512)(128)(2,1)} %param.11) | copy-start | bytes 3076
  82.4 20.0 %collective-permute-start.13 = (bf16[32,27,16,128]{3,2,1,0:T(8,128)(2,1)S(1)}, bf16[32,27,16,128]{3,2,1,0:T(8,128)(2,1)S(1)}, u32[]{:S(2)}, u32[]{:S(2)}) collective-permute-start(bf16[32,27,16,128]{3,2,1,0:T(8,128)(2,1)S(1)} %get-tuple-element.44), channel_id=1, source_target_pairs={{1,0},{3,2},{5,4},{7,6},{9,8},{11,10},{13,12},{15,14},{17,16},{19,... | collective-permute-start | bytes 10616840 | tf_op jit(solution)/shard_map/ppermute | solution.py:341
  83.9 8.5 %collective-permute-start.11 = (bf16[4,64,512]{2,1,0:T(8,128)(2,1)S(1)}, bf16[4,64,512]{2,1,0:T(8,128)(2,1)S(1)}, u32[]{:S(2)}, u32[]{:S(2)}) collective-permute-start(bf16[4,64,512]{2,1,0:T(8,128)(2,1)S(1)} %get-tuple-element.52), channel_id=1, source_target_pairs={{2,0},{4,2},{6,4},{8,6},{10,8},{12,10},{14,12},{16,14},{18,16},{20... | collective-permute-start | bytes 786440 | tf_op jit(solution)/shard_map/ppermute | solution.py:340
  92.5 9.7 %collective-permute-start.12 = (bf16[4,4,64,512]{3,2,1,0:T(8,128)(2,1)S(1)}, bf16[4,4,64,512]{3,2,1,0:T(8,128)(2,1)S(1)}, u32[]{:S(2)}, u32[]{:S(2)}) collective-permute-start(bf16[4,4,64,512]{3,2,1,0:T(8,128)(2,1)S(1)} %pad_maximum_fusion.7), channel_id=1, source_target_pairs={{0,1},{2,3},{4,5},{6,7},{8,9},{10,11},{12,13},{14,15},{16,17},{18,... | collective-permute-start | bytes 3145736 | tf_op jit(solution)/shard_map/ppermute | solution.py:342
  93.9 8.3 %collective-permute-start.10 = (bf16[4,64,512]{2,1,0:T(8,128)(2,1)S(1)}, bf16[4,64,512]{2,1,0:T(8,128)(2,1)S(1)}, u32[]{:S(2)}, u32[]{:S(2)}) collective-permute-start(bf16[4,64,512]{2,1,0:T(8,128)(2,1)S(1)} %get-tuple-element.51), channel_id=1, source_target_pairs={{0,2},{2,4},{4,6},{6,8},{8,10},{10,12},{12,14},{14,16},{16,18},{18... | collective-permute-start | bytes 786440 | tf_op jit(solution)/shard_map/ppermute | solution.py:339
  106.2 5.1 %collective-permute-start.14 = (bf16[128,4,128]{2,1,0:T(4,128)(2,1)S(1)}, bf16[128,4,128]{2,1,0:T(4,128)(2,1)S(1)}, u32[]{:S(2)}, u32[]{:S(2)}) collective-permute-start(bf16[128,4,128]{2,1,0:T(4,128)(2,1)S(1)} %get-tuple-element.46), channel_id=1, source_target_pairs={{0,64},{64,0},{128,192},{192,128},{1,65},{65,1},{129,193},{193,129... | collective-permute-start | bytes 393224 | tf_op jit(solution)/shard_map/ppermute | solution.py:350
  107.6 5.0 %collective-permute-start.15 = (bf16[128,4,128]{2,1,0:T(4,128)(2,1)S(1)}, bf16[128,4,128]{2,1,0:T(4,128)(2,1)S(1)}, u32[]{:S(2)}, u32[]{:S(2)}) collective-permute-start(bf16[128,4,128]{2,1,0:T(4,128)(2,1)S(1)} %get-tuple-element.47), channel_id=1, source_target_pairs={{0,128},{64,192},{128,0},{192,64},{1,129},{65,193},{129,1},{193,65... | collective-permute-start | bytes 393224 | tf_op jit(solution)/shard_map/ppermute | solution.py:350
  108.9 5.9 %collective-permute-start.16 = (bf16[128,4,128]{2,1,0:T(4,128)(2,1)S(1)}, bf16[128,4,128]{2,1,0:T(4,128)(2,1)S(1)}, u32[]{:S(2)}, u32[]{:S(2)}) collective-permute-start(bf16[128,4,128]{2,1,0:T(4,128)(2,1)S(1)} %get-tuple-element.48), channel_id=1, source_target_pairs={{0,192},{64,128},{128,64},{192,0},{1,193},{65,129},{129,65},{193,1... | collective-permute-start | bytes 393224 | tf_op jit(solution)/shard_map/ppermute | solution.py:350

commit v6 on v5

--- a/solution.py
+++ b/solution.py
@@ -345,9 +345,11 @@
 
     columns = jnp.where(core == 0, columns, given)
     weights = jnp.where(core == 0, brought, weights)
-    outs = list(convolve(tuple(range(QUAD)), columns, weights, bias))
-    for n in range(1, QUAD):
-        outs[n] = lax.ppermute(outs[n], "gq", [(i, i ^ n) for i in range(QUAD)])
+    outs = [None] * QUAD
+    for n in reversed(range(QUAD)):
+        outs[n] = convolve((n,), columns, weights, bias)[0]
+        if n:
+            outs[n] = lax.ppermute(outs[n], "gq", [(i, i ^ n) for i in range(QUAD)])
     out = pl.pallas_call(
         spread_kernel,
         out_shape=jax.ShapeDtypeStruct((2 * CELLS, 2 * COLS, CHANNELS), BF16),

time: 116 us -> 116 us (level)
    pallas_call x1 -> x4, Pallas kernels: 3.35 us -> 3.97 us  [convolve(): pl.pallas_call(functools.partial(conv_kernel, videos), out_shape=(jax.Sha...]
  transfers between devices with their start and end apart: 11 -> 11, of which waited for: 9 -> 9; matrix products, arithmetic and copies ran while one was open for 0% -> 0% of each run, Pallas kernels for 0% -> 1%
where the time goes in v6:
time: 116 us; the launch traced here: 115 us
  blocking collectives  65.1 us (56%)
  waiting for transfers between devices  20.9 us (18%)
  starting transfers between devices  19.1 us (16%)
  Pallas kernels  9.04 us (8%)
    all_to_all x1, blocking collectives, activations(): lax.all_to_all(packed, CHIPS, split_axis=0, concat_axis=0, tiled=True)  65.1 us
    ppermute x3, waiting for transfers between devices, activations(): videos = [active] + [lax.ppermute(active, 'gq', hop) for hop in hops]  6.37 us
    ppermute x1, waiting for transfers between devices, shards(): before = lax.ppermute(active[:, WIDE - 1], SPACE, right)  5.22 us
    ppermute x3, starting transfers between devices, activations(): videos = [active] + [lax.ppermute(active, 'gq', hop) for hop in hops]  4.77 us
    ppermute x1, starting transfers between devices, shards(): after = lax.ppermute(active[:, 0], SPACE, left)  4.64 us
    ppermute x3, waiting for transfers between devices, shards(): outs[n] = lax.ppermute(outs[n], 'gq', [(i, i ^ n) for i in range(QUAD)])  4.02 us
    pallas_call x4, Pallas kernels, convolve(): pl.pallas_call(functools.partial(conv_kernel, videos), out_shape=(jax.Sha...  3.97 us
    ppermute x1, waiting for transfers between devices, shards(): after = lax.ppermute(active[:, 0], SPACE, left)  3.74 us
  transfers between devices with their start and end apart: 11, of which 9 were waited for; matrix products, arithmetic and copies ran while one was open for 0% of the time, Pallas kernels for 1%

profile of v6, /device:TPU:108, one launch (start us, length us, event | category | flops | bytes accessed | tf_op | source)
XLA Modules:
  0.0 115.4 jit_solution(6200406906127151352)
XLA Ops:
  0.0 1.7 %parcel.1 = (bf16[64,8,128]{2,1,0:T(8,128)(2,1)}, bf16[27,8,128]{2,1,0:T(8,128)(2,1)S(1)}, bf16[16,8,512]{2,1,0:T(8,128)(2,1)}, f32[1,512]{1,0:T(1,128)S(1)}, f32[1,512]{1,0:T(1,128)S(1)}) custom-call(bf16[16,8,512]{2,1,0:T(8,128)(2,1)} %bitcast.33, bf16[27,8,512]{2,1,0:T(8,128)(2,1)} %bitcast.32, f32[1,512]{1,0:T(1,128)} %bitcast.34, f32[1,512]{1,0:T(1,128)} %bitcast.35), custom_call_target="tpu_custom_call" | custom-call | tf_op jit(solution)/shard_map/parcel/pallas_call | solution.py:265
  1.8 1.5 %collective-permute-done.9 = bf16[64,8,128]{2,1,0:T(8,128)(2,1)S(1)} collective-permute-done((bf16[64,8,128]{2,1,0:T(8,128)(2,1)}, bf16[64,8,128]{2,1,0:T(8,128)(2,1)S(1)}, u32[]{:S(2)}, u32[]{:S(2)}) %collective-permute-start.9) | collective-permute-done | bytes 131104 | tf_op jit(solution)/shard_map/ppermute | solution.py:280
  3.4 79.0 %conditional.1 = (bf16[4,4,64,512]{3,2,1,0:T(8,128)(2,1)S(1)}, bf16[32,27,16,128]{3,2,1,0:T(8,128)(2,1)S(1)}) conditional(s32[]{:T(128)} %convert_element_type.4, (bf16[64,8,128]{2,1,0:T(8,128)(2,1)S(1)}, bf16[27,8,128]{2,1,0:T(8,128)(2,1)S(1)}) %tuple.15, (bf16[16,8,512]{2,1,0:T(8,128)(2,1)}, bf16[64,8,128]{2,1,0:T(8,128)(2,1)S(1)}, ...), branch_computations={%region_0.0_spmd, %region_1.0_spmd} | conditional | flops 5971968 | bytes 31408384 | solution.py:336
  3.4 2.0 %pack.1 = bf16[32,2,2176]{2,1,0:T(2,128)(2,1)S(1)} custom-call(bf16[16,8,512]{2,1,0:T(8,128)(2,1)} %get-tuple-element.23.x_ref, bf16[64,8,128]{2,1,0:T(8,128)(2,1)S(1)} %get-tuple-element.24.y_ref), custom_call_target="tpu_custom_call" | custom-call | tf_op jit(solution)/shard_map/cond/branch_1_fun/pack/pallas_call | solution.py:298
  5.4 65.1 %all_to_all.4.r_ref = bf16[32,2,2176]{2,1,0:T(2,128)(2,1)S(1)} all-to-all(bf16[32,2,2176]{2,1,0:T(2,128)(2,1)S(1)} %pack.1), channel_id=1, replica_groups=mesh['gh'=1,'gq'=4,'zh'=8,'zl'=4,'c'=2] {'zh','zl'}, dimensions={0} | all-to-all | bytes 557056 | tf_op jit(solution)/shard_map/cond/branch_1_fun/all_to_all | solution.py:306
  71.1 1.4 %collective-permute-start.2 = (bf16[4,64,512]{2,1,0:T(8,128)(2,1)S(1)}, bf16[4,64,512]{2,1,0:T(8,128)(2,1)S(1)}, u32[]{:S(2)}, u32[]{:S(2)}) collective-permute-start(bf16[4,64,512]{2,1,0:T(8,128)(2,1)S(1)} %norm.1), channel_id=1, source_target_pairs={{0,192},{64,128},{128,64},{192,0},{1,193},{65,129},{129,65},{193,1... | collective-permute-start | bytes 786440 | tf_op jit(solution)/shard_map/cond/branch_1_fun/ppermute | solution.py:316
  72.5 3.3 %collective-permute-start.1 = (bf16[4,64,512]{2,1,0:T(8,128)(2,1)S(1)}, bf16[4,64,512]{2,1,0:T(8,128)(2,1)S(1)}, u32[]{:S(2)}, u32[]{:S(2)}) collective-permute-start(bf16[4,64,512]{2,1,0:T(8,128)(2,1)S(1)} %norm.1), channel_id=1, source_target_pairs={{0,128},{64,192},{128,0},{192,64},{1,129},{65,193},{129,1},{193,65... | collective-permute-start | bytes 786440 | tf_op jit(solution)/shard_map/cond/branch_1_fun/ppermute | solution.py:316
  75.9 2.7 %collective-permute-done.2 = bf16[4,64,512]{2,1,0:T(8,128)(2,1)S(1)} collective-permute-done((bf16[4,64,512]{2,1,0:T(8,128)(2,1)S(1)}, bf16[4,64,512]{2,1,0:T(8,128)(2,1)S(1)}, u32[]{:S(2)}, u32[]{:S(2)}) %collective-permute-start.2) | collective-permute-done | bytes 262176 | tf_op jit(solution)/shard_map/cond/branch_1_fun/ppermute | solution.py:316
  78.6 2.7 %collective-permute-done.1 = bf16[4,64,512]{2,1,0:T(8,128)(2,1)S(1)} collective-permute-done((bf16[4,64,512]{2,1,0:T(8,128)(2,1)S(1)}, bf16[4,64,512]{2,1,0:T(8,128)(2,1)S(1)}, u32[]{:S(2)}, u32[]{:S(2)}) %collective-permute-start.1) | collective-permute-done | bytes 262176 | tf_op jit(solution)/shard_map/cond/branch_1_fun/ppermute | solution.py:316
  81.3 0.9 collective-permute-done
  82.4 1.5 %collective-permute-start.13 = (bf16[32,27,16,128]{3,2,1,0:T(8,128)(2,1)S(1)}, bf16[32,27,16,128]{3,2,1,0:T(8,128)(2,1)S(1)}, u32[]{:S(2)}, u32[]{:S(2)}) collective-permute-start(bf16[32,27,16,128]{3,2,1,0:T(8,128)(2,1)S(1)} %get-tuple-element.40), channel_id=1, source_target_pairs={{1,0},{3,2},{5,4},{7,6},{9,8},{11,10},{13,12},{15,14},{17,16},{19,... | collective-permute-start | bytes 10616840 | tf_op jit(solution)/shard_map/ppermute | solution.py:341
  83.9 4.6 %collective-permute-start.11 = (bf16[4,64,512]{2,1,0:T(8,128)(2,1)S(1)}, bf16[4,64,512]{2,1,0:T(8,128)(2,1)S(1)}, u32[]{:S(2)}, u32[]{:S(2)}) collective-permute-start(bf16[4,64,512]{2,1,0:T(8,128)(2,1)S(1)} %get-tuple-element.44), channel_id=1, source_target_pairs={{2,0},{4,2},{6,4},{8,6},{10,8},{12,10},{14,12},{16,14},{18,16},{20... | collective-permute-start | bytes 786440 | tf_op jit(solution)/shard_map/ppermute | solution.py:340
  88.7 3.7 %collective-permute-done.11 = bf16[4,64,512]{2,1,0:T(8,128)(2,1)S(1)} collective-permute-done((bf16[4,64,512]{2,1,0:T(8,128)(2,1)S(1)}, bf16[4,64,512]{2,1,0:T(8,128)(2,1)S(1)}, u32[]{:S(2)}, u32[]{:S(2)}) %collective-permute-start.11) | collective-permute-done | bytes 262176 | tf_op jit(solution)/shard_map/ppermute | solution.py:340
  92.5 1.4 %collective-permute-start.12 = (bf16[4,4,64,512]{3,2,1,0:T(8,128)(2,1)S(1)}, bf16[4,4,64,512]{3,2,1,0:T(8,128)(2,1)S(1)}, u32[]{:S(2)}, u32[]{:S(2)}) collective-permute-start(bf16[4,4,64,512]{3,2,1,0:T(8,128)(2,1)S(1)} %pad_maximum_fusion.7), channel_id=1, source_target_pairs={{0,1},{2,3},{4,5},{6,7},{8,9},{10,11},{12,13},{14,15},{16,17},{18,... | collective-permute-start | bytes 3145736 | tf_op jit(solution)/shard_map/ppermute | solution.py:342
  93.9 3.0 %collective-permute-start.10 = (bf16[4,64,512]{2,1,0:T(8,128)(2,1)S(1)}, bf16[4,64,512]{2,1,0:T(8,128)(2,1)S(1)}, u32[]{:S(2)}, u32[]{:S(2)}) collective-permute-start(bf16[4,64,512]{2,1,0:T(8,128)(2,1)S(1)} %get-tuple-element.43), channel_id=1, source_target_pairs={{0,2},{2,4},{4,6},{6,8},{8,10},{10,12},{12,14},{14,16},{16,18},{18... | collective-permute-start | bytes 786440 | tf_op jit(solution)/shard_map/ppermute | solution.py:339
  97.0 5.2 %collective-permute-done.10 = bf16[4,64,512]{2,1,0:T(8,128)(2,1)S(1)} collective-permute-done((bf16[4,64,512]{2,1,0:T(8,128)(2,1)S(1)}, bf16[4,64,512]{2,1,0:T(8,128)(2,1)S(1)}, u32[]{:S(2)}, u32[]{:S(2)}) %collective-permute-start.10) | collective-permute-done | bytes 262176 | tf_op jit(solution)/shard_map/ppermute | solution.py:339
  102.8 1.0 conv.5
  103.8 1.0 conv.6
  104.8 1.0 conv.7
  105.8 1.4 %collective-permute-start.14 = (bf16[128,4,128]{2,1,0:T(4,128)(2,1)S(1)}, bf16[128,4,128]{2,1,0:T(4,128)(2,1)S(1)}, u32[]{:S(2)}, u32[]{:S(2)}) collective-permute-start(bf16[128,4,128]{2,1,0:T(4,128)(2,1)S(1)} %conv.5), channel_id=1, source_target_pairs={{0,64},{64,0},{128,192},{192,128},{1,65},{65,1},{129,193},{193,129... | collective-permute-start | bytes 393224 | tf_op jit(solution)/shard_map/ppermute | solution.py:352
  107.2 1.4 %collective-permute-start.15 = (bf16[128,4,128]{2,1,0:T(4,128)(2,1)S(1)}, bf16[128,4,128]{2,1,0:T(4,128)(2,1)S(1)}, u32[]{:S(2)}, u32[]{:S(2)}) collective-permute-start(bf16[128,4,128]{2,1,0:T(4,128)(2,1)S(1)} %conv.6), channel_id=1, source_target_pairs={{0,128},{64,192},{128,0},{192,64},{1,129},{65,193},{129,1},{193,65... | collective-permute-start | bytes 393224 | tf_op jit(solution)/shard_map/ppermute | solution.py:352
  109.4 1.0 conv.4.refs_0_
  110.9 1.3 %collective-permute-done.15.refs_2_ = bf16[128,4,128]{2,1,0:T(4,128)(2,1)S(1)} collective-permute-done((bf16[128,4,128]{2,1,0:T(4,128)(2,1)S(1)}, bf16[128,4,128]{2,1,0:T(4,128)(2,1)S(1)}, u32[]{:S(2)}, u32[]{:S(2)}) %collective-permute-start.15) | collective-permute-done | bytes 131104 | tf_op jit(solution)/shard_map/ppermute | solution.py:352
  112.2 2.3 %collective-permute-done.16.refs_3_ = bf16[128,4,128]{2,1,0:T(4,128)(2,1)S(1)} collective-permute-done((bf16[128,4,128]{2,1,0:T(4,128)(2,1)S(1)}, bf16[128,4,128]{2,1,0:T(4,128)(2,1)S(1)}, u32[]{:S(2)}, u32[]{:S(2)}) %collective-permute-start.16) | collective-permute-done | bytes 131104 | tf_op jit(solution)/shard_map/ppermute | solution.py:352
  (18 shorter events, 3.9 us)
Async XLA Ops:
  1.7 1.7 %collective-permute-start.9 = (bf16[64,8,128]{2,1,0:T(8,128)(2,1)}, bf16[64,8,128]{2,1,0:T(8,128)(2,1)S(1)}, u32[]{:S(2)}, u32[]{:S(2)}) collective-permute-start(bf16[64,8,128]{2,1,0:T(8,128)(2,1)} %get-tuple-element.34), channel_id=1, source_target_pairs={{0,1},{1,0},{2,3},{3,2},{4,5},{5,4},{6,7},{7,6},{8,9},{9,8},{10,11... | collective-permute-start | bytes 393224 | tf_op jit(solution)/shard_map/ppermute | solution.py:280
  71.1 7.5 %collective-permute-start.2 = (bf16[4,64,512]{2,1,0:T(8,128)(2,1)S(1)}, bf16[4,64,512]{2,1,0:T(8,128)(2,1)S(1)}, u32[]{:S(2)}, u32[]{:S(2)}) collective-permute-start(bf16[4,64,512]{2,1,0:T(8,128)(2,1)S(1)} %norm.1), channel_id=1, source_target_pairs={{0,192},{64,128},{128,64},{192,0},{1,193},{65,129},{129,65},{193,1... | collective-permute-start | bytes 786440 | tf_op jit(solution)/shard_map/cond/branch_1_fun/ppermute | solution.py:316
  72.5 8.8 %collective-permute-start.1 = (bf16[4,64,512]{2,1,0:T(8,128)(2,1)S(1)}, bf16[4,64,512]{2,1,0:T(8,128)(2,1)S(1)}, u32[]{:S(2)}, u32[]{:S(2)}) collective-permute-start(bf16[4,64,512]{2,1,0:T(8,128)(2,1)S(1)} %norm.1), channel_id=1, source_target_pairs={{0,128},{64,192},{128,0},{192,64},{1,129},{65,193},{129,1},{193,65... | collective-permute-start | bytes 786440 | tf_op jit(solution)/shard_map/cond/branch_1_fun/ppermute | solution.py:316
  75.9 6.4 %collective-permute-start = (bf16[4,64,512]{2,1,0:T(8,128)(2,1)S(1)}, bf16[4,64,512]{2,1,0:T(8,128)(2,1)S(1)}, u32[]{:S(2)}, u32[]{:S(2)}) collective-permute-start(bf16[4,64,512]{2,1,0:T(8,128)(2,1)S(1)} %norm.1), channel_id=1, source_target_pairs={{0,64},{64,0},{128,192},{192,128},{1,65},{65,1},{129,193},{193,129... | collective-permute-start | bytes 786440 | tf_op jit(solution)/shard_map/cond/branch_1_fun/ppermute | solution.py:316
  82.4 14.6 %copy-start = (bf16[512]{0:T(512)(128)(2,1)S(1)}, bf16[512]{0:T(512)(128)(2,1)}, u32[]{:S(2)}) copy-start(bf16[512]{0:T(512)(128)(2,1)} %param.11) | copy-start | bytes 3076
  82.4 20.0 %collective-permute-start.13 = (bf16[32,27,16,128]{3,2,1,0:T(8,128)(2,1)S(1)}, bf16[32,27,16,128]{3,2,1,0:T(8,128)(2,1)S(1)}, u32[]{:S(2)}, u32[]{:S(2)}) collective-permute-start(bf16[32,27,16,128]{3,2,1,0:T(8,128)(2,1)S(1)} %get-tuple-element.40), channel_id=1, source_target_pairs={{1,0},{3,2},{5,4},{7,6},{9,8},{11,10},{13,12},{15,14},{17,16},{19,... | collective-permute-start | bytes 10616840 | tf_op jit(solution)/shard_map/ppermute | solution.py:341
  83.9 8.5 %collective-permute-start.11 = (bf16[4,64,512]{2,1,0:T(8,128)(2,1)S(1)}, bf16[4,64,512]{2,1,0:T(8,128)(2,1)S(1)}, u32[]{:S(2)}, u32[]{:S(2)}) collective-permute-start(bf16[4,64,512]{2,1,0:T(8,128)(2,1)S(1)} %get-tuple-element.44), channel_id=1, source_target_pairs={{2,0},{4,2},{6,4},{8,6},{10,8},{12,10},{14,12},{16,14},{18,16},{20... | collective-permute-start | bytes 786440 | tf_op jit(solution)/shard_map/ppermute | solution.py:340
  92.5 9.7 %collective-permute-start.12 = (bf16[4,4,64,512]{3,2,1,0:T(8,128)(2,1)S(1)}, bf16[4,4,64,512]{3,2,1,0:T(8,128)(2,1)S(1)}, u32[]{:S(2)}, u32[]{:S(2)}) collective-permute-start(bf16[4,4,64,512]{3,2,1,0:T(8,128)(2,1)S(1)} %pad_maximum_fusion.7), channel_id=1, source_target_pairs={{0,1},{2,3},{4,5},{6,7},{8,9},{10,11},{12,13},{14,15},{16,17},{18,... | collective-permute-start | bytes 3145736 | tf_op jit(solution)/shard_map/ppermute | solution.py:342
  93.9 8.3 %collective-permute-start.10 = (bf16[4,64,512]{2,1,0:T(8,128)(2,1)S(1)}, bf16[4,64,512]{2,1,0:T(8,128)(2,1)S(1)}, u32[]{:S(2)}, u32[]{:S(2)}) collective-permute-start(bf16[4,64,512]{2,1,0:T(8,128)(2,1)S(1)} %get-tuple-element.43), channel_id=1, source_target_pairs={{0,2},{2,4},{4,6},{6,8},{8,10},{10,12},{12,14},{14,16},{16,18},{18... | collective-permute-start | bytes 786440 | tf_op jit(solution)/shard_map/ppermute | solution.py:339
  105.8 5.1 %collective-permute-start.14 = (bf16[128,4,128]{2,1,0:T(4,128)(2,1)S(1)}, bf16[128,4,128]{2,1,0:T(4,128)(2,1)S(1)}, u32[]{:S(2)}, u32[]{:S(2)}) collective-permute-start(bf16[128,4,128]{2,1,0:T(4,128)(2,1)S(1)} %conv.5), channel_id=1, source_target_pairs={{0,64},{64,0},{128,192},{192,128},{1,65},{65,1},{129,193},{193,129... | collective-permute-start | bytes 393224 | tf_op jit(solution)/shard_map/ppermute | solution.py:352
  107.2 5.0 %collective-permute-start.15 = (bf16[128,4,128]{2,1,0:T(4,128)(2,1)S(1)}, bf16[128,4,128]{2,1,0:T(4,128)(2,1)S(1)}, u32[]{:S(2)}, u32[]{:S(2)}) collective-permute-start(bf16[128,4,128]{2,1,0:T(4,128)(2,1)S(1)} %conv.6), channel_id=1, source_target_pairs={{0,128},{64,192},{128,0},{192,64},{1,129},{65,193},{129,1},{193,65... | collective-permute-start | bytes 393224 | tf_op jit(solution)/shard_map/ppermute | solution.py:352
  108.6 5.9 %collective-permute-start.16 = (bf16[128,4,128]{2,1,0:T(4,128)(2,1)S(1)}, bf16[128,4,128]{2,1,0:T(4,128)(2,1)S(1)}, u32[]{:S(2)}, u32[]{:S(2)}) collective-permute-start(bf16[128,4,128]{2,1,0:T(4,128)(2,1)S(1)} %conv.7), channel_id=1, source_target_pairs={{0,192},{64,128},{128,64},{192,0},{1,193},{65,129},{129,65},{193,1... | collective-permute-start | bytes 393224 | tf_op jit(solution)/shard_map/ppermute | solution.py:352

commit v7 on v6

--- a/solution.py
+++ b/solution.py
@@ -335,12 +335,13 @@
     core = lax.axis_index("c")
     active, weights = lax.cond(core == 0, activations, kernels, parcel, mine, row, gain, shift)
     right = [(2 * i, 2 * i + 2) for i in range(chips - 1)]
-    left = [(j, i) for i, j in right]
+    left = [(2 * i + 2, 2 * i + 1) for i in range(chips - 1)]
+    after = lax.ppermute(active[:, 0], SPACE, left)
     before = lax.ppermute(active[:, WIDE - 1], SPACE, right)
-    after = lax.ppermute(active[:, 0], SPACE, left)
     brought = lax.ppermute(weights, "c", [(1, 0)])
-    given = lax.ppermute(jnp.concatenate([active[:, 1:], after[:, None]], axis=1), "c", [(0, 1)])
-    columns = jnp.concatenate([before[:, None], active[:, :WIDE - 1]], axis=1)
+    given = lax.ppermute(active[:, 1:], "c", [(0, 1)])
+    columns = jnp.concatenate([before[:, None], active[:, : WIDE - 1]], axis=1)
+    given = jnp.concatenate([given, after[:, None]], axis=1)
     bias = conv_bias.astype(F32).reshape(QUAD, SLICE)
 
     columns = jnp.where(core == 0, columns, given)

time: 116 us -> 115 us (level)
  the two profiles are of different devices: /device:TPU:108 before, /device:TPU:37 now
where the time goes in v7:
time: 115 us
  blocking collectives  44.4 us (39%)
  starting transfers between devices  36.5 us (32%)
  waiting for transfers between devices  25.2 us (22%)
  Pallas kernels  6.41 us (6%)
  other arithmetic  1.48 us (1%)
    all_gather x1, blocking collectives, kernels(): kin = lax.all_gather(mine, 'zh', axis=0)  44.4 us
    ppermute x1, starting transfers between devices, shards(): parcel = lax.ppermute(parcel, 'c', [(0, 1), (1, 0)])  20.6 us
    ppermute x1, waiting for transfers between devices, shards(): after = lax.ppermute(active[:, 0], SPACE, left)  7.84 us
    ppermute x1, waiting for transfers between devices, kernels(): below += [lax.ppermute(back, CHIPS, ring(1))]  4.73 us
    ppermute x3, waiting for transfers between devices, shards(): outs[n] = lax.ppermute(outs[n], 'gq', [(i, i ^ n) for i in range(QUAD)])  4.28 us
    pallas_call x4, Pallas kernels, convolve(): pl.pallas_call(functools.partial(conv_kernel, videos), out_shape=(jax.Sha...  3.97 us
    ppermute x1, waiting for transfers between devices, kernels(): above = [lax.ppermute(back, CHIPS, ring(-1))]  2.89 us
    ppermute x3, starting transfers between devices, shards(): outs[n] = lax.ppermute(outs[n], 'gq', [(i, i ^ n) for i in range(QUAD)])  2.87 us
  transfers between devices with their start and end apart: 14, of which 8 were waited for; matrix products, arithmetic and copies ran while one was open for 1% of the time, Pallas kernels for 1%

profile of v7, /device:TPU:37, one launch (start us, length us, event | category | flops | bytes accessed | tf_op | source)
XLA Modules:
  0.0 114.8 jit_solution(5504403445533984351)
XLA Ops:
  0.0 1.6 %parcel.1 = (bf16[64,8,128]{2,1,0:T(8,128)(2,1)}, bf16[27,8,128]{2,1,0:T(8,128)(2,1)S(1)}, bf16[16,8,512]{2,1,0:T(8,128)(2,1)}, f32[1,512]{1,0:T(1,128)S(1)}, f32[1,512]{1,0:T(1,128)S(1)}) custom-call(bf16[16,8,512]{2,1,0:T(8,128)(2,1)} %bitcast.33, bf16[27,8,512]{2,1,0:T(8,128)(2,1)} %bitcast.32, f32[1,512]{1,0:T(1,128)} %bitcast.34, f32[1,512]{1,0:T(1,128)} %bitcast.35), custom_call_target="tpu_custom_call" | custom-call | tf_op jit(solution)/shard_map/parcel/pallas_call | solution.py:265
  1.6 20.6 %collective-permute-start.9 = (bf16[64,8,128]{2,1,0:T(8,128)(2,1)}, bf16[64,8,128]{2,1,0:T(8,128)(2,1)S(1)}, u32[]{:S(2)}, u32[]{:S(2)}) collective-permute-start(bf16[64,8,128]{2,1,0:T(8,128)(2,1)} %get-tuple-element.34), channel_id=1, source_target_pairs={{0,1},{1,0},{2,3},{3,2},{4,5},{5,4},{6,7},{7,6},{8,9},{9,8},{10,11... | collective-permute-start | bytes 393224 | tf_op jit(solution)/shard_map/ppermute | solution.py:280
  22.2 1.2 %collective-permute-done.9 = bf16[64,8,128]{2,1,0:T(8,128)(2,1)S(1)} collective-permute-done((bf16[64,8,128]{2,1,0:T(8,128)(2,1)}, bf16[64,8,128]{2,1,0:T(8,128)(2,1)S(1)}, u32[]{:S(2)}, u32[]{:S(2)}) %collective-permute-start.9) | collective-permute-done | bytes 131104 | tf_op jit(solution)/shard_map/ppermute | solution.py:280
  23.4 65.4 %conditional.1 = (bf16[4,4,64,512]{3,2,1,0:T(8,128)(2,1)S(1)}, bf16[32,27,16,128]{3,2,1,0:T(8,128)(2,1)S(1)}) conditional(s32[]{:T(128)} %convert_element_type.4, (bf16[64,8,128]{2,1,0:T(8,128)(2,1)S(1)}, bf16[27,8,128]{2,1,0:T(8,128)(2,1)S(1)}) %tuple.15, (bf16[16,8,512]{2,1,0:T(8,128)(2,1)}, bf16[64,8,128]{2,1,0:T(8,128)(2,1)S(1)}, ...), branch_computations={%region_0.0_spmd, %region_1.0_spmd} | conditional | flops 5971968 | bytes 31408384 | solution.py:336
  23.4 44.4 %all-gather = bf16[216,16,128]{2,1,0:T(8,128)(2,1)S(1)} all-gather(bf16[27,16,128]{2,1,0:T(8,128)(2,1)S(1)} %pad_maximum_fusion.5), channel_id=2, replica_groups=mesh['gh'=1,'gq'=4,'zh'=8,'zl'=4,'c'=2] {'zh'}, dimensions={0}, use_global_device_ids=true | all-gather | bytes 995328 | tf_op jit(solution)/shard_map/cond/branch_0_fun/all_gather | solution.py:321
  68.0 2.5 %collective-permute-start.6 = (bf16[4,27,16,128]{3,2,1,0:T(8,128)(2,1)S(1)}, bf16[4,27,16,128]{3,2,1,0:T(8,128)(2,1)S(1)}, u32[]{:S(2)}, u32[]{:S(2)}) collective-permute-start(bf16[4,27,16,128]{3,2,1,0:T(8,128)(2,1)S(1)} %bitcast.25), channel_id=1, source_target_pairs={{0,62},{2,0},{4,2},{6,4},{8,6},{10,8},{12,10},{14,12},{16,14},{18,... | collective-permute-start | bytes 1327112 | tf_op jit(solution)/shard_map/cond/branch_0_fun/ppermute | solution.py:324
  70.6 1.1 collective-permute-start.3
  71.7 1.3 %collective-permute-start.4 = (bf16[4,27,16,128]{3,2,1,0:T(8,128)(2,1)S(1)}, bf16[4,27,16,128]{3,2,1,0:T(8,128)(2,1)S(1)}, u32[]{:S(2)}, u32[]{:S(2)}) collective-permute-start(bf16[4,27,16,128]{3,2,1,0:T(8,128)(2,1)S(1)} %bitcast.26), channel_id=1, source_target_pairs={{0,2},{2,4},{4,6},{6,8},{8,10},{10,12},{12,14},{14,16},{16,18},{18... | collective-permute-start | bytes 1327112 | tf_op jit(solution)/shard_map/cond/branch_0_fun/ppermute | solution.py:325
  73.0 1.3 %collective-permute-start.5 = (bf16[4,27,16,128]{3,2,1,0:T(8,128)(2,1)S(1)}, bf16[4,27,16,128]{3,2,1,0:T(8,128)(2,1)S(1)}, u32[]{:S(2)}, u32[]{:S(2)}) collective-permute-start(bf16[4,27,16,128]{3,2,1,0:T(8,128)(2,1)S(1)} %bitcast.24), channel_id=1, source_target_pairs={{0,62},{2,0},{4,2},{6,4},{8,6},{10,8},{12,10},{14,12},{16,14},{18,... | collective-permute-start | bytes 1327112 | tf_op jit(solution)/shard_map/cond/branch_0_fun/ppermute | solution.py:326
  74.4 2.9 %collective-permute-done.6 = bf16[4,27,16,128]{3,2,1,0:T(8,128)(2,1)S(1)} collective-permute-done((bf16[4,27,16,128]{3,2,1,0:T(8,128)(2,1)S(1)}, bf16[4,27,16,128]{3,2,1,0:T(8,128)(2,1)S(1)}, u32[]{:S(2)}, u32[]{:S(2)}) %collective-permute-start.6) | collective-permute-done | bytes 442400 | tf_op jit(solution)/shard_map/cond/branch_0_fun/ppermute | solution.py:324
  77.3 1.7 %collective-permute-start.8 = (bf16[4,27,16,128]{3,2,1,0:T(8,128)(2,1)S(1)}, bf16[4,27,16,128]{3,2,1,0:T(8,128)(2,1)S(1)}, u32[]{:S(2)}, u32[]{:S(2)}) collective-permute-start(bf16[4,27,16,128]{3,2,1,0:T(8,128)(2,1)S(1)} %collective-permute-done.6), channel_id=1, source_target_pairs={{0,62},{2,0},{4,2},{6,4},{8,6},{10,8},{12,10},{14,12},{16,14},{18,... | collective-permute-start | bytes 1327112 | tf_op jit(solution)/shard_map/cond/branch_0_fun/ppermute | solution.py:328
  78.9 4.7 %collective-permute-done.4 = bf16[4,27,16,128]{3,2,1,0:T(8,128)(2,1)S(1)} collective-permute-done((bf16[4,27,16,128]{3,2,1,0:T(8,128)(2,1)S(1)}, bf16[4,27,16,128]{3,2,1,0:T(8,128)(2,1)S(1)}, u32[]{:S(2)}, u32[]{:S(2)}) %collective-permute-start.4) | collective-permute-done | bytes 442400 | tf_op jit(solution)/shard_map/cond/branch_0_fun/ppermute | solution.py:325
  84.2 2.6 %collective-permute-done.8 = bf16[4,27,16,128]{3,2,1,0:T(8,128)(2,1)S(1)} collective-permute-done((bf16[4,27,16,128]{3,2,1,0:T(8,128)(2,1)S(1)}, bf16[4,27,16,128]{3,2,1,0:T(8,128)(2,1)S(1)}, u32[]{:S(2)}, u32[]{:S(2)}) %collective-permute-start.8) | collective-permute-done | bytes 442400 | tf_op jit(solution)/shard_map/cond/branch_0_fun/ppermute | solution.py:328
  86.7 1.7 %collective-permute-done.7 = bf16[4,27,16,128]{3,2,1,0:T(8,128)(2,1)S(1)} collective-permute-done((bf16[4,27,16,128]{3,2,1,0:T(8,128)(2,1)S(1)}, bf16[4,27,16,128]{3,2,1,0:T(8,128)(2,1)S(1)}, u32[]{:S(2)}, u32[]{:S(2)}) %collective-permute-start.7) | collective-permute-done | bytes 442400 | tf_op jit(solution)/shard_map/cond/branch_0_fun/ppermute | solution.py:327
  88.8 1.7 %collective-permute-start.13 = (bf16[32,27,16,128]{3,2,1,0:T(8,128)(2,1)S(1)}, bf16[32,27,16,128]{3,2,1,0:T(8,128)(2,1)S(1)}, u32[]{:S(2)}, u32[]{:S(2)}) collective-permute-start(bf16[32,27,16,128]{3,2,1,0:T(8,128)(2,1)S(1)} %get-tuple-element.40), channel_id=1, source_target_pairs={{1,0},{3,2},{5,4},{7,6},{9,8},{11,10},{13,12},{15,14},{17,16},{19,... | collective-permute-start | bytes 10616840 | tf_op jit(solution)/shard_map/ppermute | solution.py:341
  90.7 1.3 %collective-permute-start.11 = (bf16[4,3,64,512]{3,2,1,0:T(8,128)(2,1)S(1)}, bf16[4,3,64,512]{3,2,1,0:T(8,128)(2,1)S(1)}, u32[]{:S(2)}, u32[]{:S(2)}) collective-permute-start(bf16[4,3,64,512]{3,2,1,0:T(8,128)(2,1)S(1)} %get-tuple-element.43), channel_id=1, source_target_pairs={{0,1},{2,3},{4,5},{6,7},{8,9},{10,11},{12,13},{14,15},{16,17},{18,... | collective-permute-start | bytes 2359304 | tf_op jit(solution)/shard_map/ppermute | solution.py:342
  92.8 1.3 %collective-permute-start.12 = (bf16[4,64,512]{2,1,0:T(8,128)(2,1)S(1)}, bf16[4,64,512]{2,1,0:T(8,128)(2,1)S(1)}, u32[]{:S(2)}, u32[]{:S(2)}) collective-permute-start(bf16[4,64,512]{2,1,0:T(8,128)(2,1)S(1)} %get-tuple-element.45), channel_id=1, source_target_pairs={{2,1},{4,3},{6,5},{8,7},{10,9},{12,11},{14,13},{16,15},{18,17},{20... | collective-permute-start | bytes 786440 | tf_op jit(solution)/shard_map/ppermute | solution.py:339
  94.1 7.8 %collective-permute-done.12 = bf16[4,64,512]{2,1,0:T(8,128)(2,1)S(1)} collective-permute-done((bf16[4,64,512]{2,1,0:T(8,128)(2,1)S(1)}, bf16[4,64,512]{2,1,0:T(8,128)(2,1)S(1)}, u32[]{:S(2)}, u32[]{:S(2)}) %collective-permute-start.12) | collective-permute-done | bytes 262176 | tf_op jit(solution)/shard_map/ppermute | solution.py:339
  102.6 1.0 conv.5
  103.6 1.0 conv.6
  104.6 1.0 conv.7
  105.6 1.5 %collective-permute-start.14 = (bf16[128,4,128]{2,1,0:T(4,128)(2,1)S(1)}, bf16[128,4,128]{2,1,0:T(4,128)(2,1)S(1)}, u32[]{:S(2)}, u32[]{:S(2)}) collective-permute-start(bf16[128,4,128]{2,1,0:T(4,128)(2,1)S(1)} %conv.5), channel_id=1, source_target_pairs={{0,64},{64,0},{128,192},{192,128},{1,65},{65,1},{129,193},{193,129... | collective-permute-start | bytes 393224 | tf_op jit(solution)/shard_map/ppermute | solution.py:353
  107.2 1.4 %collective-permute-start.15 = (bf16[128,4,128]{2,1,0:T(4,128)(2,1)S(1)}, bf16[128,4,128]{2,1,0:T(4,128)(2,1)S(1)}, u32[]{:S(2)}, u32[]{:S(2)}) collective-permute-start(bf16[128,4,128]{2,1,0:T(4,128)(2,1)S(1)} %conv.6), channel_id=1, source_target_pairs={{0,128},{64,192},{128,0},{192,64},{1,129},{65,193},{129,1},{193,65... | collective-permute-start | bytes 393224 | tf_op jit(solution)/shard_map/ppermute | solution.py:353
  110.1 3.7 %collective-permute-done.15.refs_2_ = bf16[128,4,128]{2,1,0:T(4,128)(2,1)S(1)} collective-permute-done((bf16[128,4,128]{2,1,0:T(4,128)(2,1)S(1)}, bf16[128,4,128]{2,1,0:T(4,128)(2,1)S(1)}, u32[]{:S(2)}, u32[]{:S(2)}) %collective-permute-start.15) | collective-permute-done | bytes 131104 | tf_op jit(solution)/shard_map/ppermute | solution.py:353
  (28 shorter events, 5.0 us)
Async XLA Ops:
  1.6 21.8 %collective-permute-start.9 = (bf16[64,8,128]{2,1,0:T(8,128)(2,1)}, bf16[64,8,128]{2,1,0:T(8,128)(2,1)S(1)}, u32[]{:S(2)}, u32[]{:S(2)}) collective-permute-start(bf16[64,8,128]{2,1,0:T(8,128)(2,1)} %get-tuple-element.34), channel_id=1, source_target_pairs={{0,1},{1,0},{2,3},{3,2},{4,5},{5,4},{6,7},{7,6},{8,9},{9,8},{10,11... | collective-permute-start | bytes 393224 | tf_op jit(solution)/shard_map/ppermute | solution.py:280
  68.0 9.2 %collective-permute-start.6 = (bf16[4,27,16,128]{3,2,1,0:T(8,128)(2,1)S(1)}, bf16[4,27,16,128]{3,2,1,0:T(8,128)(2,1)S(1)}, u32[]{:S(2)}, u32[]{:S(2)}) collective-permute-start(bf16[4,27,16,128]{3,2,1,0:T(8,128)(2,1)S(1)} %bitcast.25), channel_id=1, source_target_pairs={{0,62},{2,0},{4,2},{6,4},{8,6},{10,8},{12,10},{14,12},{16,14},{18,... | collective-permute-start | bytes 1327112 | tf_op jit(solution)/shard_map/cond/branch_0_fun/ppermute | solution.py:324
  70.6 8.4 %collective-permute-start.3 = (bf16[4,27,16,128]{3,2,1,0:T(8,128)(2,1)S(1)}, bf16[4,27,16,128]{3,2,1,0:T(8,128)(2,1)S(1)}, u32[]{:S(2)}, u32[]{:S(2)}) collective-permute-start(bf16[4,27,16,128]{3,2,1,0:T(8,128)(2,1)S(1)} %bitcast.23), channel_id=1, source_target_pairs={{0,2},{2,4},{4,6},{6,8},{8,10},{10,12},{12,14},{14,16},{16,18},{18... | collective-permute-start | bytes 1327112 | tf_op jit(solution)/shard_map/cond/branch_0_fun/ppermute | solution.py:323
  71.7 12.0 %collective-permute-start.4 = (bf16[4,27,16,128]{3,2,1,0:T(8,128)(2,1)S(1)}, bf16[4,27,16,128]{3,2,1,0:T(8,128)(2,1)S(1)}, u32[]{:S(2)}, u32[]{:S(2)}) collective-permute-start(bf16[4,27,16,128]{3,2,1,0:T(8,128)(2,1)S(1)} %bitcast.26), channel_id=1, source_target_pairs={{0,2},{2,4},{4,6},{6,8},{8,10},{10,12},{12,14},{14,16},{16,18},{18... | collective-permute-start | bytes 1327112 | tf_op jit(solution)/shard_map/cond/branch_0_fun/ppermute | solution.py:325
  73.0 10.7 %collective-permute-start.5 = (bf16[4,27,16,128]{3,2,1,0:T(8,128)(2,1)S(1)}, bf16[4,27,16,128]{3,2,1,0:T(8,128)(2,1)S(1)}, u32[]{:S(2)}, u32[]{:S(2)}) collective-permute-start(bf16[4,27,16,128]{3,2,1,0:T(8,128)(2,1)S(1)} %bitcast.24), channel_id=1, source_target_pairs={{0,62},{2,0},{4,2},{6,4},{8,6},{10,8},{12,10},{14,12},{16,14},{18,... | collective-permute-start | bytes 1327112 | tf_op jit(solution)/shard_map/cond/branch_0_fun/ppermute | solution.py:326
  77.3 9.5 %collective-permute-start.8 = (bf16[4,27,16,128]{3,2,1,0:T(8,128)(2,1)S(1)}, bf16[4,27,16,128]{3,2,1,0:T(8,128)(2,1)S(1)}, u32[]{:S(2)}, u32[]{:S(2)}) collective-permute-start(bf16[4,27,16,128]{3,2,1,0:T(8,128)(2,1)S(1)} %collective-permute-done.6), channel_id=1, source_target_pairs={{0,62},{2,0},{4,2},{6,4},{8,6},{10,8},{12,10},{14,12},{16,14},{18,... | collective-permute-start | bytes 1327112 | tf_op jit(solution)/shard_map/cond/branch_0_fun/ppermute | solution.py:328
  78.9 9.5 %collective-permute-start.7 = (bf16[4,27,16,128]{3,2,1,0:T(8,128)(2,1)S(1)}, bf16[4,27,16,128]{3,2,1,0:T(8,128)(2,1)S(1)}, u32[]{:S(2)}, u32[]{:S(2)}) collective-permute-start(bf16[4,27,16,128]{3,2,1,0:T(8,128)(2,1)S(1)} %collective-permute-done.3), channel_id=1, source_target_pairs={{0,2},{2,4},{4,6},{6,8},{8,10},{10,12},{12,14},{14,16},{16,18},{18... | collective-permute-start | bytes 1327112 | tf_op jit(solution)/shard_map/cond/branch_0_fun/ppermute | solution.py:327
  88.8 5.3 %copy-start = (bf16[512]{0:T(512)(128)(2,1)S(1)}, bf16[512]{0:T(512)(128)(2,1)}, u32[]{:S(2)}) copy-start(bf16[512]{0:T(512)(128)(2,1)} %param.11) | copy-start | bytes 3076
  88.8 13.3 %collective-permute-start.13 = (bf16[32,27,16,128]{3,2,1,0:T(8,128)(2,1)S(1)}, bf16[32,27,16,128]{3,2,1,0:T(8,128)(2,1)S(1)}, u32[]{:S(2)}, u32[]{:S(2)}) collective-permute-start(bf16[32,27,16,128]{3,2,1,0:T(8,128)(2,1)S(1)} %get-tuple-element.40), channel_id=1, source_target_pairs={{1,0},{3,2},{5,4},{7,6},{9,8},{11,10},{13,12},{15,14},{17,16},{19,... | collective-permute-start | bytes 10616840 | tf_op jit(solution)/shard_map/ppermute | solution.py:341
  90.7 11.2 %collective-permute-start.11 = (bf16[4,3,64,512]{3,2,1,0:T(8,128)(2,1)S(1)}, bf16[4,3,64,512]{3,2,1,0:T(8,128)(2,1)S(1)}, u32[]{:S(2)}, u32[]{:S(2)}) collective-permute-start(bf16[4,3,64,512]{3,2,1,0:T(8,128)(2,1)S(1)} %get-tuple-element.43), channel_id=1, source_target_pairs={{0,1},{2,3},{4,5},{6,7},{8,9},{10,11},{12,13},{14,15},{16,17},{18,... | collective-permute-start | bytes 2359304 | tf_op jit(solution)/shard_map/ppermute | solution.py:342
  92.1 2.0 %collective-permute-start.10 = (bf16[4,64,512]{2,1,0:T(8,128)(2,1)S(1)}, bf16[4,64,512]{2,1,0:T(8,128)(2,1)S(1)}, u32[]{:S(2)}, u32[]{:S(2)}) collective-permute-start(bf16[4,64,512]{2,1,0:T(8,128)(2,1)S(1)} %get-tuple-element.46), channel_id=1, source_target_pairs={{0,2},{2,4},{4,6},{6,8},{8,10},{10,12},{12,14},{14,16},{16,18},{18... | collective-permute-start | bytes 786440 | tf_op jit(solution)/shard_map/ppermute | solution.py:340
  92.8 9.2 %collective-permute-start.12 = (bf16[4,64,512]{2,1,0:T(8,128)(2,1)S(1)}, bf16[4,64,512]{2,1,0:T(8,128)(2,1)S(1)}, u32[]{:S(2)}, u32[]{:S(2)}) collective-permute-start(bf16[4,64,512]{2,1,0:T(8,128)(2,1)S(1)} %get-tuple-element.45), channel_id=1, source_target_pairs={{2,1},{4,3},{6,5},{8,7},{10,9},{12,11},{14,13},{16,15},{18,17},{20... | collective-permute-start | bytes 786440 | tf_op jit(solution)/shard_map/ppermute | solution.py:339
  105.6 4.4 %collective-permute-start.14 = (bf16[128,4,128]{2,1,0:T(4,128)(2,1)S(1)}, bf16[128,4,128]{2,1,0:T(4,128)(2,1)S(1)}, u32[]{:S(2)}, u32[]{:S(2)}) collective-permute-start(bf16[128,4,128]{2,1,0:T(4,128)(2,1)S(1)} %conv.5), channel_id=1, source_target_pairs={{0,64},{64,0},{128,192},{192,128},{1,65},{65,1},{129,193},{193,129... | collective-permute-start | bytes 393224 | tf_op jit(solution)/shard_map/ppermute | solution.py:353
  107.2 6.6 %collective-permute-start.15 = (bf16[128,4,128]{2,1,0:T(4,128)(2,1)S(1)}, bf16[128,4,128]{2,1,0:T(4,128)(2,1)S(1)}, u32[]{:S(2)}, u32[]{:S(2)}) collective-permute-start(bf16[128,4,128]{2,1,0:T(4,128)(2,1)S(1)} %conv.6), channel_id=1, source_target_pairs={{0,128},{64,192},{128,0},{192,64},{1,129},{65,193},{129,1},{193,65... | collective-permute-start | bytes 393224 | tf_op jit(solution)/shard_map/ppermute | solution.py:353
  108.5 5.3 %collective-permute-start.16 = (bf16[128,4,128]{2,1,0:T(4,128)(2,1)S(1)}, bf16[128,4,128]{2,1,0:T(4,128)(2,1)S(1)}, u32[]{:S(2)}, u32[]{:S(2)}) collective-permute-start(bf16[128,4,128]{2,1,0:T(4,128)(2,1)S(1)} %conv.7), channel_id=1, source_target_pairs={{0,192},{64,128},{128,64},{192,0},{1,193},{65,129},{129,65},{193,1... | collective-permute-start | bytes 393224 | tf_op jit(solution)/shard_map/ppermute | solution.py:353
